TPU v7x, 32 devices: a whole 2x2x4 slice. The times are simulated.
32 devices in a mesh: rep: 2 (over y), grp: 16 (over z, x, core).
Axes of the slice: x: 2, y: 2, z: 4, core: 2. Of those that a mesh axis runs over, the one named last changes fastest.
Arguments:
- tokens: bfloat16 [16, 512, 2048], P('grp', 'rep'), may hold values from -6 to 6
- w_qkv: bfloat16 [2048, 6144], P('grp'), may hold values from -0.125 to 0.125
- w_out: bfloat16 [2048, 2048], P('grp'), may hold values from -1 to 1
- gains: bfloat16 [4352], P('grp'), may hold values from 0.25 to 1.75
- w_gate: bfloat16 [16, 2048, 1024], P('grp'), may hold values from -0.125 to 0.125
- w_up: bfloat16 [16, 2048, 1024], P('grp'), may hold values from -0.125 to 0.125
- w_down: bfloat16 [16, 1024, 2048], P('grp'), may hold values from -0.1875 to 0.1875
- segment_ids: int32 [16, 512], P('grp'), may hold values from 0 to 7, never falling along the last dimension, each value on 1 to 256 neighbouring positions
- routes: int32 [16, 512, 8], P('grp', 'rep'), may hold values from 0 to 15, all different within a row; in each aligned block of 256 rows (0 to 255, 256 to 511, ..., all dimensions but the last counted through in order) at most 144 rows name the same one
- gate_weights: float32 [16, 512, 8], P('grp', 'rep'), may hold values from 0.1 to 1
- cotangent: bfloat16 [16, 512, 2048], P('grp', 'rep'), may hold values from -6 to 6
Outputs:
- output: float32 [16, 512, 2048], P('grp', 'rep')
- d_tokens: float32 [16, 512, 2048], P('grp', 'rep')
- d_w_qkv: float32 [2048, 6144], P('grp')
- d_w_out: float32 [2048, 2048], P('grp')
- d_gains: float32 [4352], P('grp')
- d_w_gate: float32 [16, 2048, 1024], P('grp')
- d_w_up: float32 [16, 2048, 1024], P('grp')
- d_w_down: float32 [16, 1024, 2048], P('grp')
Inputs may be any that keep to these rules, and one draw needn't show every extreme that they name: `routes`: each token names 8 different experts. Among the tokens of one device (aligned blocks of 256 tokens of a sequence) no expert is named by more than 144 of them, and some expert reaches 144 on some device. `segment_ids`: document numbers never fall along a sequence; a document has 1 to 256 tokens, and one has exactly that many.
All inputs are finite; a program needn't handle non-finite values.
Results may differ from a plain program's by a relative error of at most 0.02.
Values may be sent and summed in bfloat16 or wider, within the bound.
A program may use at most 320 MiB of HBM per device.

v0:
```python
import jax
import jax.numpy as jnp
from jax import lax
from jax.sharding import PartitionSpec as P

D = 2048
HEADS = 16
HD = 128
TOP = 8


epsilon = 1e-06
rope_base = 10000.0


def rms_forward(values, gain_vec):
    inverse = lax.rsqrt(jnp.mean(values * values, axis=-1, keepdims=True) + epsilon)
    normed = values * inverse
    return (normed * gain_vec, normed, inverse)


def rms_backward(grad_out, normed, inverse, gain_vec):
    scaled = grad_out * gain_vec
    grad_in = inverse * (scaled - normed * jnp.mean(scaled * normed, axis=-1, keepdims=True))
    return (grad_in, grad_out * normed)


def rotate(values, positions, direction):
    half_size = values.shape[-1] // 2
    frequency = rope_base ** (-2.0 * jnp.arange(half_size, dtype=jnp.float32) / values.shape[-1])
    angles = positions[:, None] * frequency[None, :]
    cosine_table = jnp.cos(angles)[:, None, :]
    sine_table = direction * jnp.sin(angles)[:, None, :]
    first_half = values[..., :half_size]
    second_half = values[..., half_size:]
    return jnp.concatenate(
        [
            first_half * cosine_table - second_half * sine_table,
            second_half * cosine_table + first_half * sine_table,
        ],
        axis=-1,
    )


def per_device(
    tokens, w_qkv, w_out, gains, w_gate, w_up, w_down, segment_ids, routes, gate_weights, cotangent
):
    groups = lax.axis_size("grp")
    tok_rows = tokens.shape[1]
    seq_len = segment_ids.shape[1]
    score_scale = HD ** (-0.5)
    rows_in = tokens[0].astype(jnp.float32)
    full_qkv, full_out, full_gains = (
        lax.all_gather(w_qkv, "grp", axis=0, tiled=True),
        lax.all_gather(w_out, "grp", axis=0, tiled=True),
        lax.all_gather(gains, "grp", axis=0, tiled=True),
    )
    gains_f = full_gains.astype(jnp.float32)
    g_attn = gains_f[:D]
    g_ffn = gains_f[D : 2 * D]
    g_query = gains_f[2 * D : 2 * D + HD]
    g_key = gains_f[2 * D + HD :]
    normed_one, hat_one, inv_one = rms_forward(rows_in, g_attn)
    h1_b = normed_one.astype(jnp.bfloat16)
    projected = jnp.dot(h1_b, full_qkv, preferred_element_type=jnp.float32)
    q_pre = projected[:, :D].reshape(tok_rows, HEADS, HD)
    k_pre = projected[:, D : 2 * D].reshape(tok_rows, HEADS, HD)
    v_pre = projected[:, 2 * D :]
    q_normed, q_hat, q_inv = rms_forward(q_pre, g_query)
    k_normed, k_hat, k_inv = rms_forward(k_pre, g_key)
    rep_start = lax.axis_index("rep") * tok_rows
    positions = (rep_start + jnp.arange(tok_rows, dtype=jnp.int32)).astype(jnp.float32)
    q_b = rotate(q_normed, positions, 1.0).astype(jnp.bfloat16)
    k_b = rotate(k_normed, positions, 1.0).reshape(tok_rows, D).astype(jnp.bfloat16)
    v_b = v_pre.astype(jnp.bfloat16)
    keys_all, vals_all = (
        lax.all_gather(k_b, "rep", axis=0, tiled=True),
        lax.all_gather(v_b, "rep", axis=0, tiled=True),
    )
    keys_h = keys_all.reshape(seq_len, HEADS, HD)
    vals_h = vals_all.reshape(seq_len, HEADS, HD)
    own_docs = lax.dynamic_slice_in_dim(segment_ids[0], rep_start, tok_rows)
    same_doc = (own_docs[:, None] == segment_ids[0][None, :])[None]

    def masked_scores():
        raw = (
            jnp.einsum("qhd,khd->hqk", q_b, keys_h, preferred_element_type=jnp.float32)
            * score_scale
        )
        return jnp.where(same_doc, raw, -1e30)

    scores = masked_scores()
    row_max = jnp.max(scores, axis=-1, keepdims=True)
    log_total = row_max + jnp.log(jnp.sum(jnp.exp(scores - row_max), axis=-1, keepdims=True))
    probs_b = jnp.exp(scores - log_total).astype(jnp.bfloat16)
    attended = jnp.einsum("hqk,khd->qhd", probs_b, vals_h, preferred_element_type=jnp.float32)
    attended_b = attended.reshape(tok_rows, D).astype(jnp.bfloat16)
    mid_rows = rows_in + jnp.dot(attended_b, full_out, preferred_element_type=jnp.float32)
    normed_two, hat_two, inv_two = rms_forward(mid_rows, g_ffn)
    h2_b = normed_two.astype(jnp.bfloat16)
    entries = tok_rows * TOP
    capacity = min(tok_rows, (9 * entries + 8 * groups - 1) // (8 * groups))
    flat_routes = routes[0].reshape(entries)
    owner_hot = (flat_routes[:, None] == jnp.arange(groups, dtype=jnp.int32)[None, :]).astype(
        jnp.int32
    )
    slot_index = jnp.sum(jnp.cumsum(owner_hot, axis=0) * owner_hot, axis=1) - 1
    target = flat_routes * capacity + slot_index
    source = (
        jnp.full((groups * capacity,), entries, jnp.int32)
        .at[target]
        .set(jnp.arange(entries, dtype=jnp.int32))
    )
    token_of = jnp.where(source < entries, source // TOP, tok_rows)

    def dispatch_rows(rows_b):
        padded = jnp.concatenate([rows_b, jnp.zeros((1, D), jnp.bfloat16)], axis=0)
        return padded[token_of].reshape(groups, capacity, D)

    arrived = lax.all_to_all(dispatch_rows(h2_b), "grp", split_axis=0, concat_axis=0, tiled=True)
    expert_in = arrived.reshape(groups * capacity, D)
    gate_pre = jnp.dot(expert_in, w_gate[0], preferred_element_type=jnp.float32)
    up_pre = jnp.dot(expert_in, w_up[0], preferred_element_type=jnp.float32)
    act_b = (jax.nn.silu(gate_pre) * up_pre).astype(jnp.bfloat16)
    expert_out = jnp.dot(act_b, w_down[0], preferred_element_type=jnp.float32).astype(jnp.bfloat16)
    returned = lax.all_to_all(
        expert_out.reshape(groups, capacity, D), "grp", split_axis=0, concat_axis=0, tiled=True
    )
    per_entry = (
        returned.reshape(groups * capacity, D)[target].reshape(tok_rows, TOP, D).astype(jnp.float32)
    )
    gates_f = gate_weights[0]
    result = mid_rows + jnp.sum(gates_f[:, :, None] * per_entry, axis=1)
    grad_out = cotangent[0].astype(jnp.float32)
    entry_grads = (
        (gates_f[:, :, None] * grad_out[:, None, :]).astype(jnp.bfloat16).reshape(entries, D)
    )
    padded_grads = jnp.concatenate([entry_grads, jnp.zeros((1, D), jnp.bfloat16)], axis=0)
    grad_buffer = padded_grads[jnp.minimum(source, entries)].reshape(groups, capacity, D)
    grad_arrived = lax.all_to_all(
        grad_buffer, "grp", split_axis=0, concat_axis=0, tiled=True
    ).reshape(groups * capacity, D)
    qkv_weights, out_weights = (
        lax.all_gather(w_qkv, "grp", axis=0, tiled=True),
        lax.all_gather(w_out, "grp", axis=0, tiled=True),
    )
    rows_again = lax.all_to_all(dispatch_rows(h2_b), "grp", split_axis=0, concat_axis=0, tiled=True)
    expert_rows = rows_again.reshape(groups * capacity, D)
    grad_act = jnp.einsum("rd,fd->rf", grad_arrived, w_down[0], preferred_element_type=jnp.float32)
    sigmoid_gate = jax.nn.sigmoid(gate_pre)
    grad_gate = (grad_act * up_pre * sigmoid_gate * (1.0 + gate_pre * (1.0 - sigmoid_gate))).astype(
        jnp.bfloat16
    )
    grad_up = (grad_act * gate_pre * sigmoid_gate).astype(jnp.bfloat16)
    grad_rows = (
        jnp.einsum("rf,df->rd", grad_gate, w_gate[0], preferred_element_type=jnp.float32)
        + jnp.einsum("rf,df->rd", grad_up, w_up[0], preferred_element_type=jnp.float32)
    ).astype(jnp.bfloat16)
    grad_wgate = jnp.einsum(
        "rd,rf->df", expert_rows, grad_gate, preferred_element_type=jnp.float32
    )[None]
    grad_wup = jnp.einsum("rd,rf->df", expert_rows, grad_up, preferred_element_type=jnp.float32)[
        None
    ]
    grad_wdown = jnp.einsum("rf,rd->fd", act_b, grad_arrived, preferred_element_type=jnp.float32)[
        None
    ]
    back_rows = lax.all_to_all(
        grad_rows.reshape(groups, capacity, D), "grp", split_axis=0, concat_axis=0, tiled=True
    )
    grad_h2 = jnp.sum(
        back_rows.reshape(groups * capacity, D)[target]
        .reshape(tok_rows, TOP, D)
        .astype(jnp.float32),
        axis=1,
    )
    grad_mid_norm, ffn_terms = rms_backward(grad_h2, hat_two, inv_two, g_ffn)
    grad_mid = grad_out + grad_mid_norm
    grad_branch_b = grad_mid.astype(jnp.bfloat16)
    grad_wout = jnp.einsum(
        "td,te->de", attended_b, grad_branch_b, preferred_element_type=jnp.float32
    )
    grad_attn = jnp.einsum(
        "te,de->td", grad_branch_b, out_weights, preferred_element_type=jnp.float32
    )
    grad_attn_b = grad_attn.astype(jnp.bfloat16).reshape(tok_rows, HEADS, HD)
    probs_f = jnp.exp(masked_scores() - log_total)
    probs_again = probs_f.astype(jnp.bfloat16)
    grad_probs = jnp.einsum("qhd,khd->hqk", grad_attn_b, vals_h, preferred_element_type=jnp.float32)
    grad_vals = jnp.einsum(
        "hqk,qhd->khd", probs_again, grad_attn_b, preferred_element_type=jnp.float32
    )
    grad_scores = (
        probs_f * (grad_probs - jnp.sum(probs_f * grad_probs, axis=-1, keepdims=True))
    ).astype(jnp.bfloat16)
    grad_q = (
        jnp.einsum("hqk,khd->qhd", grad_scores, keys_h, preferred_element_type=jnp.float32)
        * score_scale
    )
    grad_k = (
        jnp.einsum("hqk,qhd->khd", grad_scores, q_b, preferred_element_type=jnp.float32)
        * score_scale
    )
    grad_k_own, grad_v_own = (
        lax.psum_scatter(
            grad_k.reshape(seq_len, D).astype(jnp.bfloat16), "rep", scatter_dimension=0, tiled=True
        ).astype(jnp.float32),
        lax.psum_scatter(
            grad_vals.reshape(seq_len, D).astype(jnp.bfloat16),
            "rep",
            scatter_dimension=0,
            tiled=True,
        ).astype(jnp.float32),
    )
    grad_qn = rotate(grad_q, positions, -1.0)
    grad_kn = rotate(grad_k_own.reshape(tok_rows, HEADS, HD), positions, -1.0)
    grad_q_pre, query_terms = rms_backward(grad_qn, q_hat, q_inv, g_query)
    grad_k_pre, key_terms = rms_backward(grad_kn, k_hat, k_inv, g_key)
    grad_proj = jnp.concatenate(
        [grad_q_pre.reshape(tok_rows, D), grad_k_pre.reshape(tok_rows, D), grad_v_own], axis=1
    ).astype(jnp.bfloat16)
    grad_wqkv = jnp.einsum("td,te->de", h1_b, grad_proj, preferred_element_type=jnp.float32)
    grad_h1 = jnp.einsum("te,de->td", grad_proj, qkv_weights, preferred_element_type=jnp.float32)
    grad_rows_one, attn_terms = rms_backward(grad_h1, hat_one, inv_one, g_attn)
    grad_tokens = grad_mid + grad_rows_one
    grad_gains = jnp.concatenate(
        [
            jnp.sum(attn_terms, axis=0),
            jnp.sum(ffn_terms, axis=0),
            jnp.sum(query_terms, axis=(0, 1)),
            jnp.sum(key_terms, axis=(0, 1)),
        ]
    )
    shard_qkv, shard_out, shard_gains = (
        lax.psum_scatter(
            grad_wqkv.astype(jnp.bfloat16), "grp", scatter_dimension=0, tiled=True
        ).astype(jnp.float32),
        lax.psum_scatter(
            grad_wout.astype(jnp.bfloat16), "grp", scatter_dimension=0, tiled=True
        ).astype(jnp.float32),
        lax.psum_scatter(
            grad_gains.astype(jnp.bfloat16), "grp", scatter_dimension=0, tiled=True
        ).astype(jnp.float32),
    )
    sum_gate, sum_up, sum_down, shard_qkv, shard_out, shard_gains = (
        lax.psum(grad_wgate.astype(jnp.bfloat16), "rep").astype(jnp.float32),
        lax.psum(grad_wup.astype(jnp.bfloat16), "rep").astype(jnp.float32),
        lax.psum(grad_wdown.astype(jnp.bfloat16), "rep").astype(jnp.float32),
        lax.psum(shard_qkv.astype(jnp.bfloat16), "rep").astype(jnp.float32),
        lax.psum(shard_out.astype(jnp.bfloat16), "rep").astype(jnp.float32),
        lax.psum(shard_gains.astype(jnp.bfloat16), "rep").astype(jnp.float32),
    )
    return (
        result[None],
        grad_tokens[None],
        shard_qkv,
        shard_out,
        shard_gains,
        sum_gate,
        sum_up,
        sum_down,
    )


def solution(mesh):
    in_specs = (
        P("grp", "rep", None),
        P("grp", None),
        P("grp", None),
        P("grp"),
        P("grp", None, None),
        P("grp", None, None),
        P("grp", None, None),
        P("grp", None),
        P("grp", "rep", None),
        P("grp", "rep", None),
        P("grp", "rep", None),
    )
    out_specs = (
        P("grp", "rep", None),
        P("grp", "rep", None),
        P("grp", None),
        P("grp", None),
        P("grp"),
        P("grp", None, None),
        P("grp", None, None),
        P("grp", None, None),
    )
    return jax.shard_map(
        per_device, mesh=mesh, in_specs=in_specs, out_specs=out_specs, check_vma=False
    )
```

profile of v0, /device:TPU:0, one launch (start us, length us, event | category | flops | bytes accessed | tf_op | source)
XLA Modules:
  0.0 2068.2 jit_solution(16994504124687573132)
XLA Ops:
  10.8 66.0 %all-reduce.2 = bf16[4352]{0:T(1024)(128)(2,1)S(1)} all-reduce(bf16[4352]{0:T(1024)(128)(2,1)S(1)} %dynamic-update-slice), channel_id=1, replica_groups=mesh['rep'=2,'grp'=16] {'grp'}, use_global_device_ids=true, to_apply=%add.2 | all-reduce | flops 4352 | bytes 17408
  79.7 62.0 %all-gather.5.cloned.1.call-done = bf16[2048,6144]{1,0:T(8,128)(2,1)} async-done(((bf16[128,6144]{1,0:T(8,128)(2,1)}), bf16[2048,6144]{1,0:T(8,128)(2,1)}) %all-gather.5.cloned.1.call-update) | async-done | bytes 25165840 | tf_op jit(solution)/shard_map/all_gather | solution.py:54
  141.8 12.0 fusion.51
  176.8 18.3 scatter_custom_fusion
  195.3 5.5 all-gather.9.cloned.1.call-done
  207.9 28.2 %all-gather.7.cloned.1.call-done = bf16[512,2048]{1,0:T(8,128)(2,1)} async-done(((bf16[256,2048]{1,0:T(8,128)(2,1)}), bf16[512,2048]{1,0:T(8,128)(2,1)}) %all-gather.7.cloned.1.call-update) | async-done | bytes 2097168 | tf_op jit(solution)/shard_map/all_gather | solution.py:78
  236.1 6.5 fusion.42
  242.6 69.8 %all-gather.11.cloned.1.call-done = bf16[2048,2048]{1,0:T(8,128)(2,1)} async-done(((bf16[128,2048]{1,0:T(8,128)(2,1)}), bf16[2048,2048]{1,0:T(8,128)(2,1)}) %all-gather.11.cloned.1.call-update) | async-done | bytes 8388624 | tf_op jit(solution)/shard_map/all_gather | solution.py:55
  312.4 5.8 multiply_reduce_fusion.5
  319.9 9.8 gather_fusion
  329.8 5.0 all-to-all-start
  339.4 8.3 concatenate.36
  347.7 22.8 %gather_fusion.2 = bf16[2304,2048]{1,0:T(8,128)(2,1)} fusion(bf16[2049,2048]{1,0:T(8,128)(2,1)} %concatenate.36, s32[3072]{0:T(1024)S(1)} %get-tuple-element.70), kind=kCustom, calls=%fused_computation.2 | custom fusion | bytes 18883584 | tf_op jit(solution)/shard_map/gather | solution.py:139
  370.5 133.0 %all-to-all-done = bf16[16,144,2048]{2,1,0:T(8,128)(2,1)} async-done(((bf16[16,144,2048]{2,1,0:T(8,128)(2,1)}), bf16[16,144,2048]{2,1,0:T(8,128)(2,1)}, u32[]{:S(2)}, u32[]{:S(2)}) %all-to-all-start) | async-done | bytes 9437216 | tf_op jit(solution)/shard_map/all_to_all | solution.py:120
  503.5 41.0 %all-to-all-start.2 = ((bf16[16,144,2048]{2,1,0:T(8,128)(2,1)}), bf16[16,144,2048]{2,1,0:T(8,128)(2,1)}, u32[]{:S(2)}, u32[]{:S(2)}) async-start(bf16[16,144,2048]{2,1,0:T(8,128)(2,1)} %bitcast.223), calls=%async_computation.2 | async-start | bytes 18874368 | tf_op jit(solution)/shard_map/all_to_all | solution.py:140
  544.5 16.0 fusion.8
  560.5 14.7 fusion.12
  575.2 138.0 %all-to-all-done.2 = bf16[16,144,2048]{2,1,0:T(8,128)(2,1)} async-done(((bf16[16,144,2048]{2,1,0:T(8,128)(2,1)}), bf16[16,144,2048]{2,1,0:T(8,128)(2,1)}, u32[]{:S(2)}, u32[]{:S(2)}) %all-to-all-start.2) | async-done | bytes 9437216 | tf_op jit(solution)/shard_map/all_to_all | solution.py:140
  713.3 26.1 %multiply_convert_fusion = (bf16[2304,1024]{1,0:T(8,128)(2,1)}, bf16[2304,1024]{1,0:T(8,128)(2,1)}, bf16[2304,1024]{1,0:T(8,128)(2,1)}) fusion(f32[2304,1024]{1,0:T(8,128)} %fusion.12, f32[2304,1024]{1,0:T(8,128)} %fusion.8, bf16[2304,2048]{1,0:T(8,128)(2,1)} %bitcast.26, bf16[1,1024,2048]{2,1,0:T(8,128)(2,1)} %param.17), kind=kOutput, calls=%fused_computation.13 | convolution fusion | flops 9701425152 | bytes 46661632 | tf_op jit(solution)/shard_map/rd,fd->rf/dot_general | solution.py:149
  739.3 15.3 convolution_convert_fusion.1
  754.7 40.9 %all-to-all-start.1 = ((bf16[16,144,2048]{2,1,0:T(8,128)(2,1)}), bf16[16,144,2048]{2,1,0:T(8,128)(2,1)}, u32[]{:S(2)}, u32[]{:S(2)}) async-start(bf16[16,144,2048]{2,1,0:T(8,128)(2,1)} %bitcast.225), calls=%async_computation.1 | async-start | bytes 18874368 | tf_op jit(solution)/shard_map/all_to_all | solution.py:126
  795.6 17.0 fusion.10
  812.6 16.6 add_convert_fusion
  829.2 135.3 %all-to-all-done.1 = bf16[16,144,2048]{2,1,0:T(8,128)(2,1)} async-done(((bf16[16,144,2048]{2,1,0:T(8,128)(2,1)}), bf16[16,144,2048]{2,1,0:T(8,128)(2,1)}, u32[]{:S(2)}, u32[]{:S(2)}) %all-to-all-start.1) | async-done | bytes 9437216 | tf_op jit(solution)/shard_map/all_to_all | solution.py:126
  964.4 40.9 %all-to-all-start.3 = ((bf16[16,144,2048]{2,1,0:T(8,128)(2,1)}), bf16[16,144,2048]{2,1,0:T(8,128)(2,1)}, u32[]{:S(2)}, u32[]{:S(2)}) async-start(bf16[16,144,2048]{2,1,0:T(8,128)(2,1)} %bitcast.224), calls=%async_computation.3 | async-start | bytes 18874368 | tf_op jit(solution)/shard_map/all_to_all | solution.py:168
  1005.5 21.2 %gather_fusion.1 = bf16[2048,2048]{1,0:T(8,128)(2,1)} fusion(bf16[2304,2048]{1,0:T(8,128)(2,1)} %bitcast.19, s32[2048]{0:T(1024)S(1)} %broadcast_clamp_fusion), kind=kCustom, calls=%fused_computation.1 | custom fusion | bytes 16785408 | tf_op jit(solution)/shard_map/gather | solution.py:130
  1026.7 147.4 %all-to-all-done.3 = bf16[16,144,2048]{2,1,0:T(8,128)(2,1)} async-done(((bf16[16,144,2048]{2,1,0:T(8,128)(2,1)}), bf16[16,144,2048]{2,1,0:T(8,128)(2,1)}, u32[]{:S(2)}, u32[]{:S(2)}) %all-to-all-start.3) | async-done | bytes 9437216 | tf_op jit(solution)/shard_map/all_to_all | solution.py:168
  1174.2 21.4 %gather_fusion.3 = bf16[2048,2048]{1,0:T(8,128)(2,1)} fusion(bf16[2304,2048]{1,0:T(8,128)(2,1)} %bitcast.28, s32[2048]{0:T(1024)S(1)} %broadcast_clamp_fusion), kind=kCustom, calls=%fused_computation.3 | custom fusion | bytes 16785408 | tf_op jit(solution)/shard_map/gather | solution.py:172
  1195.6 11.4 convert_reduce_fusion
  1209.8 12.9 fusion
  1228.3 6.8 convolution_convert_fusion.3
  1236.9 6.8 multiply_reduce_fusion
  1249.2 7.0 convolution_convert_fusion.4
  1260.5 5.7 convolution_convert_fusion.2
  1268.4 5.4 multiply_bitcast_fusion
  1273.8 43.4 %reduce-scatter.5.cloned.1.call-done = bf16[256,2048]{0,1:T(8,128)(2,1)} async-done(((bf16[512,2048]{0,1:T(8,128)(2,1)}), bf16[256,2048]{0,1:T(8,128)(2,1)}) %reduce-scatter.5.cloned.1.call-update) | async-done | bytes 1048592 | tf_op jit(solution)/shard_map/reduce_scatter | solution.py:205
  1324.7 6.8 multiply_subtract_fusion.1
  1342.1 8.1 fusion.33
  1351.2 14.8 convolution_convert_fusion
  1366.1 17.2 convert_bitcast_fusion.1
  1383.2 15.4 convert_bitcast_fusion.2
  1398.7 14.6 convert_bitcast_fusion
  1413.3 46.0 %reduce-scatter.11.cloned.1.call-done = bf16[128,2048]{1,0:T(8,128)(2,1)} async-done(((bf16[2048,2048]{1,0:T(8,128)(2,1)}), bf16[128,2048]{1,0:T(8,128)(2,1)}) %reduce-scatter.11.cloned.1.call-update) | async-done | bytes 524304 | tf_op jit(solution)/shard_map/reduce_scatter | solution.py:238
  1459.3 247.3 %reduce-scatter.9.cloned.1.call-done = bf16[128,6144]{1,0:T(8,128)(2,1)} async-done(((bf16[2048,6144]{1,0:T(8,128)(2,1)}), bf16[128,6144]{1,0:T(8,128)(2,1)}) %reduce-scatter.9.cloned.1.call-update) | async-done | bytes 1572880 | tf_op jit(solution)/shard_map/reduce_scatter | solution.py:235
  1707.3 14.4 fusion.24
  1721.7 60.0 %all-reduce.3 = bf16[4352]{0:T(1024)(128)(2,1)S(1)} all-reduce(bf16[4352]{0:T(1024)(128)(2,1)S(1)} %pad_maximum_fusion.9), channel_id=6, replica_groups=mesh['rep'=2,'grp'=16] {'grp'}, use_global_device_ids=true, to_apply=%region_29.30.clone | all-reduce | flops 4352 | bytes 17408
  1781.8 5.1 psum.44
  1791.0 251.5 %all-reduce.7.cloned.1.call-done = (bf16[128,6144]{1,0:T(8,128)(2,1)}, bf16[128,2048]{1,0:T(8,128)(2,1)}, bf16[1,2048,1024]{2,1,0:T(8,128)(2,1)}, bf16[1,2048,1024]{2,1,0:T(8,128)(2,1)}, bf16[1,1024,2048]{2,1,0:T(8,128)(2,1)}) async-done(((bf16[128,6144]{1,0:T(8,128)(2,1)}, bf16[128,2048]{1,0:T(8,128)(2,1)}, bf16[1,2048,1024]{2,1,0:T(8,128)(2,1)}, bf16[1,2048,1024]{2,1,0:T(8,128)(2,1)}, ...) | async-done | bytes 14680080 | tf_op jit(solution)/shard_map/psum | solution.py:249
  (245 shorter events, 106.5 us)
Async XLA Ops:
  7.2 134.6 %all-gather.5.cloned.1.call-start = ((), (), s32[]{:S(2)}) async-start(), calls=%async_computation.8 | async-start | bytes 26738688 | tf_op jit(solution)/shard_map/all_gather | solution.py:54
  7.9 192.9 %all-gather.9.cloned.1.call-start = ((), (), s32[]{:S(2)}) async-start(), calls=%async_computation.10 | async-start | bytes 3145728 | tf_op jit(solution)/shard_map/all_gather | solution.py:77
  78.5 75.3 %copy-start.42 = (f32[256]{0:T(256)}, f32[256]{0:T(256)S(1)}, u32[]{:S(2)}) copy-start(f32[256]{0:T(256)S(1)} %add_rsqrt_fusion.3) | copy-start | bytes 3076
  78.5 83.0 %copy-start.54 = (f32[128]{0:T(128)}, f32[128]{0:T(128)S(1)}, u32[]{:S(2)}) copy-start(f32[128]{0:T(128)S(1)} %get-tuple-element.52) | copy-start | bytes 1540
  78.5 83.0 %copy-start.57 = (f32[128]{0:T(128)}, f32[128]{0:T(128)S(1)}, u32[]{:S(2)}) copy-start(f32[128]{0:T(128)S(1)} %get-tuple-element.53) | copy-start | bytes 1540
  78.5 63.2 %copy-start.29 = (f32[2048]{0:T(1024)}, f32[2048]{0:T(1024)S(1)}, u32[]{:S(2)}) copy-start(f32[2048]{0:T(1024)S(1)} %get-tuple-element.51) | copy-start | bytes 24580
  78.5 239.8 %copy-start.40 = (f32[2048]{0:T(1024)}, f32[2048]{0:T(1024)S(1)}, u32[]{:S(2)}) copy-start(f32[2048]{0:T(1024)S(1)} %get-tuple-element.50) | copy-start | bytes 24580
  79.7 84.3 %copy-start.27 = (f32[256,64]{1,0:T(8,128)}, f32[256,64]{1,0:T(8,128)S(1)}, u32[]{:S(2)}) copy-start(f32[256,64]{1,0:T(8,128)S(1)} %get-tuple-element.56) | copy-start | bytes 196612
  165.4 35.4 %copy-start.11 = (bf16[256,16,64]{2,0,1:T(8,128)(2,1)}, bf16[256,16,64]{2,0,1:T(8,128)(2,1)S(1)}, u32[]{:S(2)}) copy-start(bf16[256,16,64]{2,0,1:T(8,128)(2,1)S(1)} %get-tuple-element.36) | copy-start | bytes 1572868
  165.4 35.4 %copy-start.13 = (bf16[256,16,64]{2,0,1:T(8,128)(2,1)}, bf16[256,16,64]{2,0,1:T(8,128)(2,1)S(1)}, u32[]{:S(2)}) copy-start(bf16[256,16,64]{2,0,1:T(8,128)(2,1)S(1)} %get-tuple-element.37) | copy-start | bytes 1572868
  167.3 27.7 %copy-start.60 = (s32[1,512]{1,0:T(1,128)S(1)}, s32[1,512]{1,0:T(1,128)}, u32[]{:S(2)}) copy-start(s32[1,512]{1,0:T(1,128)} %param.18) | copy-start | bytes 6148
  167.4 68.7 %all-gather.7.cloned.1.call-start = ((), (), s32[]{:S(2)}) async-start(), calls=%async_computation.9 | async-start | bytes 3145728 | tf_op jit(solution)/shard_map/all_gather | solution.py:78
  170.2 142.2 %all-gather.11.cloned.1.call-start = ((), (), s32[]{:S(2)}) async-start(), calls=%async_computation.11 | async-start | bytes 8912896 | tf_op jit(solution)/shard_map/all_gather | solution.py:55
  176.8 18.3 copy-start.49
  195.3 40.8 %copy-start.24 = (pred[256,512]{1,0:T(8,128)(4,1)}, pred[256,512]{1,0:T(8,128)(4,1)S(1)}, u32[]{:S(2)}) copy-start(pred[256,512]{1,0:T(8,128)(4,1)S(1)} %broadcast_compare_fusion) | copy-start | bytes 393220
  207.9 34.7 %copy-start.38 = (f32[16,256]{1,0:T(8,128)}, f32[16,256]{1,0:T(8,128)S(1)}, u32[]{:S(2)}) copy-start(f32[16,256]{1,0:T(8,128)S(1)} %log_add_fusion) | copy-start | bytes 49156
  207.9 104.5 %copy-start.8 = (bf16[1,256,2048]{2,1,0:T(8,128)(2,1)S(1)}, bf16[1,256,2048]{2,1,0:T(8,128)(2,1)}, u32[]{:S(2)}) copy-start(bf16[1,256,2048]{2,1,0:T(8,128)(2,1)} %param.11) | copy-start | bytes 3145732
  242.6 75.7 %copy-start.17 = (bf16[16,128,256]{2,1,0:T(8,128)(2,1)}, bf16[16,128,256]{2,1,0:T(8,128)(2,1)S(1)}, u32[]{:S(2)}) copy-start(bf16[16,128,256]{2,1,0:T(8,128)(2,1)S(1)} %fusion.42) | copy-start | bytes 3145732
  318.3 11.5 copy-start.51
  329.8 173.7 %all-to-all-start = ((bf16[16,144,2048]{2,1,0:T(8,128)(2,1)}), bf16[16,144,2048]{2,1,0:T(8,128)(2,1)}, u32[]{:S(2)}, u32[]{:S(2)}) async-start(bf16[16,144,2048]{2,1,0:T(8,128)(2,1)} %bitcast.222), calls=%async_computation | async-start | bytes 18874368 | tf_op jit(solution)/shard_map/all_to_all | solution.py:120
  503.5 209.8 %all-to-all-start.2 = ((bf16[16,144,2048]{2,1,0:T(8,128)(2,1)}), bf16[16,144,2048]{2,1,0:T(8,128)(2,1)}, u32[]{:S(2)}, u32[]{:S(2)}) async-start(bf16[16,144,2048]{2,1,0:T(8,128)(2,1)} %bitcast.223), calls=%async_computation.2 | async-start | bytes 18874368 | tf_op jit(solution)/shard_map/all_to_all | solution.py:140
  544.5 16.1 copy-start.61
  754.7 209.8 %all-to-all-start.1 = ((bf16[16,144,2048]{2,1,0:T(8,128)(2,1)}), bf16[16,144,2048]{2,1,0:T(8,128)(2,1)}, u32[]{:S(2)}, u32[]{:S(2)}) async-start(bf16[16,144,2048]{2,1,0:T(8,128)(2,1)} %bitcast.225), calls=%async_computation.1 | async-start | bytes 18874368 | tf_op jit(solution)/shard_map/all_to_all | solution.py:126
  795.6 17.0 copy-start.62
  964.4 40.9 %copy-start.47 = (f32[1,256,8]{1,2,0:T(8,128)S(1)}, f32[1,256,8]{1,2,0:T(8,128)}, u32[]{:S(2)}) copy-start(f32[1,256,8]{1,2,0:T(8,128)} %param.20) | copy-start | bytes 24580
  964.4 41.1 %copy-start.50 = (s32[2048,1]{0,1:T(1,128)S(1)}, s32[2048,1]{0,1:T(1,128)}, u32[]{:S(2)}) copy-start(s32[2048,1]{0,1:T(1,128)} %copy-done.49) | copy-start | bytes 24580
  964.4 209.7 %all-to-all-start.3 = ((bf16[16,144,2048]{2,1,0:T(8,128)(2,1)}), bf16[16,144,2048]{2,1,0:T(8,128)(2,1)}, u32[]{:S(2)}, u32[]{:S(2)}) async-start(bf16[16,144,2048]{2,1,0:T(8,128)(2,1)} %bitcast.224), calls=%async_computation.3 | async-start | bytes 18874368 | tf_op jit(solution)/shard_map/all_to_all | solution.py:168
  1005.3 311.8 %reduce-scatter.5.cloned.1.call-start = ((), (), s32[]{:S(2)}) async-start(), calls=%async_computation.12 | async-start | bytes 3145728 | tf_op jit(solution)/shard_map/reduce_scatter | solution.py:205
  1195.6 11.5 copy-start.3
  1195.6 11.4 copy-start.41
  1195.6 11.4 copy-start.52
  1209.8 13.0 copy-start.23
  1228.3 8.4 copy-start.25
  1228.3 8.4 copy-start.39
  1236.7 7.1 slice-start
  1236.9 6.8 slice-start.1
  1249.0 102.1 %reduce-scatter.7.cloned.1.call-start = ((), (), s32[]{:S(2)}) async-start(), calls=%async_computation.13 | async-start | bytes 3145728 | tf_op jit(solution)/shard_map/reduce_scatter | solution.py:208
  1260.4 198.9 %reduce-scatter.11.cloned.1.call-start = ((), (), s32[]{:S(2)}) async-start(), calls=%async_computation.15 | async-start | bytes 8912896 | tf_op jit(solution)/shard_map/reduce_scatter | solution.py:238
  1266.3 440.4 %reduce-scatter.9.cloned.1.call-start = ((), (), s32[]{:S(2)}) async-start(), calls=%async_computation.14 | async-start | bytes 26738688 | tf_op jit(solution)/shard_map/reduce_scatter | solution.py:235
  1324.7 6.8 copy-start.7
  1324.7 6.8 copy-start.37
  1342.1 9.0 copy-start.9
  1342.1 9.0 copy-start.30
  1342.1 9.0 copy-start.43
  1366.0 676.5 %all-reduce.7.cloned.1.call-start = ((), (), s32[]{:S(2)}) async-start(), calls=%async_computation.16 | async-start | bytes 29360128 | tf_op jit(solution)/shard_map/psum | solution.py:249
  1366.1 32.6 %slice-start.2 = ((s8[4718592]{0:T(1024)(128)(4,1)}), s8[4194304]{0:T(1024)(128)(4,1)S(1)}, s32[]{:S(2)}) async-start(s8[4718592]{0:T(1024)(128)(4,1)} %bitcast.250), calls=%async_computation.19 | async-start | bytes 8388608
  1383.2 15.4 slice-start.3
  1707.3 14.4 copy-start.53
  (32 other events, 104.5 us)
Sparse Core Ops, SparseCore 0:
  9.6 132.1 all-gather.4
  167.5 33.3 all-gather.8
  203.0 33.0 all-gather.6
  238.1 74.2 all-gather.10
  1249.1 67.9 reduce-scatter.4
  1319.2 31.8 reduce-scatter.6
  1355.8 103.4 reduce-scatter.10
  1463.4 243.1 reduce-scatter.8
  1710.0 332.4 all-reduce.6
where the time goes:
time: 2080 us; the launch traced here: 2070 us
  waiting for transfers between devices  1310 us (63%)
  matrix products  245 us (12%)
  local copies, waits for them, and re-layouts  139 us (7%)
  blocking collectives  131 us (6%)
  starting transfers between devices  128 us (6%)
  other arithmetic  99.8 us (5%)
    psum x1, waiting for transfers between devices, per_device(): lax.psum(shard_qkv.astype(jnp.bfloat16), 'rep').astype(jnp.float32)  251 us
    reduce_scatter x1, waiting for transfers between devices, per_device(): lax.psum_scatter(grad_wqkv.astype(jnp.bfloat16), 'grp', scatter_dimension...  247 us
    all_to_all x1, waiting for transfers between devices, per_device(): lax.all_to_all(grad_rows.reshape(groups, capacity, D), 'grp', split_axis=...  147 us
    all_to_all x1, waiting for transfers between devices, per_device(): lax.all_to_all(grad_buffer, 'grp', split_axis=0, concat_axis=0, tiled=True)  138 us
    all_to_all x1, waiting for transfers between devices, per_device(): lax.all_to_all(expert_out.reshape(groups, capacity, D), 'grp', split_axis...  135 us
    all_to_all x1, waiting for transfers between devices, per_device(): lax.all_to_all(dispatch_rows(h2_b), 'grp', split_axis=0, concat_axis=0, t...  133 us
    unnamed x2, blocking collectives  126 us
    all_gather x1, waiting for transfers between devices, per_device(): lax.all_gather(w_out, 'grp', axis=0, tiled=True)  69.8 us
  transfers between devices with their start and end apart: 13, of which 13 were waited for; matrix products, arithmetic and copies ran while one was open for 15% of the time, Pallas kernels for 0%

commit v1 on v0

v1 whole, which is shorter than its diff:
```python
import jax
import jax.numpy as jnp
import numpy as np
from jax import lax
from jax.sharding import PartitionSpec as P

D = 2048
HEADS = 16
HD = 128
TOP = 8
BF = jnp.bfloat16
F32 = jnp.float32

epsilon = 1e-06
rope_base = 10000.0


def rms_forward(values, gain_vec):
    inverse = lax.rsqrt(jnp.mean(values * values, axis=-1, keepdims=True) + epsilon)
    normed = values * inverse
    return (normed * gain_vec, normed, inverse)


def rms_backward(grad_out, normed, inverse, gain_vec):
    scaled = grad_out * gain_vec
    grad_in = inverse * (scaled - normed * jnp.mean(scaled * normed, axis=-1, keepdims=True))
    return (grad_in, grad_out * normed)


def rotate(values, positions, direction):
    half_size = values.shape[-1] // 2
    frequency = rope_base ** (-2.0 * jnp.arange(half_size, dtype=jnp.float32) / values.shape[-1])
    angles = positions[:, None] * frequency[None, :]
    cosine_table = jnp.cos(angles)[:, None, :]
    sine_table = direction * jnp.sin(angles)[:, None, :]
    first_half = values[..., :half_size]
    second_half = values[..., half_size:]
    return jnp.concatenate(
        [
            first_half * cosine_table - second_half * sine_table,
            second_half * cosine_table + first_half * sine_table,
        ],
        axis=-1,
    )


def dot32(a, b):
    return jnp.dot(a, b, preferred_element_type=F32)


class Ring:
    def __init__(self, devices):
        self.devices = devices
        self.chips = devices // 2
        outer = 4 if self.chips % 4 == 0 else 2
        inner = self.chips // outer
        cycle = [(a, 0) for a in range(outer)]
        for step, a in enumerate(reversed(range(outer))):
            columns = range(1, inner)
            cycle += [(a, b) for b in (columns if step % 2 == 0 else reversed(columns))]
        self.cycle = [a * inner + b for a, b in cycle]
        self.place = {chip: i for i, chip in enumerate(self.cycle)}
        self.half = self.chips // 2

    def perm(self, shift):
        pairs = []
        for chip in range(self.chips):
            other = self.cycle[(self.place[chip] + shift) % self.chips]
            pairs += [(2 * chip + core, 2 * other + core) for core in range(2)]
        return pairs

    def table(self):
        out = np.zeros((self.devices, self.chips, 2), np.int32)
        for dev in range(self.devices):
            chip, core = dev // 2, dev % 2
            for d in range(self.chips):
                other = self.cycle[(self.place[chip] + d) % self.chips]
                out[dev, d, 0] = 2 * other + core
                out[dev, d, 1] = 2 * other + (1 - core)
        return out

    def ahead(self, v):
        return lax.ppermute(v, "grp", self.perm(1))

    def back(self, v):
        return lax.ppermute(v, "grp", self.perm(-1))

    def flip(self, v):
        return lax.ppermute(v, "grp", [(i, i ^ 1) for i in range(self.devices)])

    def gather(self, own):
        rows = own.shape[0] // 2
        blocks = {0: (own, self.flip(own))}
        up = down = own
        for step in range(1, self.half):
            up, down = self.ahead(up), self.back(down)
            blocks[-step % self.chips] = (up, self.flip(up))
            blocks[step] = (down, self.flip(down))
        first, last = self.ahead(up[:rows]), self.back(down[rows:])
        far = jnp.concatenate([first, last], axis=0)
        blocks[self.half] = (far, self.flip(far))
        return blocks

    def scatter_sum(self, blocks):
        def joined(d):
            same, other = blocks[d]
            return same.astype(F32) + self.flip(other.astype(BF)).astype(F32)

        far = joined(self.half).astype(BF)
        rows = far.shape[0] // 2
        up, down = self.ahead(far[:rows]), self.back(far[rows:])
        zero = jnp.zeros_like(up)
        up = jnp.concatenate([up, zero], axis=0)
        down = jnp.concatenate([zero, down], axis=0)
        for step in range(self.half - 1, 0, -1):
            up = self.ahead((joined(step) + up.astype(F32)).astype(BF))
            down = self.back((joined(-step % self.chips) + down.astype(F32)).astype(BF))
        return joined(0) + up.astype(F32) + down.astype(F32)


def per_device(
    tokens, w_qkv, w_out, gains, w_gate, w_up, w_down, segment_ids, routes, gate_weights, cotangent
):
    groups = lax.axis_size("grp")
    reps = lax.axis_size("rep")
    ring = Ring(groups)
    rep, grp = lax.axis_index("rep"), lax.axis_index("grp")
    rel = jnp.asarray(ring.table())[grp]
    rel_flat = rel.reshape(-1)
    tok_rows = tokens.shape[1]
    seq_len = segment_ids.shape[1]
    heads = HEADS // reps
    wide = heads * HD
    score_scale = HD ** (-0.5)

    def from_rep(v, k):
        return lax.ppermute(v, "rep", [((s + k) % reps, s) for s in range(reps)])

    def to_rep(v, k):
        return lax.ppermute(v, "rep", [(s, (s + k) % reps) for s in range(reps)])

    def rep_gather(v):
        return jnp.concatenate([v] + [from_rep(v, k) for k in range(1, reps)], axis=0)

    def rep_scatter(v):
        parts = v.reshape(reps, tok_rows, v.shape[-1])
        out = parts[0].astype(F32)
        for k in range(1, reps):
            out = out + to_rep(parts[k].astype(BF), k).astype(F32)
        return out

    own_b = tokens[0]
    seq_b = rep_gather(own_b)
    gates_f = gate_weights[0]
    experts = jnp.arange(groups, dtype=jnp.int32)
    weight_of = jnp.sum(
        jnp.where(routes[0][None] == experts[:, None, None], gates_f[None], 0.0), axis=-1
    )
    small = jnp.concatenate(
        [
            weight_of,
            jnp.broadcast_to(gains.astype(F32)[None], (groups, gains.shape[0])),
        ],
        axis=1,
    )
    small = lax.all_to_all(small, "grp", split_axis=0, concat_axis=0, tiled=True)
    gains_f = small[:, tok_rows:].reshape(-1)
    weight_in = small[:, :tok_rows][rel_flat]
    g_attn = gains_f[:D]
    g_ffn = gains_f[D : 2 * D]
    g_query = gains_f[2 * D : 2 * D + HD]
    g_key = gains_f[2 * D + HD :]

    my_qkv = lax.dynamic_index_in_dim(
        w_qkv.reshape(w_qkv.shape[0], 3, heads, reps, HD), rep, axis=3, keepdims=False
    ).reshape(w_qkv.shape[0], 3 * wide)
    shard = my_qkv.shape[0]
    full_qkv = jnp.zeros((D, 3 * wide), BF)
    for d, pair in ring.gather(my_qkv).items():
        for k in range(2):
            full_qkv = lax.dynamic_update_slice(full_qkv, pair[k], (rel[d, k] * shard, 0))
    full_out = lax.all_gather(w_out, "grp", axis=0, tiled=True)
    my_out = lax.dynamic_index_in_dim(
        full_out.reshape(heads, reps, HD, D), rep, axis=1, keepdims=False
    ).reshape(wide, D)

    seq_f = seq_b.astype(F32)
    normed_one, hat_one, inv_one = rms_forward(seq_f, g_attn)
    h1_b = normed_one.astype(BF)
    projected = dot32(h1_b, full_qkv)
    q_pre = projected[:, :wide].reshape(seq_len, heads, HD)
    k_pre = projected[:, wide : 2 * wide].reshape(seq_len, heads, HD)
    v_pre = projected[:, 2 * wide :]
    q_normed, q_hat, q_inv = rms_forward(q_pre, g_query)
    k_normed, k_hat, k_inv = rms_forward(k_pre, g_key)
    order = jnp.concatenate(
        [((rep + k) % reps) * tok_rows + jnp.arange(tok_rows, dtype=jnp.int32) for k in range(reps)]
    )
    positions = order.astype(F32)
    q_b = rotate(q_normed, positions, 1.0).astype(BF)
    k_b = rotate(k_normed, positions, 1.0).astype(BF)
    v_b = v_pre.astype(BF).reshape(seq_len, heads, HD)
    docs = segment_ids[0][order]
    same_doc = (docs[:, None] == docs[None, :])[None]
    scores = jnp.where(
        same_doc,
        jnp.einsum("qhd,khd->hqk", q_b, k_b, preferred_element_type=F32) * score_scale,
        -1e30,
    )
    row_max = jnp.max(scores, axis=-1, keepdims=True)
    log_total = row_max + jnp.log(jnp.sum(jnp.exp(scores - row_max), axis=-1, keepdims=True))
    probs_f = jnp.exp(scores - log_total)
    probs_b = probs_f.astype(BF)
    attended = jnp.einsum("hqk,khd->qhd", probs_b, v_b, preferred_element_type=F32)
    attended_b = attended.reshape(seq_len, wide).astype(BF)
    mid_rows = own_b.astype(F32) + rep_scatter(dot32(attended_b, my_out))
    normed_two, hat_two, inv_two = rms_forward(mid_rows, g_ffn)
    h2_b = normed_two.astype(BF)

    entries = tok_rows * TOP
    capacity = min(tok_rows, (9 * entries + 8 * groups - 1) // (8 * groups))
    named = weight_in > 0
    before = dot32(
        named.astype(BF), jnp.tri(tok_rows, dtype=BF).T
    )
    slot = jnp.where(named, before - 1.0, -1.0).astype(jnp.int32)
    pick = (slot[:, None, :] == jnp.arange(capacity, dtype=jnp.int32)[None, :, None]).astype(BF)
    row_weight = jnp.sum(pick.astype(F32) * weight_in[:, None, :], axis=-1)

    chips, half = ring.chips, ring.half
    batches = [(0,)] + [(d, chips - d) for d in range(1, half)] + [(half,)]

    def select(blocks, batch):
        return jnp.concatenate(
            [dot32(pick[2 * d + k], blocks[d][k]).astype(BF) for d in batch for k in range(2)], axis=0
        )

    def spread(rows, batch):
        out, at = {}, 0
        for d in batch:
            pair = []
            for k in range(2):
                part = rows[at : at + capacity]
                pair.append(
                    lax.dot_general(
                        pick[2 * d + k], part, (((0,), (0,)), ((), ())), preferred_element_type=F32
                    ).astype(BF)
                )
                at += capacity
            out[d] = tuple(pair)
        return out

    def weights_of(batch):
        return jnp.concatenate([row_weight[2 * d + k] for d in batch for k in range(2)])[:, None]

    dy_blocks = ring.gather(cotangent[0])
    h2_blocks = ring.gather(h2_b)
    acts, upres, gpres, rows_in, grads_in, grad_acts = [], [], [], [], [], []
    for batch in batches:
        picked = select(h2_blocks, batch)
        grads = (weights_of(batch) * select(dy_blocks, batch).astype(F32)).astype(BF)
        rows_in.append(picked)
        grads_in.append(grads)
        gpres.append(dot32(picked, w_gate[0]))
        upres.append(dot32(picked, w_up[0]))
        acts.append((jax.nn.silu(gpres[-1]) * upres[-1]).astype(BF))
        grad_acts.append(
            jnp.einsum("rd,fd->rf", grads, w_down[0], preferred_element_type=F32)
        )
    grad_gates, grad_ups = [], []
    back_blocks = {}
    for i in reversed(range(len(batches))):
        sig = jax.nn.sigmoid(gpres[i])
        grad_gates.insert(
            0, (grad_acts[i] * upres[i] * sig * (1.0 + gpres[i] * (1.0 - sig))).astype(BF)
        )
        grad_ups.insert(0, (grad_acts[i] * gpres[i] * sig).astype(BF))
        drow = (
            jnp.einsum("rf,df->rd", grad_gates[0], w_gate[0], preferred_element_type=F32)
            + jnp.einsum("rf,df->rd", grad_ups[0], w_up[0], preferred_element_type=F32)
        ).astype(BF)
        back_blocks.update(spread(drow, batches[i]))
    grad_h2 = ring.scatter_sum(back_blocks)

    acts_late, _ = lax.optimization_barrier((acts, grad_h2))
    out_blocks = {}
    for i in reversed(range(len(batches))):
        eout = dot32(acts_late[i], w_down[0]).astype(BF).astype(F32)
        out_blocks.update(spread((weights_of(batches[i]) * eout).astype(BF), batches[i]))
    result = mid_rows + ring.scatter_sum(out_blocks)

    all_rows = jnp.concatenate(rows_in, axis=0)
    all_grads = jnp.concatenate(grads_in, axis=0)
    all_acts = jnp.concatenate(acts, axis=0)
    all_gates = jnp.concatenate(grad_gates, axis=0)
    all_ups = jnp.concatenate(grad_ups, axis=0)

    def rep_sum(v):
        v = v.astype(BF)
        out = v.astype(F32)
        for k in range(1, reps):
            out = out + from_rep(v, k).astype(F32)
        return out

    grad_wdown = rep_sum(jnp.einsum("rf,rd->fd", all_acts, all_grads, preferred_element_type=F32))
    grad_wgate = rep_sum(jnp.einsum("rd,rf->df", all_rows, all_gates, preferred_element_type=F32))
    grad_wup = rep_sum(jnp.einsum("rd,rf->df", all_rows, all_ups, preferred_element_type=F32))

    grad_out = cotangent[0].astype(F32)
    grad_mid_norm, ffn_terms = rms_backward(grad_h2, hat_two, inv_two, g_ffn)
    grad_mid = grad_out + grad_mid_norm
    grad_branch_b = rep_gather(grad_mid.astype(BF))
    grad_wout = jnp.einsum("td,te->de", attended_b, grad_branch_b, preferred_element_type=F32)
    grad_attn_b = (
        jnp.einsum("te,de->td", grad_branch_b, my_out, preferred_element_type=F32)
        .astype(BF)
        .reshape(seq_len, heads, HD)
    )
    grad_probs = jnp.einsum("qhd,khd->hqk", grad_attn_b, v_b, preferred_element_type=F32)
    grad_vals = jnp.einsum("hqk,qhd->khd", probs_b, grad_attn_b, preferred_element_type=F32)
    grad_scores = (
        probs_f * (grad_probs - jnp.sum(probs_f * grad_probs, axis=-1, keepdims=True))
    ).astype(BF)
    grad_q = jnp.einsum("hqk,khd->qhd", grad_scores, k_b, preferred_element_type=F32) * score_scale
    grad_k = jnp.einsum("hqk,qhd->khd", grad_scores, q_b, preferred_element_type=F32) * score_scale
    grad_qn = rotate(grad_q, positions, -1.0)
    grad_kn = rotate(grad_k, positions, -1.0)
    grad_q_pre, query_terms = rms_backward(grad_qn, q_hat, q_inv, g_query)
    grad_k_pre, key_terms = rms_backward(grad_kn, k_hat, k_inv, g_key)
    grad_proj = jnp.concatenate(
        [
            grad_q_pre.reshape(seq_len, wide),
            grad_k_pre.reshape(seq_len, wide),
            grad_vals.reshape(seq_len, wide),
        ],
        axis=1,
    ).astype(BF)
    grad_wqkv = jnp.einsum("td,te->de", h1_b, grad_proj, preferred_element_type=F32).astype(BF)
    grad_h1 = rep_scatter(
        jnp.einsum("te,de->td", grad_proj, full_qkv, preferred_element_type=F32)
    )
    grad_rows_one, attn_terms = rms_backward(
        grad_h1, hat_one[:tok_rows], inv_one[:tok_rows], g_attn
    )
    grad_tokens = grad_mid + grad_rows_one

    qkv_blocks = {
        d: tuple(
            lax.dynamic_slice(grad_wqkv, (rel[d, k] * shard, 0), (shard, 3 * wide))
            for k in range(2)
        )
        for d in range(chips)
    }
    shard_qkv = ring.scatter_sum(qkv_blocks).astype(BF)
    qkv_all = [shard_qkv] + [from_rep(shard_qkv, k) for k in range(1, reps)]
    columns = jnp.stack(qkv_all, axis=0).reshape(reps, shard, 3, heads, HD)
    columns = columns[(jnp.arange(reps) - rep) % reps]
    shard_qkv = columns.transpose(1, 2, 3, 0, 4).reshape(shard, 3 * D).astype(F32)

    zero_out = jnp.zeros((heads, reps, HD, D), BF)
    whole_out = lax.dynamic_update_slice(
        zero_out, grad_wout.astype(BF).reshape(heads, 1, HD, D), (0, rep, 0, 0)
    ).reshape(D, D)
    shard_out = lax.psum(
        lax.psum_scatter(whole_out, "grp", scatter_dimension=0, tiled=True), "rep"
    ).astype(F32)

    grad_gains = jnp.concatenate(
        [
            jnp.sum(attn_terms, axis=0),
            jnp.sum(ffn_terms, axis=0),
            jnp.sum(query_terms, axis=(0, 1)),
            jnp.sum(key_terms, axis=(0, 1)),
        ]
    )
    pieces = lax.all_to_all(
        grad_gains.reshape(groups, -1), "grp", split_axis=0, concat_axis=0, tiled=True
    )
    shard_gains = jnp.sum(pieces, axis=0)
    total = shard_gains
    for k in range(1, reps):
        total = total + from_rep(shard_gains, k)
    return (
        result[None],
        grad_tokens[None],
        shard_qkv,
        shard_out,
        total,
        grad_wgate[None],
        grad_wup[None],
        grad_wdown[None],
    )


def solution(mesh):
    in_specs = (
        P("grp", "rep", None),
        P("grp", None),
        P("grp", None),
        P("grp"),
        P("grp", None, None),
        P("grp", None, None),
        P("grp", None, None),
        P("grp", None),
        P("grp", "rep", None),
        P("grp", "rep", None),
        P("grp", "rep", None),
    )
    out_specs = (
        P("grp", "rep", None),
        P("grp", "rep", None),
        P("grp", None),
        P("grp", None),
        P("grp"),
        P("grp", None, None),
        P("grp", None, None),
        P("grp", None, None),
    )
    return jax.shard_map(
        per_device, mesh=mesh, in_specs=in_specs, out_specs=out_specs, check_vma=False
    )
```

time: 2080 us -> 1200 us (0.58)
  waiting for transfers between devices: 1310 us -> 527 us
  blocking collectives: 131 us -> 0 us
  matrix products: 245 us -> 290 us
    all_to_all x4 -> x2, waiting for transfers between devices: 554 us -> 0.01 us  [the longest x1 0.01 us: per_device(): lax.all_to_all(small, 'grp', split_axis=0, concat_axis=0, tiled=True)]
    ppermute x0 -> x105, waiting for transfers between devices: none -> 527 us  [the longest x7 213 us: from_rep(): return lax.ppermute(v, 'rep', [((s + k) % reps, s) for s in range(reps)])]
    reduce_scatter x4 -> x1, waiting for transfers between devices: 338 us -> 0.01 us  [per_device(): lax.psum_scatter(whole_out, 'grp', scatter_dimension=0, tiled=True)]
    psum x1, waiting for transfers between devices: 251 us -> 0.01 us  [per_device(): lax.psum(lax.psum_scatter(whole_out, 'grp', scatter_dimension=0, tiled=Tr...]
    all_gather x4 -> x1, waiting for transfers between devices: 166 us -> 0.01 us  [per_device(): full_out = lax.all_gather(w_out, 'grp', axis=0, tiled=True)]
    unnamed x2 -> x0, blocking collectives: 126 us -> none
    all_to_all x4 -> x2, starting transfers between devices: 128 us -> 9.55 us  [the longest x1 5.91 us: per_device(): lax.all_to_all(small, 'grp', split_axis=0, concat_axis=0, tiled=True)]
    ppermute x0 -> x105, starting transfers between devices: none -> 102 us  [the longest x24 48.6 us: back(): return lax.ppermute(v, 'grp', self.perm(-1))]
  transfers between devices with their start and end apart: 13 -> 110, of which waited for: 13 -> 30; matrix products, arithmetic and copies ran while one was open for 15% -> 40% of each run, Pallas kernels for 0% -> 0%
where the time goes in v1:
time: 1200 us; the launch traced here: 1190 us
  waiting for transfers between devices  527 us (44%)
  matrix products  290 us (24%)
  local copies, waits for them, and re-layouts  122 us (10%)
  other arithmetic  115 us (10%)
  starting transfers between devices  112 us (9%)
  between operations  26.6 us (2%)
    ppermute x7, waiting for transfers between devices, from_rep(): return lax.ppermute(v, 'rep', [((s + k) % reps, s) for s in range(reps)])  213 us
    ppermute x24, waiting for transfers between devices, back(): return lax.ppermute(v, 'grp', self.perm(-1))  158 us
    ppermute x24, waiting for transfers between devices, ahead(): return lax.ppermute(v, 'grp', self.perm(1))  142 us
    dot_general x50, matrix products, dot32(): return jnp.dot(a, b, preferred_element_type=F32)  102 us
    ppermute x24, starting transfers between devices, back(): return lax.ppermute(v, 'grp', self.perm(-1))  48.6 us
    dot_general x32, matrix products, spread(): lax.dot_general(pick[2 * d + k], part, (((0,), (0,)), ((), ())), preferre...  44.2 us
    ppermute x24, starting transfers between devices, ahead(): return lax.ppermute(v, 'grp', self.perm(1))  37 us
    unnamed x270, local copies, waits for them, and re-layouts  34.3 us
  transfers between devices with their start and end apart: 110, of which 30 were waited for; matrix products, arithmetic and copies ran while one was open for 40% of the time, Pallas kernels for 0%

profile of v1, /device:TPU:0, one launch (start us, length us, event | category | flops | bytes accessed | tf_op | source)
XLA Modules:
  0.0 1192.5 jit_solution(5099936604191144063)
XLA Ops:
  17.8 5.9 all-to-all-start
  40.4 6.1 broadcast_in_dim.47
  68.8 29.7 %collective-permute-done.38 = bf16[256,2048]{1,0:T(8,128)(2,1)S(1)} collective-permute-done((bf16[256,2048]{1,0:T(8,128)(2,1)S(1)}, bf16[256,2048]{1,0:T(8,128)(2,1)S(1)}, u32[]{:S(2)}, u32[]{:S(2)}) %collective-permute-start.38) | collective-permute-done | bytes 1048608 | tf_op jit(solution)/shard_map/ppermute | solution.py:83
  98.5 16.3 %collective-permute-start.8 = (bf16[128,3072]{0,1:T(8,128)(2,1)}, bf16[128,3072]{0,1:T(8,128)(2,1)}, u32[]{:S(2)}, u32[]{:S(2)}) collective-permute-start(bf16[128,3072]{0,1:T(8,128)(2,1)} %collective-permute-done.4), channel_id=1, source_target_pairs={{0,2},{1,3},{2,6},{3,7},{4,0},{5,1},{6,10},{7,11},{8,4},{9,5},{10,... | collective-permute-start | bytes 2359304 | tf_op jit(solution)/shard_map/ppermute | solution.py:86
  124.1 5.1 collective-permute-done.6
  141.5 11.1 collective-permute-done.43
  185.3 17.8 %collective-permute-done.14 = bf16[64,3072]{1,0:T(8,128)(2,1)} collective-permute-done((bf16[64,3072]{1,0:T(8,128)(2,1)}, bf16[64,3072]{1,0:T(8,128)(2,1)}, u32[]{:S(2)}, u32[]{:S(2)}) %collective-permute-start.14) | collective-permute-done | bytes 393248 | tf_op jit(solution)/shard_map/ppermute | solution.py:83
  207.6 5.8 collective-permute-done.15
  249.5 9.7 fusion.156
  297.1 5.1 constant_dynamic-update-slice_fusion.38
  307.9 13.5 %collective-permute-done.17 = bf16[256,2048]{1,0:T(8,128)(2,1)S(1)} collective-permute-done((bf16[256,2048]{1,0:T(8,128)(2,1)S(1)}, bf16[256,2048]{1,0:T(8,128)(2,1)S(1)}, u32[]{:S(2)}, u32[]{:S(2)}) %collective-permute-start.17) | collective-permute-done | bytes 1048608 | tf_op jit(solution)/shard_map/ppermute | solution.py:140
  330.2 19.1 %collective-permute-done.19 = bf16[256,2048]{1,0:T(8,128)(2,1)S(1)} collective-permute-done((bf16[256,2048]{1,0:T(8,128)(2,1)S(1)}, bf16[256,2048]{1,0:T(8,128)(2,1)S(1)}, u32[]{:S(2)}, u32[]{:S(2)}) %collective-permute-start.19) | collective-permute-done | bytes 1048608 | tf_op jit(solution)/shard_map/ppermute | solution.py:86
  365.2 9.8 constant_dynamic-update-slice_fusion.25
  395.0 9.8 constant_dynamic-update-slice_fusion.24
  404.8 6.5 fusion.27
  411.9 5.8 add_convert_fusion.1
  423.2 9.4 collective-permute-done.31
  440.6 10.5 constant_dynamic-update-slice_fusion.23
  451.4 6.8 fusion.25
  478.5 14.1 %convolution_convert_fusion.1 = bf16[1024,2048]{1,0:T(8,128)(2,1)S(1)} fusion(bf16[2304,1024]{1,0:T(8,128)(2,1)} %get-tuple-element.97, bf16[2304,2048]{1,0:T(8,128)(2,1)} %constant_dynamic-update-slice_fusion.37), kind=kOutput, calls=%fused_computation.87 | convolution fusion | flops 9665773568 | bytes 18350080 | tf_op jit(solution)/shard_map/rf,rd->fd/dot_general | solution.py:305
  495.3 14.3 %convolution_convert_fusion.2 = bf16[2048,1024]{1,0:T(8,128)(2,1)S(1)} fusion(bf16[2304,2048]{1,0:T(8,128)(2,1)} %copy-done.79, bf16[2304,1024]{1,0:T(8,128)(2,1)} %get-tuple-element.99), kind=kOutput, calls=%fused_computation.88 | convolution fusion | flops 9665773568 | bytes 18350080 | tf_op jit(solution)/shard_map/rd,rf->df/dot_general | solution.py:307
  513.4 5.1 collective-permute-done.56
  522.3 15.4 %convolution_convert_fusion.3 = bf16[2048,1024]{1,0:T(8,128)(2,1)} fusion(bf16[2304,2048]{1,0:T(8,128)(2,1)} %copy-done.79, bf16[2304,1024]{1,0:T(8,128)(2,1)} %get-tuple-element.44), kind=kOutput, calls=%fused_computation.89 | convolution fusion | flops 9665773568 | bytes 18350080 | tf_op jit(solution)/shard_map/rd,rf->df/dot_general | solution.py:306
  547.9 23.1 %collective-permute-done.64 = bf16[256,2048]{1,0:T(8,128)(2,1)S(1)} collective-permute-done((bf16[256,2048]{1,0:T(8,128)(2,1)S(1)}, bf16[256,2048]{1,0:T(8,128)(2,1)S(1)}, u32[]{:S(2)}, u32[]{:S(2)}) %collective-permute-start.64) | collective-permute-done | bytes 1048608 | tf_op jit(solution)/shard_map/ppermute | solution.py:86
  572.8 30.3 %collective-permute-done.104 = bf16[1024,2048]{1,0:T(8,128)(2,1)S(1)} collective-permute-done((bf16[1024,2048]{1,0:T(8,128)(2,1)S(1)}, bf16[1024,2048]{1,0:T(8,128)(2,1)S(1)}, u32[]{:S(2)}, u32[]{:S(2)}) %collective-permute-start.104) | collective-permute-done | bytes 4194336 | tf_op jit(solution)/shard_map/ppermute | solution.py:137
  603.9 5.3 add_bitcast_fusion
  609.2 83.9 %collective-permute-done.103 = bf16[2048,1024]{1,0:T(8,128)(2,1)S(1)} collective-permute-done((bf16[2048,1024]{1,0:T(8,128)(2,1)S(1)}, bf16[2048,1024]{1,0:T(8,128)(2,1)S(1)}, u32[]{:S(2)}, u32[]{:S(2)}) %collective-permute-start.103) | collective-permute-done | bytes 4194336 | tf_op jit(solution)/shard_map/ppermute | solution.py:137
  693.1 5.4 add_bitcast_fusion.1
  698.5 84.1 %collective-permute-done.102 = bf16[2048,1024]{1,0:T(8,128)(2,1)} collective-permute-done((bf16[2048,1024]{1,0:T(8,128)(2,1)}, bf16[2048,1024]{1,0:T(8,128)(2,1)}, u32[]{:S(2)}, u32[]{:S(2)}) %collective-permute-start.102) | collective-permute-done | bytes 4194336 | tf_op jit(solution)/shard_map/ppermute | solution.py:137
  782.5 8.8 add_bitcast_fusion.2
  827.4 14.5 %collective-permute-done.82 = bf16[256,2048]{1,0:T(8,128)(2,1)S(1)} collective-permute-done((bf16[256,2048]{1,0:T(8,128)(2,1)S(1)}, bf16[256,2048]{1,0:T(8,128)(2,1)S(1)}, u32[]{:S(2)}, u32[]{:S(2)}) %collective-permute-start.82) | collective-permute-done | bytes 1048608 | tf_op jit(solution)/shard_map/ppermute | solution.py:137
  848.5 7.4 multiply_reduce_fusion
  882.5 5.6 fusion.143
  888.2 9.7 convolution_convert_fusion
  921.5 10.3 fusion.147
  938.9 25.4 %collective-permute-done.90 = bf16[128,3072]{1,0:T(8,128)(2,1)S(1)} collective-permute-done((bf16[128,3072]{1,0:T(8,128)(2,1)S(1)}, bf16[128,3072]{1,0:T(8,128)(2,1)S(1)}, u32[]{:S(2)}, u32[]{:S(2)}) %collective-permute-start.90) | collective-permute-done | bytes 786464 | tf_op jit(solution)/shard_map/ppermute | solution.py:83
  964.2 8.5 collective-permute-start.71
  977.8 18.4 %collective-permute-done.71 = bf16[128,2048]{1,0:T(8,128)(2,1)S(1)} collective-permute-done((bf16[128,2048]{1,0:T(8,128)(2,1)S(1)}, bf16[128,2048]{1,0:T(8,128)(2,1)S(1)}, u32[]{:S(2)}, u32[]{:S(2)}) %collective-permute-start.71) | collective-permute-done | bytes 524320 | tf_op jit(solution)/shard_map/ppermute | solution.py:83
  999.1 4.9 collective-permute-start.96
  1009.7 6.7 collective-permute-done.96
  1023.0 20.6 %collective-permute-done.78 = bf16[128,2048]{1,0:T(8,128)(2,1)S(1)} collective-permute-done((bf16[128,2048]{1,0:T(8,128)(2,1)}, bf16[128,2048]{1,0:T(8,128)(2,1)S(1)}, u32[]{:S(2)}, u32[]{:S(2)}) %collective-permute-start.78) | collective-permute-done | bytes 524320 | tf_op jit(solution)/shard_map/ppermute | solution.py:86
  1046.6 11.7 collective-permute-done.72
  1068.4 17.8 %collective-permute-done.79 = bf16[256,2048]{1,0:T(8,128)(2,1)S(1)} collective-permute-done((bf16[256,2048]{1,0:T(8,128)(2,1)}, bf16[256,2048]{1,0:T(8,128)(2,1)S(1)}, u32[]{:S(2)}, u32[]{:S(2)}) %collective-permute-start.79) | collective-permute-done | bytes 1048608 | tf_op jit(solution)/shard_map/ppermute | solution.py:86
  1092.6 14.1 %collective-permute-done.98 = bf16[128,3072]{1,0:T(8,128)(2,1)S(1)} collective-permute-done((bf16[128,3072]{1,0:T(8,128)(2,1)S(1)}, bf16[128,3072]{1,0:T(8,128)(2,1)S(1)}, u32[]{:S(2)}, u32[]{:S(2)}) %collective-permute-start.98) | collective-permute-done | bytes 786464 | tf_op jit(solution)/shard_map/ppermute | solution.py:86
  1109.5 16.5 %collective-permute-done.80 = bf16[256,2048]{1,0:T(8,128)(2,1)S(1)} collective-permute-done((bf16[256,2048]{1,0:T(8,128)(2,1)S(1)}, bf16[256,2048]{1,0:T(8,128)(2,1)S(1)}, u32[]{:S(2)}, u32[]{:S(2)}) %collective-permute-start.80) | collective-permute-done | bytes 1048608 | tf_op jit(solution)/shard_map/ppermute | solution.py:86
  1134.1 12.3 %collective-permute-done.99 = bf16[128,3072]{1,0:T(8,128)(2,1)S(1)} collective-permute-done((bf16[128,3072]{1,0:T(8,128)(2,1)S(1)}, bf16[128,3072]{1,0:T(8,128)(2,1)S(1)}, u32[]{:S(2)}, u32[]{:S(2)}) %collective-permute-start.99) | collective-permute-done | bytes 786464 | tf_op jit(solution)/shard_map/ppermute | solution.py:86
  1153.0 13.4 %collective-permute-done.81 = bf16[256,2048]{1,0:T(8,128)(2,1)} collective-permute-done((bf16[256,2048]{1,0:T(8,128)(2,1)}, bf16[256,2048]{1,0:T(8,128)(2,1)}, u32[]{:S(2)}, u32[]{:S(2)}) %collective-permute-start.81) | collective-permute-done | bytes 1048608 | tf_op jit(solution)/shard_map/ppermute | solution.py:86
  1166.4 7.1 add_bitcast_fusion.3
  (705 shorter events, 447.3 us)
Async XLA Ops:
  12.1 42.4 %collective-permute-start.1 = (bf16[128,3072]{0,1:T(8,128)(2,1)}, bf16[128,3072]{0,1:T(8,128)(2,1)}, u32[]{:S(2)}, u32[]{:S(2)}) collective-permute-start(bf16[128,3072]{0,1:T(8,128)(2,1)} %bitcast.4), channel_id=1, source_target_pairs={{0,1},{1,0},{2,3},{3,2},{4,5},{5,4},{6,7},{7,6},{8,9},{9,8},{10,11... | collective-permute-start | bytes 2359304 | tf_op jit(solution)/shard_map/ppermute | solution.py:89
  12.5 45.6 %collective-permute-start.2 = (bf16[128,3072]{0,1:T(8,128)(2,1)}, bf16[128,3072]{0,1:T(8,128)(2,1)}, u32[]{:S(2)}, u32[]{:S(2)}) collective-permute-start(bf16[128,3072]{0,1:T(8,128)(2,1)} %bitcast.4), channel_id=1, source_target_pairs={{0,4},{1,5},{2,0},{3,1},{4,8},{5,9},{6,2},{7,3},{8,12},{9,13},{10,... | collective-permute-start | bytes 2359304 | tf_op jit(solution)/shard_map/ppermute | solution.py:83
  15.1 47.8 %collective-permute-start.4 = (bf16[128,3072]{0,1:T(8,128)(2,1)}, bf16[128,3072]{0,1:T(8,128)(2,1)}, u32[]{:S(2)}, u32[]{:S(2)}) collective-permute-start(bf16[128,3072]{0,1:T(8,128)(2,1)} %bitcast.4), channel_id=1, source_target_pairs={{0,2},{1,3},{2,6},{3,7},{4,0},{5,1},{6,10},{7,11},{8,4},{9,5},{10,... | collective-permute-start | bytes 2359304 | tf_op jit(solution)/shard_map/ppermute | solution.py:86
  15.1 45.9 %collective-permute-start = (bf16[256,2048]{1,0:T(8,128)(2,1)S(1)}, bf16[256,2048]{1,0:T(8,128)(2,1)}, u32[]{:S(2)}, u32[]{:S(2)}) collective-permute-start(bf16[256,2048]{1,0:T(8,128)(2,1)S(1)} %bitcast.503), channel_id=1, source_target_pairs={{16,0},{0,16},{17,1},{1,17},{18,2},{2,18},{19,3},{3,19},{20,4},{4,... | collective-permute-start | bytes 3145736 | tf_op jit(solution)/shard_map/ppermute | solution.py:137
  23.7 267.0 %all-gather.2.cloned.1.call-start = ((), (), s32[]{:S(2)}) async-start(), calls=%async_computation.3 | async-start | bytes 8912896 | tf_op jit(solution)/shard_map/all_gather | solution.py:182
  24.5 1125.6 %reduce-scatter.2.cloned.1.call-start = ((), (), s32[]{:S(2)}) async-start(), calls=%async_computation.4 | async-start | bytes 8912896 | tf_op jit(solution)/shard_map/reduce_scatter | solution.py:365
  24.5 40.2 %collective-permute-start.34 = (bf16[256,2048]{1,0:T(8,128)(2,1)S(1)}, bf16[256,2048]{1,0:T(8,128)(2,1)}, u32[]{:S(2)}, u32[]{:S(2)}) collective-permute-start(bf16[256,2048]{1,0:T(8,128)(2,1)S(1)} %bitcast.500), channel_id=1, source_target_pairs={{0,1},{1,0},{2,3},{3,2},{4,5},{5,4},{6,7},{7,6},{8,9},{9,8},{10,11... | collective-permute-start | bytes 3145736 | tf_op jit(solution)/shard_map/ppermute | solution.py:89
  54.5 44.0 %collective-permute-start.38 = (bf16[256,2048]{1,0:T(8,128)(2,1)S(1)}, bf16[256,2048]{1,0:T(8,128)(2,1)S(1)}, u32[]{:S(2)}, u32[]{:S(2)}) collective-permute-start(bf16[256,2048]{1,0:T(8,128)(2,1)S(1)} %bitcast.501), channel_id=1, source_target_pairs={{0,4},{1,5},{2,0},{3,1},{4,8},{5,9},{6,2},{7,3},{8,12},{9,13},{10,... | collective-permute-start | bytes 3145736 | tf_op jit(solution)/shard_map/ppermute | solution.py:83
  58.2 60.9 %collective-permute-start.36 = (bf16[256,2048]{1,0:T(8,128)(2,1)S(1)}, bf16[256,2048]{1,0:T(8,128)(2,1)S(1)}, u32[]{:S(2)}, u32[]{:S(2)}) collective-permute-start(bf16[256,2048]{1,0:T(8,128)(2,1)S(1)} %bitcast.502), channel_id=1, source_target_pairs={{0,2},{1,3},{2,6},{3,7},{4,0},{5,1},{6,10},{7,11},{8,4},{9,5},{10,... | collective-permute-start | bytes 3145736 | tf_op jit(solution)/shard_map/ppermute | solution.py:86
  61.0 58.4 %collective-permute-start.3 = (bf16[128,3072]{0,1:T(8,128)(2,1)}, bf16[128,3072]{0,1:T(8,128)(2,1)S(1)}, u32[]{:S(2)}, u32[]{:S(2)}) collective-permute-start(bf16[128,3072]{0,1:T(8,128)(2,1)} %collective-permute-done.2), channel_id=1, source_target_pairs={{0,1},{1,0},{2,3},{3,2},{4,5},{5,4},{6,7},{7,6},{8,9},{9,8},{10,11... | collective-permute-start | bytes 2359304 | tf_op jit(solution)/shard_map/ppermute | solution.py:89
  63.0 66.2 %collective-permute-start.6 = (bf16[128,3072]{0,1:T(8,128)(2,1)}, bf16[128,3072]{0,1:T(8,128)(2,1)}, u32[]{:S(2)}, u32[]{:S(2)}) collective-permute-start(bf16[128,3072]{0,1:T(8,128)(2,1)} %collective-permute-done.2), channel_id=1, source_target_pairs={{0,4},{1,5},{2,0},{3,1},{4,8},{5,9},{6,2},{7,3},{8,12},{9,13},{10,... | collective-permute-start | bytes 2359304 | tf_op jit(solution)/shard_map/ppermute | solution.py:83
  64.7 58.3 %collective-permute-start.5 = (bf16[128,3072]{0,1:T(8,128)(2,1)}, bf16[128,3072]{0,1:T(8,128)(2,1)S(1)}, u32[]{:S(2)}, u32[]{:S(2)}) collective-permute-start(bf16[128,3072]{0,1:T(8,128)(2,1)} %collective-permute-done.4), channel_id=1, source_target_pairs={{0,1},{1,0},{2,3},{3,2},{4,5},{5,4},{6,7},{7,6},{8,9},{9,8},{10,11... | collective-permute-start | bytes 2359304 | tf_op jit(solution)/shard_map/ppermute | solution.py:89
  98.5 36.7 %collective-permute-start.8 = (bf16[128,3072]{0,1:T(8,128)(2,1)}, bf16[128,3072]{0,1:T(8,128)(2,1)}, u32[]{:S(2)}, u32[]{:S(2)}) collective-permute-start(bf16[128,3072]{0,1:T(8,128)(2,1)} %collective-permute-done.4), channel_id=1, source_target_pairs={{0,2},{1,3},{2,6},{3,7},{4,0},{5,1},{6,10},{7,11},{8,4},{9,5},{10,... | collective-permute-start | bytes 2359304 | tf_op jit(solution)/shard_map/ppermute | solution.py:86
  134.9 37.5 %collective-permute-start.7 = (bf16[128,3072]{0,1:T(8,128)(2,1)}, bf16[128,3072]{0,1:T(8,128)(2,1)}, u32[]{:S(2)}, u32[]{:S(2)}) collective-permute-start(bf16[128,3072]{0,1:T(8,128)(2,1)} %collective-permute-done.6), channel_id=1, source_target_pairs={{0,1},{1,0},{2,3},{3,2},{4,5},{5,4},{6,7},{7,6},{8,9},{9,8},{10,11... | collective-permute-start | bytes 2359304 | tf_op jit(solution)/shard_map/ppermute | solution.py:89
  137.1 41.0 %collective-permute-start.9 = (bf16[128,3072]{0,1:T(8,128)(2,1)}, bf16[128,3072]{0,1:T(8,128)(2,1)}, u32[]{:S(2)}, u32[]{:S(2)}) collective-permute-start(bf16[128,3072]{0,1:T(8,128)(2,1)} %collective-permute-done.8), channel_id=1, source_target_pairs={{0,1},{1,0},{2,3},{3,2},{4,5},{5,4},{6,7},{7,6},{8,9},{9,8},{10,11... | collective-permute-start | bytes 2359304 | tf_op jit(solution)/shard_map/ppermute | solution.py:89
  161.4 59.7 %collective-permute-start.44 = (bf16[256,2048]{1,0:T(8,128)(2,1)}, bf16[256,2048]{1,0:T(8,128)(2,1)}, u32[]{:S(2)}, u32[]{:S(2)}) collective-permute-start(bf16[256,2048]{1,0:T(8,128)(2,1)} %collective-permute-done.43), channel_id=1, source_target_pairs={{0,1},{1,0},{2,3},{3,2},{4,5},{5,4},{6,7},{7,6},{8,9},{9,8},{10,11... | collective-permute-start | bytes 3145736 | tf_op jit(solution)/shard_map/ppermute | solution.py:89
  169.0 47.5 %collective-permute-start.48 = (bf16[256,2048]{1,0:T(8,128)(2,1)}, bf16[256,2048]{1,0:T(8,128)(2,1)}, u32[]{:S(2)}, u32[]{:S(2)}) collective-permute-start(bf16[256,2048]{1,0:T(8,128)(2,1)} %collective-permute-done.43), channel_id=1, source_target_pairs={{0,4},{1,5},{2,0},{3,1},{4,8},{5,9},{6,2},{7,3},{8,12},{9,13},{10,... | collective-permute-start | bytes 3145736 | tf_op jit(solution)/shard_map/ppermute | solution.py:83
  178.2 40.8 %collective-permute-start.46 = (bf16[256,2048]{1,0:T(8,128)(2,1)}, bf16[256,2048]{1,0:T(8,128)(2,1)}, u32[]{:S(2)}, u32[]{:S(2)}) collective-permute-start(bf16[256,2048]{1,0:T(8,128)(2,1)} %collective-permute-done.41), channel_id=1, source_target_pairs={{0,2},{1,3},{2,6},{3,7},{4,0},{5,1},{6,10},{7,11},{8,4},{9,5},{10,... | collective-permute-start | bytes 3145736 | tf_op jit(solution)/shard_map/ppermute | solution.py:86
  180.9 43.2 %collective-permute-start.42 = (bf16[256,2048]{1,0:T(8,128)(2,1)}, bf16[256,2048]{1,0:T(8,128)(2,1)}, u32[]{:S(2)}, u32[]{:S(2)}) collective-permute-start(bf16[256,2048]{1,0:T(8,128)(2,1)} %collective-permute-done.41), channel_id=1, source_target_pairs={{0,1},{1,0},{2,3},{3,2},{4,5},{5,4},{6,7},{7,6},{8,9},{9,8},{10,11... | collective-permute-start | bytes 3145736 | tf_op jit(solution)/shard_map/ppermute | solution.py:89
  221.1 62.2 %collective-permute-start.51 = (bf16[128,2048]{1,0:T(8,128)(2,1)}, bf16[128,2048]{1,0:T(8,128)(2,1)}, u32[]{:S(2)}, u32[]{:S(2)}) collective-permute-start(bf16[128,2048]{1,0:T(8,128)(2,1)} %slice.613), channel_id=1, source_target_pairs={{0,4},{1,5},{2,0},{3,1},{4,8},{5,9},{6,2},{7,3},{8,12},{9,13},{10,... | collective-permute-start | bytes 1572872 | tf_op jit(solution)/shard_map/ppermute | solution.py:83
  224.1 60.3 %collective-permute-start.52 = (bf16[128,2048]{1,0:T(8,128)(2,1)}, bf16[128,2048]{1,0:T(8,128)(2,1)}, u32[]{:S(2)}, u32[]{:S(2)}) collective-permute-start(bf16[128,2048]{1,0:T(8,128)(2,1)} %slice.614), channel_id=1, source_target_pairs={{0,2},{1,3},{2,6},{3,7},{4,0},{5,1},{6,10},{7,11},{8,4},{9,5},{10,... | collective-permute-start | bytes 1572872 | tf_op jit(solution)/shard_map/ppermute | solution.py:86
  240.1 45.9 %collective-permute-start.49 = (bf16[256,2048]{1,0:T(8,128)(2,1)}, bf16[256,2048]{1,0:T(8,128)(2,1)}, u32[]{:S(2)}, u32[]{:S(2)}) collective-permute-start(bf16[256,2048]{1,0:T(8,128)(2,1)} %collective-permute-done.48), channel_id=1, source_target_pairs={{0,1},{1,0},{2,3},{3,2},{4,5},{5,4},{6,7},{7,6},{8,9},{9,8},{10,11... | collective-permute-start | bytes 3145736 | tf_op jit(solution)/shard_map/ppermute | solution.py:89
  244.5 43.9 %collective-permute-start.47 = (bf16[256,2048]{1,0:T(8,128)(2,1)}, bf16[256,2048]{1,0:T(8,128)(2,1)}, u32[]{:S(2)}, u32[]{:S(2)}) collective-permute-start(bf16[256,2048]{1,0:T(8,128)(2,1)} %collective-permute-done.46), channel_id=1, source_target_pairs={{0,1},{1,0},{2,3},{3,2},{4,5},{5,4},{6,7},{7,6},{8,9},{9,8},{10,11... | collective-permute-start | bytes 3145736 | tf_op jit(solution)/shard_map/ppermute | solution.py:89
  422.3 89.5 %collective-permute-start.45 = (bf16[256,2048]{1,0:T(8,128)(2,1)S(1)}, bf16[256,2048]{1,0:T(8,128)(2,1)}, u32[]{:S(2)}, u32[]{:S(2)}) collective-permute-start(bf16[256,2048]{1,0:T(8,128)(2,1)S(1)} %convolution_convert_fusion.31), channel_id=1, source_target_pairs={{0,1},{1,0},{2,3},{3,2},{4,5},{5,4},{6,7},{7,6},{8,9},{9,8},{10,11... | collective-permute-start | bytes 3145736 | tf_op jit(solution)/shard_map/ppermute | solution.py:89
  432.6 88.2 %collective-permute-start.60 = (bf16[256,2048]{1,0:T(8,128)(2,1)}, bf16[256,2048]{1,0:T(8,128)(2,1)}, u32[]{:S(2)}, u32[]{:S(2)}) collective-permute-start(bf16[256,2048]{1,0:T(8,128)(2,1)} %convolution_convert_fusion.23), channel_id=1, source_target_pairs={{0,1},{1,0},{2,3},{3,2},{4,5},{5,4},{6,7},{7,6},{8,9},{9,8},{10,11... | collective-permute-start | bytes 3145736 | tf_op jit(solution)/shard_map/ppermute | solution.py:89
  509.7 93.5 %collective-permute-start.104 = (bf16[1024,2048]{1,0:T(8,128)(2,1)S(1)}, bf16[1024,2048]{1,0:T(8,128)(2,1)S(1)}, u32[]{:S(2)}, u32[]{:S(2)}) collective-permute-start(bf16[1024,2048]{1,0:T(8,128)(2,1)S(1)} %convolution_convert_fusion.1), channel_id=1, source_target_pairs={{16,0},{0,16},{17,1},{1,17},{18,2},{2,18},{19,3},{3,19},{20,4},{4,... | collective-permute-start | bytes 12582920 | tf_op jit(solution)/shard_map/ppermute | solution.py:137
  511.8 181.3 %collective-permute-start.103 = (bf16[2048,1024]{1,0:T(8,128)(2,1)S(1)}, bf16[2048,1024]{1,0:T(8,128)(2,1)S(1)}, u32[]{:S(2)}, u32[]{:S(2)}) collective-permute-start(bf16[2048,1024]{1,0:T(8,128)(2,1)S(1)} %convolution_convert_fusion.2), channel_id=1, source_target_pairs={{16,0},{0,16},{17,1},{1,17},{18,2},{2,18},{19,3},{3,19},{20,4},{4,... | collective-permute-start | bytes 12582920 | tf_op jit(solution)/shard_map/ppermute | solution.py:137
  542.2 240.3 %collective-permute-start.102 = (bf16[2048,1024]{1,0:T(8,128)(2,1)}, bf16[2048,1024]{1,0:T(8,128)(2,1)}, u32[]{:S(2)}, u32[]{:S(2)}) collective-permute-start(bf16[2048,1024]{1,0:T(8,128)(2,1)} %convolution_convert_fusion.3), channel_id=1, source_target_pairs={{16,0},{0,16},{17,1},{1,17},{18,2},{2,18},{19,3},{3,19},{20,4},{4,... | collective-permute-start | bytes 12582920 | tf_op jit(solution)/shard_map/ppermute | solution.py:137
  547.7 243.6 %collective-permute-start.35 = (bf16[256,2048]{1,0:T(8,128)(2,1)}, bf16[256,2048]{1,0:T(8,128)(2,1)}, u32[]{:S(2)}, u32[]{:S(2)}) collective-permute-start(bf16[256,2048]{1,0:T(8,128)(2,1)} %convolution_convert_fusion.35), channel_id=1, source_target_pairs={{0,1},{1,0},{2,3},{3,2},{4,5},{5,4},{6,7},{7,6},{8,9},{9,8},{10,11... | collective-permute-start | bytes 3145736 | tf_op jit(solution)/shard_map/ppermute | solution.py:89
  571.0 220.3 %collective-permute-start.58 = (bf16[256,2048]{1,0:T(8,128)(2,1)S(1)}, bf16[256,2048]{1,0:T(8,128)(2,1)}, u32[]{:S(2)}, u32[]{:S(2)}) collective-permute-start(bf16[256,2048]{1,0:T(8,128)(2,1)S(1)} %add_convert_fusion.13), channel_id=1, source_target_pairs={{0,4},{1,5},{2,0},{3,1},{4,8},{5,9},{6,2},{7,3},{8,12},{9,13},{10,... | collective-permute-start | bytes 3145736 | tf_op jit(solution)/shard_map/ppermute | solution.py:83
  603.2 188.2 %collective-permute-start.65 = (bf16[256,2048]{1,0:T(8,128)(2,1)S(1)}, bf16[256,2048]{1,0:T(8,128)(2,1)}, u32[]{:S(2)}, u32[]{:S(2)}) collective-permute-start(bf16[256,2048]{1,0:T(8,128)(2,1)S(1)} %add_convert_fusion.10), channel_id=1, source_target_pairs={{0,2},{1,3},{2,6},{3,7},{4,0},{5,1},{6,10},{7,11},{8,4},{9,5},{10,... | collective-permute-start | bytes 3145736 | tf_op jit(solution)/shard_map/ppermute | solution.py:86
  820.6 115.0 %collective-permute-start.70 = (bf16[256,2048]{1,0:T(8,128)(2,1)}, bf16[256,2048]{1,0:T(8,128)(2,1)}, u32[]{:S(2)}, u32[]{:S(2)}) collective-permute-start(bf16[256,2048]{1,0:T(8,128)(2,1)} %convolution_convert_fusion.11), channel_id=1, source_target_pairs={{0,1},{1,0},{2,3},{3,2},{4,5},{5,4},{6,7},{7,6},{8,9},{9,8},{10,11... | collective-permute-start | bytes 3145736 | tf_op jit(solution)/shard_map/ppermute | solution.py:89
  820.6 154.5 %collective-permute-start.69 = (bf16[256,2048]{1,0:T(8,128)(2,1)}, bf16[256,2048]{1,0:T(8,128)(2,1)}, u32[]{:S(2)}, u32[]{:S(2)}) collective-permute-start(bf16[256,2048]{1,0:T(8,128)(2,1)} %convolution_convert_fusion.13), channel_id=1, source_target_pairs={{0,1},{1,0},{2,3},{3,2},{4,5},{5,4},{6,7},{7,6},{8,9},{9,8},{10,11... | collective-permute-start | bytes 3145736 | tf_op jit(solution)/shard_map/ppermute | solution.py:89
  932.0 67.1 %collective-permute-start.83 = (bf16[256,2048]{1,0:T(8,128)(2,1)S(1)}, bf16[256,2048]{1,0:T(8,128)(2,1)S(1)}, u32[]{:S(2)}, u32[]{:S(2)}) collective-permute-start(bf16[256,2048]{1,0:T(8,128)(2,1)S(1)} %slice.850), channel_id=1, source_target_pairs={{0,16},{16,0},{1,17},{17,1},{2,18},{18,2},{3,19},{19,3},{4,20},{20... | collective-permute-start | bytes 3145736 | tf_op jit(solution)/shard_map/ppermute | solution.py:140
  935.7 73.5 %collective-permute-start.85 = (bf16[128,3072]{1,0:T(8,128)(2,1)}, bf16[128,3072]{1,0:T(8,128)(2,1)}, u32[]{:S(2)}, u32[]{:S(2)}) collective-permute-start(bf16[128,3072]{1,0:T(8,128)(2,1)} %get-tuple-element.64), channel_id=1, source_target_pairs={{0,1},{1,0},{2,3},{3,2},{4,5},{5,4},{6,7},{7,6},{8,9},{9,8},{10,11... | collective-permute-start | bytes 2359304 | tf_op jit(solution)/shard_map/ppermute | solution.py:89
  938.4 71.2 %collective-permute-start.95 = (bf16[128,3072]{1,0:T(8,128)(2,1)}, bf16[128,3072]{1,0:T(8,128)(2,1)}, u32[]{:S(2)}, u32[]{:S(2)}) collective-permute-start(bf16[128,3072]{1,0:T(8,128)(2,1)} %get-tuple-element.58), channel_id=1, source_target_pairs={{0,1},{1,0},{2,3},{3,2},{4,5},{5,4},{6,7},{7,6},{8,9},{9,8},{10,11... | collective-permute-start | bytes 2359304 | tf_op jit(solution)/shard_map/ppermute | solution.py:89
  975.2 43.8 %collective-permute-start.91 = (bf16[128,3072]{1,0:T(8,128)(2,1)}, bf16[128,3072]{1,0:T(8,128)(2,1)}, u32[]{:S(2)}, u32[]{:S(2)}) collective-permute-start(bf16[128,3072]{1,0:T(8,128)(2,1)} %add_convert_fusion.24), channel_id=1, source_target_pairs={{0,4},{1,5},{2,0},{3,1},{4,8},{5,9},{6,2},{7,3},{8,12},{9,13},{10,... | collective-permute-start | bytes 2359304 | tf_op jit(solution)/shard_map/ppermute | solution.py:83
  1005.5 41.1 %all-to-all-start.1 = ((f32[16,1,272]{2,1,0:T(1,128)}), f32[16,1,272]{2,1,0:T(1,128)S(1)}, u32[]{:S(2)}, u32[]{:S(2)}) async-start(f32[16,1,272]{2,1,0:T(1,128)} %all_to_all.17), calls=%async_computation.2 | async-start | bytes 49152 | tf_op jit(solution)/shard_map/all_to_all | solution.py:376
  1009.1 174.5 %all-reduce.8.cloned.1.call-start = ((), (), s32[]{:S(2)}) async-start(), calls=%async_computation.5 | async-start | bytes 1048576 | tf_op jit(solution)/shard_map/psum | solution.py:364
  1009.2 37.4 %collective-permute-start.68 = (bf16[256,2048]{1,0:T(8,128)(2,1)}, bf16[256,2048]{1,0:T(8,128)(2,1)}, u32[]{:S(2)}, u32[]{:S(2)}) collective-permute-start(bf16[256,2048]{1,0:T(8,128)(2,1)} %convolution_convert_fusion.15), channel_id=1, source_target_pairs={{0,1},{1,0},{2,3},{3,2},{4,5},{5,4},{6,7},{7,6},{8,9},{9,8},{10,11... | collective-permute-start | bytes 3145736 | tf_op jit(solution)/shard_map/ppermute | solution.py:89
  1009.6 77.6 %collective-permute-start.67 = (bf16[256,2048]{1,0:T(8,128)(2,1)}, bf16[256,2048]{1,0:T(8,128)(2,1)}, u32[]{:S(2)}, u32[]{:S(2)}) collective-permute-start(bf16[256,2048]{1,0:T(8,128)(2,1)} %convolution_convert_fusion.17), channel_id=1, source_target_pairs={{0,1},{1,0},{2,3},{3,2},{4,5},{5,4},{6,7},{7,6},{8,9},{9,8},{10,11... | collective-permute-start | bytes 3145736 | tf_op jit(solution)/shard_map/ppermute | solution.py:89
  1018.9 39.4 %collective-permute-start.72 = (bf16[256,2048]{1,0:T(8,128)(2,1)}, bf16[256,2048]{1,0:T(8,128)(2,1)}, u32[]{:S(2)}, u32[]{:S(2)}) collective-permute-start(bf16[256,2048]{1,0:T(8,128)(2,1)} %add_convert_fusion.8), channel_id=1, source_target_pairs={{0,4},{1,5},{2,0},{3,1},{4,8},{5,9},{6,2},{7,3},{8,12},{9,13},{10,... | collective-permute-start | bytes 3145736 | tf_op jit(solution)/shard_map/ppermute | solution.py:83
  1023.0 40.4 %collective-permute-start.94 = (bf16[128,3072]{1,0:T(8,128)(2,1)}, bf16[128,3072]{1,0:T(8,128)(2,1)}, u32[]{:S(2)}, u32[]{:S(2)}) collective-permute-start(bf16[128,3072]{1,0:T(8,128)(2,1)} %get-tuple-element.59), channel_id=1, source_target_pairs={{0,1},{1,0},{2,3},{3,2},{4,5},{5,4},{6,7},{7,6},{8,9},{9,8},{10,11... | collective-permute-start | bytes 2359304 | tf_op jit(solution)/shard_map/ppermute | solution.py:89
  1063.4 45.5 %collective-permute-start.75 = (bf16[256,2048]{1,0:T(8,128)(2,1)S(1)}, bf16[256,2048]{1,0:T(8,128)(2,1)S(1)}, u32[]{:S(2)}, u32[]{:S(2)}) collective-permute-start(bf16[256,2048]{1,0:T(8,128)(2,1)S(1)} %copy-done.55), channel_id=1, source_target_pairs={{0,1},{1,0},{2,3},{3,2},{4,5},{5,4},{6,7},{7,6},{8,9},{9,8},{10,11... | collective-permute-start | bytes 3145736 | tf_op jit(solution)/shard_map/ppermute | solution.py:89
  1087.2 62.9 %collective-permute-start.66 = (bf16[256,2048]{1,0:T(8,128)(2,1)}, bf16[256,2048]{1,0:T(8,128)(2,1)}, u32[]{:S(2)}, u32[]{:S(2)}) collective-permute-start(bf16[256,2048]{1,0:T(8,128)(2,1)} %convolution_convert_fusion.19), channel_id=1, source_target_pairs={{0,1},{1,0},{2,3},{3,2},{4,5},{5,4},{6,7},{7,6},{8,9},{9,8},{10,11... | collective-permute-start | bytes 3145736 | tf_op jit(solution)/shard_map/ppermute | solution.py:89
  1089.1 37.0 %collective-permute-start.80 = (bf16[256,2048]{1,0:T(8,128)(2,1)S(1)}, bf16[256,2048]{1,0:T(8,128)(2,1)S(1)}, u32[]{:S(2)}, u32[]{:S(2)}) collective-permute-start(bf16[256,2048]{1,0:T(8,128)(2,1)S(1)} %add_convert_fusion.4), channel_id=1, source_target_pairs={{0,2},{1,3},{2,6},{3,7},{4,0},{5,1},{6,10},{7,11},{8,4},{9,5},{10,... | collective-permute-start | bytes 3145736 | tf_op jit(solution)/shard_map/ppermute | solution.py:86
  1092.4 36.7 %collective-permute-start.84 = (bf16[128,3072]{1,0:T(8,128)(2,1)S(1)}, bf16[128,3072]{1,0:T(8,128)(2,1)S(1)}, u32[]{:S(2)}, u32[]{:S(2)}) collective-permute-start(bf16[128,3072]{1,0:T(8,128)(2,1)S(1)} %get-tuple-element.57), channel_id=1, source_target_pairs={{0,1},{1,0},{2,3},{3,2},{4,5},{5,4},{6,7},{7,6},{8,9},{9,8},{10,11... | collective-permute-start | bytes 2359304 | tf_op jit(solution)/shard_map/ppermute | solution.py:89
  1129.5 36.9 %collective-permute-start.81 = (bf16[256,2048]{1,0:T(8,128)(2,1)}, bf16[256,2048]{1,0:T(8,128)(2,1)}, u32[]{:S(2)}, u32[]{:S(2)}) collective-permute-start(bf16[256,2048]{1,0:T(8,128)(2,1)} %add_convert_fusion.3), channel_id=1, source_target_pairs={{0,2},{1,3},{2,6},{3,7},{4,0},{5,1},{6,10},{7,11},{8,4},{9,5},{10,... | collective-permute-start | bytes 3145736 | tf_op jit(solution)/shard_map/ppermute | solution.py:86
  (192 other events, 5040.8 us)
Sparse Core Ops, SparseCore 0:
  26.7 104.7 all-gather.1
  914.0 143.7 reduce-scatter.1
  1150.2 31.5 all-reduce.7

commit v2 on v1

--- a/solution.py
+++ b/solution.py
@@ -1,7 +1,11 @@
+import functools
+
 import jax
 import jax.numpy as jnp
 import numpy as np
 from jax import lax
+from jax.experimental import pallas as pl
+from jax.experimental.pallas import tpu as pltpu
 from jax.sharding import PartitionSpec as P
 
 D = 2048
@@ -118,6 +122,549 @@
         return joined(0) + up.astype(F32) + down.astype(F32)
 
 
+MESH = pl.DeviceIdType.MESH
+DMA = pltpu.SemaphoreType.DMA
+VMEM_LIMIT = 60 << 20
+
+
+class Hops:
+    def __init__(self, chips):
+        self.chips, self.half = chips, chips // 2
+        self.outer = 4 if chips % 4 == 0 else 2
+        self.inner = chips // self.outer
+        self.me = lax.axis_index("grp")
+        chip, self.core = self.me // 2, self.me % 2
+        a, b = chip // self.inner, chip % self.inner
+        row = self.outer - 1 - a
+        along = jnp.where(row % 2 == 0, b - 1, self.inner - 1 - b)
+        self.place = jnp.where(b == 0, a, self.outer + row * (self.inner - 1) + along)
+        self.ahead, self.back = self.device(1), self.device(-1)
+        self.flip = self.me + 1 - 2 * self.core
+        self.started = []
+
+    def chip(self, d):
+        p = (self.place + (d % self.chips)) % self.chips
+        q = jnp.maximum(p - self.outer, 0)
+        k, m = q // (self.inner - 1), q % (self.inner - 1)
+        b = jnp.where(k % 2 == 0, m + 1, self.inner - 1 - m)
+        return jnp.where(
+            p < self.outer, p * self.inner, (self.outer - 1 - k) * self.inner + b
+        )
+
+    def device(self, d):
+        return 2 * self.chip(d) + self.core
+
+    def meet(self):
+        barrier = pltpu.get_barrier_semaphore()
+        for dev in (self.ahead, self.back, self.flip):
+            pl.semaphore_signal(barrier, inc=1, device_id={"grp": dev}, device_id_type=MESH)
+        pl.semaphore_wait(barrier, 3)
+
+    def copy(self, src, dst, send_sem, recv_sem, dev):
+        return pltpu.make_async_remote_copy(
+            src_ref=src,
+            dst_ref=dst,
+            send_sem=send_sem,
+            recv_sem=recv_sem,
+            device_id={"grp": dev},
+            device_id_type=MESH,
+        )
+
+    def send(self, src, dst, sems, at, dev):
+        c = self.copy(src, dst, sems.at[0, at], sems.at[1, at], dev)
+        c.start()
+        self.started.append(c)
+
+    def wait(self, dst, sems, at):
+        self.copy(dst, dst, sems.at[0, at], sems.at[1, at], self.flip).wait_recv()
+
+    def drain(self):
+        for c in self.started:
+            c.wait_send()
+
+    def gather(self, own, slot, up, down, side, use):
+        half, rows = self.half, own.shape[0]
+        cut = rows // 2
+        self.send(own, slot(self.me), up, 0, self.ahead)
+        self.send(own, slot(self.me), down, 0, self.back)
+        self.send(own, slot(self.me), side, 0, self.flip)
+
+        def ready(d):
+            dev = self.device(d)
+            self.wait(slot(dev + 1 - 2 * self.core), side, d % self.chips)
+            use(d)
+
+        for s in range(1, half):
+            last = s == half - 1
+            a, b = slot(self.device(-s)), slot(self.device(s))
+            self.wait(a, up, s - 1)
+            part = a.at[pl.ds(0, cut)] if last else a
+            self.send(part, part, up, s, self.ahead)
+            self.send(a, a, side, -s % self.chips, self.flip)
+            self.wait(b, down, s - 1)
+            part = b.at[pl.ds(cut, rows - cut)] if last else b
+            self.send(part, part, down, s, self.back)
+            self.send(b, b, side, s, self.flip)
+            for d in sorted({1 - s, s - 1}):
+                ready(d)
+        far = slot(self.device(half))
+        self.wait(far.at[pl.ds(0, cut)], up, half - 1)
+        self.wait(far.at[pl.ds(cut, rows - cut)], down, half - 1)
+        self.send(far, far, side, half, self.flip)
+        for d in sorted({1 - half, half - 1}):
+            ready(d)
+        ready(half)
+        self.drain()
+
+
+    def scatter(self, rows, produce, mine, out, came, far, up_in, down_in, up, down, side, finish):
+        half, chips = self.half, self.chips
+        cut = rows // 2
+        strip = 16
+        made = {}
+
+        def make(d):
+            made[d] = len(made) % mine.shape[0]
+            produce(d, mine.at[made[d]], out.at[d % chips])
+            self.send(out.at[d % chips], came.at[d % chips], side, d % chips, self.flip)
+
+        def joined(d, at):
+            return mine[made[d], at, :] + came[d % chips, at, :].astype(F32)
+
+        def strips(first, last, body):
+            def step(i, carry):
+                body(pl.ds(pl.multiple_of(first + i * strip, strip), strip))
+                return carry
+
+            lax.fori_loop(0, (last - first) // strip, step, 0)
+
+        for d in (half, half - 1, 1 - half):
+            make(d)
+        self.wait(came.at[half], side, half)
+
+        def far_sum(at):
+            far[at, :] = joined(half, at).astype(BF)
+
+        strips(0, rows, far_sum)
+        low, high = pl.ds(0, cut), pl.ds(cut, rows - cut)
+        self.send(far.at[low], up_in.at[0, low], up, 0, self.ahead)
+        self.send(far.at[high], down_in.at[0, high], down, 0, self.back)
+        for s in range(half - 1, 0, -1):
+            i = half - s
+            for d in sorted({s - 1, 1 - s}):
+                make(d)
+            for d, buf, sems, target in (
+                (s, up_in, up, self.ahead),
+                (-s, down_in, down, self.back),
+            ):
+                self.wait(came.at[d % chips], side, d % chips)
+
+                def fresh(at, d=d, buf=buf, i=i):
+                    buf[i - 1, at, :] = joined(d, at).astype(BF)
+
+                def onto(at, d=d, buf=buf, i=i):
+                    buf[i - 1, at, :] = (joined(d, at) + buf[i - 1, at, :].astype(F32)).astype(BF)
+
+                if i > 1:
+                    self.wait(buf.at[i - 1], sems, i - 1)
+                    strips(0, rows, onto)
+                elif d > 0:
+                    self.wait(buf.at[0, low], sems, 0)
+                    strips(0, cut, onto)
+                    strips(cut, rows, fresh)
+                else:
+                    self.wait(buf.at[0, high], sems, 0)
+                    strips(0, cut, fresh)
+                    strips(cut, rows, onto)
+                self.send(buf.at[i - 1], buf.at[i], sems, i, target)
+        self.wait(came.at[0], side, 0)
+        self.wait(up_in.at[half - 1], up, half - 1)
+        self.wait(down_in.at[half - 1], down, half - 1)
+
+        def total(at):
+            finish(
+                joined(0, at)
+                + up_in[half - 1, at, :].astype(F32)
+                + down_in[half - 1, at, :].astype(F32),
+                at,
+            )
+
+        strips(0, rows, total)
+        self.drain()
+
+
+def scatter_scratch(chips, rows, width):
+    half = chips // 2
+    return [
+        pltpu.VMEM((4, rows, width), F32),
+        pltpu.VMEM((chips, rows, width), BF),
+        pltpu.VMEM((chips, rows, width), BF),
+        pltpu.VMEM((rows, width), BF),
+        pltpu.VMEM((half, rows, width), BF),
+        pltpu.VMEM((half, rows, width), BF),
+    ]
+
+
+def dot_nt(a, b):
+    return lax.dot_general(a, b, (((1,), (1,)), ((), ())), preferred_element_type=F32)
+
+
+def tiles(count, width, body):
+    def step(i, carry):
+        body(pl.ds(pl.multiple_of(i * width, width), width))
+        return carry
+
+    lax.fori_loop(0, count, step, 0)
+
+
+def experts_kernel(
+    chips, cap,
+    h2_ref, dy_ref, slot_ref, weight_ref, wg_hbm, wu_hbm, wd_hbm,
+    xs_ref, de_ref, act_ref, dg_ref, du_ref,
+    held, dy, wg, wu, wd, xs_b, de_b, act_b, dg_b, du_b,
+    up, down, side, w_sem, dy_sem, own_sem, out_sem,
+):
+    hops = Hops(chips)
+    half = chips // 2
+    tok, width = h2_ref.shape
+    ff = wg.shape[1]
+    order = [0]
+    for s in range(1, half):
+        order += [-s, s]
+    order += [half]
+    number = {d: i for i, d in enumerate(order)}
+
+    loads = [
+        pltpu.make_async_copy(a, b, w_sem.at[i])
+        for i, (a, b) in enumerate(((wg_hbm, wg), (wu_hbm, wu), (wd_hbm, wd)))
+    ]
+
+    def dy_copy(i):
+        chip = hops.chip(order[i])
+        return pltpu.make_async_copy(dy_ref.at[pl.ds(2 * chip, 2)], dy.at[i % 2], dy_sem.at[i % 2])
+
+    def out_copies(i):
+        chip = hops.chip(order[i])
+        pairs = ((xs_b, xs_ref), (de_b, de_ref), (act_b, act_ref), (dg_b, dg_ref), (du_b, du_ref))
+        return [
+            pltpu.make_async_copy(b.at[i % 2], r.at[chip], out_sem.at[i % 2, j])
+            for j, (b, r) in enumerate(pairs)
+        ]
+
+    hops.meet()
+    own = pltpu.make_async_copy(h2_ref, held.at[hops.me], own_sem)
+    own.start()
+
+    def use(d):
+        i = number[d]
+        p = i % 2
+        if i == 0:
+            own.wait()
+            for c in loads:
+                c.start()
+            dy_copy(0).start()
+            for c in loads:
+                c.wait()
+        dy_copy(i).wait()
+        if i + 1 < chips:
+            dy_copy(i + 1).start()
+        if i >= 2:
+            for c in out_copies(i - 2):
+                c.wait()
+        chip = hops.chip(d)
+        for k in range(2):
+            dev = 2 * chip + k
+            hit = slot_ref[pl.ds(dev, 1), :] == lax.broadcasted_iota(jnp.int32, (cap, tok), 0)
+            pick = hit.astype(F32).astype(BF)
+            scale = jnp.sum(
+                jnp.where(hit, weight_ref[pl.ds(dev, 1), :], 0.0), axis=1, keepdims=True
+            )
+            rows = pl.ds(k * cap, cap)
+
+            def choose(at, k=k, dev=dev, pick=pick, scale=scale, rows=rows):
+                xs_b[p, rows, at] = dot32(pick, held[dev, :, at]).astype(BF)
+                de_b[p, rows, at] = (scale * dot32(pick, dy[p, k, :, at])).astype(BF)
+
+            tiles(width // 512, 512, choose)
+
+        def hidden(at):
+            gpre = dot32(xs_b[p], wg[:, at])
+            upre = dot32(xs_b[p], wu[:, at])
+            dact = dot_nt(de_b[p], wd[at, :])
+            sig = 1.0 / (1.0 + jnp.exp(-gpre))
+            act_b[p, :, at] = (gpre * sig * upre).astype(BF)
+            dg_b[p, :, at] = (dact * upre * sig * (1.0 + gpre * (1.0 - sig))).astype(BF)
+            du_b[p, :, at] = (dact * gpre * sig).astype(BF)
+
+        tiles(ff // 256, 256, hidden)
+        for c in out_copies(i):
+            c.start()
+
+    hops.gather(h2_ref, lambda dev: held.at[dev], up, down, side, use)
+    for i in (chips - 2, chips - 1):
+        for c in out_copies(i):
+            c.wait()
+
+
+def expert_rows(chips, cap, h2, dy_all, slot, weight, wg, wu, wd, collective_id):
+    tok, width = h2.shape
+    ff = wg.shape[1]
+    anywhere = pl.BlockSpec(memory_space=pl.ANY)
+    vmem = pl.BlockSpec(memory_space=pltpu.VMEM)
+    wide = jax.ShapeDtypeStruct((chips, 2 * cap, width), BF)
+    thin = jax.ShapeDtypeStruct((chips, 2 * cap, ff), BF)
+    return pl.pallas_call(
+        functools.partial(experts_kernel, chips, cap),
+        out_shape=(wide, wide, thin, thin, thin),
+        in_specs=[anywhere, anywhere, vmem, vmem, anywhere, anywhere, anywhere],
+        out_specs=(anywhere,) * 5,
+        scratch_shapes=[
+            pltpu.VMEM((2 * chips, tok, width), BF),
+            pltpu.VMEM((2, 2, tok, width), BF),
+            pltpu.VMEM((width, ff), BF),
+            pltpu.VMEM((width, ff), BF),
+            pltpu.VMEM((ff, width), BF),
+            pltpu.VMEM((2, 2 * cap, width), BF),
+            pltpu.VMEM((2, 2 * cap, width), BF),
+            pltpu.VMEM((2, 2 * cap, ff), BF),
+            pltpu.VMEM((2, 2 * cap, ff), BF),
+            pltpu.VMEM((2, 2 * cap, ff), BF),
+            *ring_sems(chips),
+            DMA((3,)),
+            DMA((2,)),
+            DMA,
+            DMA((2, 5)),
+        ],
+        compiler_params=pltpu.CompilerParams(
+            collective_id=collective_id, has_side_effects=True, vmem_limit_bytes=VMEM_LIMIT
+        ),
+        cost_estimate=pl.CostEstimate(
+            flops=2 * chips * cap * width * ff * 6, transcendentals=0, bytes_accessed=200 << 20
+        ),
+        name="experts",
+    )(h2, dy_all, slot, weight, wg, wu, wd)
+
+
+def rows_back_kernel(
+    chips, cap,
+    dg_ref, du_ref, slot_ref, wg_hbm, wu_hbm, total_ref,
+    wg, wu, dg, du, drow, mine, out, came, far, up_in, down_in,
+    up, down, side, w_sem, in_sem,
+):
+    hops = Hops(chips)
+    half = chips // 2
+    tok, width = total_ref.shape
+    order = [half]
+    for s in range(half - 1, 0, -1):
+        order += [s, -s] if s == half - 1 else [-s, s]
+    order += [0]
+    number = {d: i for i, d in enumerate(order)}
+    loads = [
+        pltpu.make_async_copy(a, b, w_sem.at[i])
+        for i, (a, b) in enumerate(((wg_hbm, wg), (wu_hbm, wu)))
+    ]
+
+    def in_copies(i):
+        chip = hops.chip(order[i])
+        return [
+            pltpu.make_async_copy(r.at[chip], b.at[i % 2], in_sem.at[i % 2, j])
+            for j, (r, b) in enumerate(((dg_ref, dg), (du_ref, du)))
+        ]
+
+    for c in loads + in_copies(0):
+        c.start()
+    hops.meet()
+    for c in loads:
+        c.wait()
+
+    def produce(d, same_ref, other_ref):
+        i = number[d]
+        p = i % 2
+        for c in in_copies(i):
+            c.wait()
+        if i + 1 < chips:
+            for c in in_copies(i + 1):
+                c.start()
+
+        def back(at):
+            drow[:, at] = (dot_nt(dg[p], wg[at, :]) + dot_nt(du[p], wu[at, :])).astype(BF)
+
+        tiles(width // 256, 256, back)
+        chip = hops.chip(d)
+        lanes = lax.broadcasted_iota(jnp.int32, (tok, cap), 1)
+
+        def pick(k):
+            return (slot_ref[2 * chip + k] == lanes).astype(F32).astype(BF)
+
+        same, other = hops.core, 1 - hops.core
+        same_pick, other_pick = pick(same), pick(other)
+        same_rows = pl.ds(pl.multiple_of(same * cap, 16), cap)
+        other_rows = pl.ds(pl.multiple_of(other * cap, 16), cap)
+
+        def spread(at):
+            same_ref[:, at] = dot32(same_pick, drow[same_rows, at])
+            other_ref[:, at] = dot32(other_pick, drow[other_rows, at]).astype(BF)
+
+        tiles(width // 512, 512, spread)
+
+    def finish(value, at):
+        total_ref[at, :] = value
+
+    hops.scatter(
+        tok, produce, mine, out, came, far, up_in, down_in, up, down, side, finish
+    )
+
+
+def rows_back(chips, cap, dg, du, slot, wg, wu, collective_id):
+    tok = slot.shape[1]
+    width, ff = wg.shape
+    anywhere = pl.BlockSpec(memory_space=pl.ANY)
+    vmem = pl.BlockSpec(memory_space=pltpu.VMEM)
+    return pl.pallas_call(
+        functools.partial(rows_back_kernel, chips, cap),
+        out_shape=jax.ShapeDtypeStruct((tok, width), F32),
+        in_specs=[anywhere, anywhere, vmem, anywhere, anywhere],
+        out_specs=vmem,
+        scratch_shapes=[
+            pltpu.VMEM((width, ff), BF),
+            pltpu.VMEM((width, ff), BF),
+            pltpu.VMEM((2, 2 * cap, ff), BF),
+            pltpu.VMEM((2, 2 * cap, ff), BF),
+            pltpu.VMEM((2 * cap, width), BF),
+            *scatter_scratch(chips, tok, width),
+            *ring_sems(chips),
+            DMA((2,)),
+            DMA((2, 2)),
+        ],
+        compiler_params=pltpu.CompilerParams(
+            collective_id=collective_id, has_side_effects=True, vmem_limit_bytes=VMEM_LIMIT
+        ),
+        cost_estimate=pl.CostEstimate(
+            flops=2 * chips * cap * width * ff * 6, transcendentals=0, bytes_accessed=200 << 20
+        ),
+        name="rows_back",
+    )(dg, du, slot, wg, wu)
+
+
+def qkv_gradient_kernel(
+    chips, h1_ref, grad_ref, total_ref, mine, out, came, far, up_in, down_in, up, down, side
+):
+    hops = Hops(chips)
+    shard, width = total_ref.shape
+    hops.meet()
+
+    def produce(d, same_ref, other_ref):
+        first = 2 * hops.chip(d) * shard
+        rows = pl.ds(pl.multiple_of(first, 2 * shard), 2 * shard)
+
+        def block(at):
+            value = dot32(h1_ref[rows, :], grad_ref[:, at])
+            same_ref[:, at] = value[:shard]
+            other_ref[:, at] = value[shard:].astype(BF)
+
+        tiles(width // 512, 512, block)
+
+    def finish(value, at):
+        total_ref[at, :] = value.astype(BF)
+
+    hops.scatter(
+        shard, produce, mine, out, came, far, up_in, down_in, up, down, side, finish
+    )
+
+
+def qkv_gradient(chips, h1_t, grad, collective_id):
+    shard = h1_t.shape[0] // (2 * chips)
+    width = grad.shape[1]
+    vmem = pl.BlockSpec(memory_space=pltpu.VMEM)
+    return pl.pallas_call(
+        functools.partial(qkv_gradient_kernel, chips),
+        out_shape=jax.ShapeDtypeStruct((shard, width), BF),
+        in_specs=[vmem, vmem],
+        out_specs=vmem,
+        scratch_shapes=[*scatter_scratch(chips, shard, width), *ring_sems(chips)],
+        compiler_params=pltpu.CompilerParams(
+            collective_id=collective_id, has_side_effects=True, vmem_limit_bytes=VMEM_LIMIT
+        ),
+        cost_estimate=pl.CostEstimate(
+            flops=2 * h1_t.size * width, transcendentals=0, bytes_accessed=200 << 20
+        ),
+        name="qkv_gradient",
+    )(h1_t, grad)
+
+
+def gather_kernel(chips, own_ref, all_ref, up, down, side, local):
+    hops = Hops(chips)
+    hops.meet()
+    mine = pltpu.make_async_copy(own_ref, all_ref.at[hops.me], local)
+    mine.start()
+    hops.gather(own_ref, lambda dev: all_ref.at[dev], up, down, side, lambda d: None)
+    mine.wait()
+
+
+def ring_sems(chips):
+    return [DMA((2, chips // 2)), DMA((2, chips // 2)), DMA((2, chips))]
+
+
+def ring_gather(chips, own, collective_id, name):
+    anywhere = pl.BlockSpec(memory_space=pl.ANY)
+    return pl.pallas_call(
+        functools.partial(gather_kernel, chips),
+        out_shape=jax.ShapeDtypeStruct((2 * chips, *own.shape), own.dtype),
+        in_specs=[anywhere],
+        out_specs=anywhere,
+        scratch_shapes=[*ring_sems(chips), DMA],
+        compiler_params=pltpu.CompilerParams(collective_id=collective_id, has_side_effects=True),
+        cost_estimate=pl.CostEstimate(
+            flops=0, transcendentals=0, bytes_accessed=4 * chips * own.size * own.dtype.itemsize
+        ),
+        name=name,
+    )(own)
+
+
+def out_gradient(ring, grad, reps, heads, rel, rep, grp):
+    if reps != 2 or heads != ring.chips:
+        whole = lax.dynamic_update_slice(
+            jnp.zeros((heads, reps, HD, D), BF), grad.reshape(heads, 1, HD, D), (0, rep, 0, 0)
+        ).reshape(D, D)
+        part = lax.psum_scatter(whole, "grp", scatter_dimension=0, tiled=True)
+        return lax.psum(part, "rep").astype(F32)
+    n = ring.devices
+    owners = [(r, 2 * chip + r) for r in range(2) for chip in range(ring.chips)]
+
+    def send(v, where):
+        pairs = []
+        for r, dev in owners:
+            src, dst = where(r, dev)
+            pairs.append((src[0] * n + src[1], dst[0] * n + dst[1]))
+        return lax.ppermute(v, ("rep", "grp"), pairs)
+
+    def hop(v, shift):
+        def to(r, dev):
+            chip = ring.cycle[(ring.place[dev // 2] + shift) % ring.chips]
+            return (r, dev), (r, 2 * chip + r)
+
+        return send(v, to)
+
+    other = send(grad, lambda r, dev: ((r, dev ^ 1), (r, dev)))
+    both = (grad.astype(F32) + other.astype(F32)).reshape(heads, HD, D)
+
+    def block(d):
+        return lax.dynamic_index_in_dim(both, rel[d, 0] // 2, 0, False)
+
+    far = block(ring.half).astype(BF)
+    rows = HD // 2
+    up, down = hop(far[:rows], 1), hop(far[rows:], -1)
+    zero = jnp.zeros_like(up)
+    up = jnp.concatenate([up, zero], axis=0)
+    down = jnp.concatenate([zero, down], axis=0)
+    for step in range(ring.half - 1, 0, -1):
+        up = hop((block(step) + up.astype(F32)).astype(BF), 1)
+        down = hop((block(-step % ring.chips) + down.astype(F32)).astype(BF), -1)
+    total = (block(0) + up.astype(F32) + down.astype(F32)).astype(BF)
+    mine = send(total, lambda r, dev: ((r, dev), (1 - r, dev)))
+    return jnp.where(grp % 2 == rep, total, mine).astype(F32)
+
+
 def per_device(
     tokens, w_qkv, w_out, gains, w_gate, w_up, w_down, segment_ids, routes, gate_weights, cotangent
 ):
@@ -126,7 +673,6 @@
     ring = Ring(groups)
     rep, grp = lax.axis_index("rep"), lax.axis_index("grp")
     rel = jnp.asarray(ring.table())[grp]
-    rel_flat = rel.reshape(-1)
     tok_rows = tokens.shape[1]
     seq_len = segment_ids.shape[1]
     heads = HEADS // reps
@@ -165,7 +711,7 @@
     )
     small = lax.all_to_all(small, "grp", split_axis=0, concat_axis=0, tiled=True)
     gains_f = small[:, tok_rows:].reshape(-1)
-    weight_in = small[:, :tok_rows][rel_flat]
+    weight_in = small[:, :tok_rows]
     g_attn = gains_f[:D]
     g_ffn = gains_f[D : 2 * D]
     g_query = gains_f[2 * D : 2 * D + HD]
@@ -175,14 +721,14 @@
         w_qkv.reshape(w_qkv.shape[0], 3, heads, reps, HD), rep, axis=3, keepdims=False
     ).reshape(w_qkv.shape[0], 3 * wide)
     shard = my_qkv.shape[0]
-    full_qkv = jnp.zeros((D, 3 * wide), BF)
-    for d, pair in ring.gather(my_qkv).items():
-        for k in range(2):
-            full_qkv = lax.dynamic_update_slice(full_qkv, pair[k], (rel[d, k] * shard, 0))
+    full_qkv = ring_gather(ring.chips, my_qkv, 1, "gather_qkv").reshape(D, 3 * wide)
     full_out = lax.all_gather(w_out, "grp", axis=0, tiled=True)
     my_out = lax.dynamic_index_in_dim(
         full_out.reshape(heads, reps, HD, D), rep, axis=1, keepdims=False
     ).reshape(wide, D)
+
+    cot_late, full_qkv = lax.optimization_barrier((cotangent[0], full_qkv))
+    dy_all = lax.all_gather(cot_late, "grp", axis=0, tiled=False)
 
     seq_f = seq_b.astype(F32)
     normed_one, hat_one, inv_one = rms_forward(seq_f, g_attn)
@@ -217,94 +763,57 @@
     normed_two, hat_two, inv_two = rms_forward(mid_rows, g_ffn)
     h2_b = normed_two.astype(BF)
 
+    chips = ring.chips
     entries = tok_rows * TOP
     capacity = min(tok_rows, (9 * entries + 8 * groups - 1) // (8 * groups))
+    capacity = -(-capacity // 16) * 16
     named = weight_in > 0
     before = dot32(
         named.astype(BF), jnp.tri(tok_rows, dtype=BF).T
     )
     slot = jnp.where(named, before - 1.0, -1.0).astype(jnp.int32)
+    rows_in, grads_in, acts, grad_gates, grad_ups = expert_rows(
+        chips, capacity, h2_b, dy_all, slot, weight_in, w_gate[0], w_up[0], w_down[0], 2
+    )
+    cuts = 1 if chips <= 8 else chips // 8
+    grad_h2 = jnp.concatenate(
+        [
+            rows_back(chips, capacity, grad_gates, grad_ups, slot[:, :, None], wg, wu, 8 + i)
+            for i, (wg, wu) in enumerate(
+                zip(jnp.split(w_gate[0], cuts), jnp.split(w_up[0], cuts), strict=True)
+            )
+        ],
+        axis=1,
+    )
+
     pick = (slot[:, None, :] == jnp.arange(capacity, dtype=jnp.int32)[None, :, None]).astype(BF)
     row_weight = jnp.sum(pick.astype(F32) * weight_in[:, None, :], axis=-1)
-
-    chips, half = ring.chips, ring.half
-    batches = [(0,)] + [(d, chips - d) for d in range(1, half)] + [(half,)]
-
-    def select(blocks, batch):
-        return jnp.concatenate(
-            [dot32(pick[2 * d + k], blocks[d][k]).astype(BF) for d in batch for k in range(2)], axis=0
-        )
-
-    def spread(rows, batch):
-        out, at = {}, 0
-        for d in batch:
-            pair = []
-            for k in range(2):
-                part = rows[at : at + capacity]
-                pair.append(
-                    lax.dot_general(
-                        pick[2 * d + k], part, (((0,), (0,)), ((), ())), preferred_element_type=F32
-                    ).astype(BF)
-                )
-                at += capacity
-            out[d] = tuple(pair)
+    all_rows = rows_in.reshape(-1, D)
+    all_grads = grads_in.reshape(-1, D)
+    all_acts = acts.reshape(groups * capacity, -1)
+    all_gates = grad_gates.reshape(groups * capacity, -1)
+    all_ups = grad_ups.reshape(groups * capacity, -1)
+    eout = dot32(all_acts, w_down[0]).astype(BF).astype(F32)
+    eout = (row_weight.reshape(-1, 1) * eout).astype(BF).reshape(groups, capacity, D)
+    out_all = jnp.einsum("gct,gcd->gtd", pick, eout, preferred_element_type=F32).astype(BF)
+    out_sum = lax.psum_scatter(
+        out_all.reshape(groups * tok_rows, D), "grp", scatter_dimension=0, tiled=True
+    )
+
+    def rep_send(v):
+        v = v.astype(BF)
+        return [v] + [from_rep(v, k) for k in range(1, reps)]
+
+    def rep_sum(parts, after):
+        parts, _ = lax.optimization_barrier((parts, after))
+        out = parts[0].astype(F32)
+        for part in parts[1:]:
+            out = out + part.astype(F32)
         return out
 
-    def weights_of(batch):
-        return jnp.concatenate([row_weight[2 * d + k] for d in batch for k in range(2)])[:, None]
-
-    dy_blocks = ring.gather(cotangent[0])
-    h2_blocks = ring.gather(h2_b)
-    acts, upres, gpres, rows_in, grads_in, grad_acts = [], [], [], [], [], []
-    for batch in batches:
-        picked = select(h2_blocks, batch)
-        grads = (weights_of(batch) * select(dy_blocks, batch).astype(F32)).astype(BF)
-        rows_in.append(picked)
-        grads_in.append(grads)
-        gpres.append(dot32(picked, w_gate[0]))
-        upres.append(dot32(picked, w_up[0]))
-        acts.append((jax.nn.silu(gpres[-1]) * upres[-1]).astype(BF))
-        grad_acts.append(
-            jnp.einsum("rd,fd->rf", grads, w_down[0], preferred_element_type=F32)
-        )
-    grad_gates, grad_ups = [], []
-    back_blocks = {}
-    for i in reversed(range(len(batches))):
-        sig = jax.nn.sigmoid(gpres[i])
-        grad_gates.insert(
-            0, (grad_acts[i] * upres[i] * sig * (1.0 + gpres[i] * (1.0 - sig))).astype(BF)
-        )
-        grad_ups.insert(0, (grad_acts[i] * gpres[i] * sig).astype(BF))
-        drow = (
-            jnp.einsum("rf,df->rd", grad_gates[0], w_gate[0], preferred_element_type=F32)
-            + jnp.einsum("rf,df->rd", grad_ups[0], w_up[0], preferred_element_type=F32)
-        ).astype(BF)
-        back_blocks.update(spread(drow, batches[i]))
-    grad_h2 = ring.scatter_sum(back_blocks)
-
-    acts_late, _ = lax.optimization_barrier((acts, grad_h2))
-    out_blocks = {}
-    for i in reversed(range(len(batches))):
-        eout = dot32(acts_late[i], w_down[0]).astype(BF).astype(F32)
-        out_blocks.update(spread((weights_of(batches[i]) * eout).astype(BF), batches[i]))
-    result = mid_rows + ring.scatter_sum(out_blocks)
-
-    all_rows = jnp.concatenate(rows_in, axis=0)
-    all_grads = jnp.concatenate(grads_in, axis=0)
-    all_acts = jnp.concatenate(acts, axis=0)
-    all_gates = jnp.concatenate(grad_gates, axis=0)
-    all_ups = jnp.concatenate(grad_ups, axis=0)
-
-    def rep_sum(v):
-        v = v.astype(BF)
-        out = v.astype(F32)
-        for k in range(1, reps):
-            out = out + from_rep(v, k).astype(F32)
-        return out
-
-    grad_wdown = rep_sum(jnp.einsum("rf,rd->fd", all_acts, all_grads, preferred_element_type=F32))
-    grad_wgate = rep_sum(jnp.einsum("rd,rf->df", all_rows, all_gates, preferred_element_type=F32))
-    grad_wup = rep_sum(jnp.einsum("rd,rf->df", all_rows, all_ups, preferred_element_type=F32))
+    grad_wdown = rep_send(jnp.einsum("rf,rd->fd", all_acts, all_grads, preferred_element_type=F32))
+    grad_wgate = rep_send(jnp.einsum("rd,rf->df", all_rows, all_gates, preferred_element_type=F32))
+    grad_wup = rep_send(jnp.einsum("rd,rf->df", all_rows, all_ups, preferred_element_type=F32))
 
     grad_out = cotangent[0].astype(F32)
     grad_mid_norm, ffn_terms = rms_backward(grad_h2, hat_two, inv_two, g_ffn)
@@ -335,7 +844,6 @@
         ],
         axis=1,
     ).astype(BF)
-    grad_wqkv = jnp.einsum("td,te->de", h1_b, grad_proj, preferred_element_type=F32).astype(BF)
     grad_h1 = rep_scatter(
         jnp.einsum("te,de->td", grad_proj, full_qkv, preferred_element_type=F32)
     )
@@ -344,26 +852,20 @@
     )
     grad_tokens = grad_mid + grad_rows_one
 
-    qkv_blocks = {
-        d: tuple(
-            lax.dynamic_slice(grad_wqkv, (rel[d, k] * shard, 0), (shard, 3 * wide))
-            for k in range(2)
-        )
-        for d in range(chips)
-    }
-    shard_qkv = ring.scatter_sum(qkv_blocks).astype(BF)
+    h1_t = h1_b.T.reshape(chips, 2, shard, seq_len)
+    h1_t = jnp.where(grp % 2 == 0, h1_t, h1_t[:, ::-1]).reshape(D, seq_len)
+    shard_qkv = qkv_gradient(chips, h1_t, grad_proj, 4)
+    grad_wdown = rep_sum(grad_wdown, grad_proj)
     qkv_all = [shard_qkv] + [from_rep(shard_qkv, k) for k in range(1, reps)]
     columns = jnp.stack(qkv_all, axis=0).reshape(reps, shard, 3, heads, HD)
     columns = columns[(jnp.arange(reps) - rep) % reps]
     shard_qkv = columns.transpose(1, 2, 3, 0, 4).reshape(shard, 3 * D).astype(F32)
 
-    zero_out = jnp.zeros((heads, reps, HD, D), BF)
-    whole_out = lax.dynamic_update_slice(
-        zero_out, grad_wout.astype(BF).reshape(heads, 1, HD, D), (0, rep, 0, 0)
-    ).reshape(D, D)
-    shard_out = lax.psum(
-        lax.psum_scatter(whole_out, "grp", scatter_dimension=0, tiled=True), "rep"
-    ).astype(F32)
+    grad_wgate = rep_sum(grad_wgate, shard_qkv)
+    grad_wup = rep_sum(grad_wup, shard_qkv)
+    result = mid_rows + lax.optimization_barrier((out_sum, shard_qkv))[0].astype(F32)
+
+    shard_out = out_gradient(ring, grad_wout.astype(BF), reps, heads, rel, rep, grp)
 
     grad_gains = jnp.concatenate(
         [

time: 1200 us -> 947 us (0.79)
  Pallas kernels: 0 us -> 442 us
  waiting for transfers between devices: 527 us -> 133 us
  matrix products: 290 us -> 118 us
  starting transfers between devices: 112 us -> 47 us
  local copies, waits for them, and re-layouts: 122 us -> 62.4 us
  other arithmetic: 115 us -> 99.9 us
    pallas_call x0 -> x4, Pallas kernels: none -> 442 us  [the longest x1 120 us: ring_gather(): pl.pallas_call(functools.partial(gather_kernel, chips), out_shape=jax.Sha...]
    ppermute x96 -> x10, waiting for transfers between devices: 300 us -> 0.03 us  [send(): return lax.ppermute(v, ('rep', 'grp'), pairs)]
    ppermute x7, waiting for transfers between devices: 213 us -> 91.9 us  [from_rep(): return lax.ppermute(v, 'rep', [((s + k) % reps, s) for s in range(reps)])]
    dot_general x48 -> x1, matrix products: 107 us -> 8.2 us  [per_device(): jnp.einsum('gct,gcd->gtd', pick, eout, preferred_element_type=F32)]
    dot_general x50 -> x4, matrix products: 102 us -> 24.4 us  [dot32(): return jnp.dot(a, b, preferred_element_type=F32)]
    ppermute x96 -> x10, starting transfers between devices: 94.1 us -> 31.9 us  [send(): return lax.ppermute(v, ('rep', 'grp'), pairs)]
    dynamic_update_slice x17 -> x0, local copies, waits for them, and re-layouts: 30.2 us -> none  [the longest x16 27.9 us: per_device(): lax.dynamic_update_slice(full_qkv, pair[k], (rel[d, k] * shard, 0))]
    convert_element_type x16 -> x7, other arithmetic: 31.1 us -> 12.6 us  [the longest x3 7.33 us: out_gradient(): up = hop((block(step) + up.astype(F32)).astype(BF), 1)]
  transfers between devices with their start and end apart: 110 -> 24, of which waited for: 30 -> 5; matrix products, arithmetic and copies ran while one was open for 40% -> 27% of each run, Pallas kernels for 0% -> 25%
where the time goes in v2:
time: 947 us; the launch traced here: 939 us
  Pallas kernels  442 us (47%)
  waiting for transfers between devices  133 us (14%)
  matrix products  118 us (12%)
  other arithmetic  99.9 us (11%)
  local copies, waits for them, and re-layouts  62.4 us (7%)
  starting transfers between devices  47 us (5%)
  between operations  36.2 us (4%)
    pallas_call x1, Pallas kernels, ring_gather(): pl.pallas_call(functools.partial(gather_kernel, chips), out_shape=jax.Sha...  120 us
    pallas_call x1, Pallas kernels, qkv_gradient(): pl.pallas_call(functools.partial(qkv_gradient_kernel, chips), out_shape=j...  111 us
    pallas_call x1, Pallas kernels, expert_rows(): pl.pallas_call(functools.partial(experts_kernel, chips, cap), out_shape=(...  109 us
    pallas_call x1, Pallas kernels, rows_back(): pl.pallas_call(functools.partial(rows_back_kernel, chips, cap), out_shape...  103 us
    ppermute x7, waiting for transfers between devices, from_rep(): return lax.ppermute(v, 'rep', [((s + k) % reps, s) for s in range(reps)])  91.9 us
    ppermute x10, starting transfers between devices, send(): return lax.ppermute(v, ('rep', 'grp'), pairs)  31.9 us
    ppermute x2, waiting for transfers between devices, to_rep(): return lax.ppermute(v, 'rep', [(s, (s + k) % reps) for s in range(reps)])  25.5 us
    dot_general x4, matrix products, dot32(): return jnp.dot(a, b, preferred_element_type=F32)  24.4 us
  transfers between devices with their start and end apart: 24, of which 5 were waited for; matrix products, arithmetic and copies ran while one was open for 27% of the time, Pallas kernels for 25%

profile of v2, /device:TPU:0, one launch (start us, length us, event | category | flops | bytes accessed | tf_op | source)
XLA Modules:
  0.0 939.1 jit_solution(10221858058656320098)
XLA Ops:
  8.0 4.1 reshape.421
  12.0 4.7 dynamic-slice_reduce_fusion
  17.8 119.9 %gather_qkv.1 = bf16[16,128,3072]{2,1,0:T(8,128)(2,1)} custom-call(bf16[128,3072]{1,0:T(8,128)(2,1)} %bitcast.266), custom_call_target="tpu_custom_call" | custom-call | bytes 25165824 | tf_op jit(solution)/shard_map/gather_qkv/pallas_call | solution.py:610
  140.1 3.7 all-to-all-start
  144.3 3.5 gather_fusion
  175.8 9.4 %fusion.33 = f32[512,3072]{1,0:T(8,128)S(1)} fusion(bf16[2048,3072]{1,0:T(8,128)(2,1)} %bitcast.249, f32[2048]{0:T(1024)S(1)} %get-tuple-element.75, f32[512]{0:T(512)S(1)} %add_rsqrt_fusion.2, bf16[256,2048]{1,0:T(8,128)(2,1)S(1)} %collective-permute-done, bf16[256,2048]{1,0:T(8,128)(2,1)S(1)} %bitcast.254), kind=kOutput, calls=%fused_computation.121 | convolution fusion | flops 6449790976 | bytes 20981760 | tf_op jit(solution)/shard_map/dot_general | solution.py:52
  185.3 3.3 slice_bitcast_fusion.3
  197.4 3.2 fusion.13
  208.3 4.0 convolution_convert_fusion.4
  212.3 3.0 constant_dynamic-slice_fusion.1
  222.4 3.4 convert_multiply_fusion
  230.6 15.1 %collective-permute-done.1 = bf16[256,2048]{1,0:T(8,128)(2,1)} collective-permute-done((bf16[256,2048]{1,0:T(8,128)(2,1)}, bf16[256,2048]{1,0:T(8,128)(2,1)}, u32[]{:S(2)}, u32[]{:S(2)}) %collective-permute-start.1) | collective-permute-done | bytes 1048608 | tf_op jit(solution)/shard_map/ppermute | solution.py:686
  248.9 14.6 %all-gather.6.cloned.1.call-done = bf16[4096,2048]{1,0:T(8,128)(2,1)} async-done(((bf16[256,2048]{1,0:T(8,128)(2,1)}), bf16[4096,2048]{1,0:T(8,128)(2,1)}) %all-gather.6.cloned.1.call-update) | async-done | bytes 16777232 | tf_op jit(solution)/shard_map/all_gather | solution.py:731
  263.5 109.0 %experts.1 = (bf16[8,288,2048]{2,1,0:T(8,128)(2,1)}, bf16[8,288,2048]{2,1,0:T(8,128)(2,1)}, bf16[8,288,1024]{2,1,0:T(8,128)(2,1)}, bf16[8,288,1024]{2,1,0:T(8,128)(2,1)}, bf16[8,288,1024]{2,1,0:T(8,128)(2,1)}) custom-call(bf16[256,2048]{1,0:T(8,128)(2,1)} %multiply_convert_fusion.3.h2_ref, bf16[16,256,2048]{2,1,0:T(8,128)(2,1)} %bitcast.284, ...), custom_call_target="tpu_custom_call" | custom-call | flops 28991029248 | bytes 209715200 | tf_op jit(solution)/shard_map/experts/pallas_call | solution.py:416
  372.5 102.6 %rows_back.1 = f32[256,2048]{1,0:T(8,128)} custom-call(bf16[8,288,1024]{2,1,0:T(8,128)(2,1)} %get-tuple-element.25.dg_ref, bf16[8,288,1024]{2,1,0:T(8,128)(2,1)} %get-tuple-element.26.du_ref, s32[16,256,1]{2,1,0:T(8,128)} %copy.206.slot_ref, bf16[2048,1024]{1,0:T(8,128)(2,1)} %bitcast.286, bf16[2048,1024]{1,0:T(8,128)(2,1)} %bitcast.288), custom_call_target="tpu_custom_call" | custom-call | flops 28991029248 | bytes 209715200 | tf_op jit(solution)/shard_map/rows_back/pallas_call | solution.py:523
  480.8 12.4 %multiply_convert_fusion = bf16[2304,2048]{1,0:T(8,128)(2,1)S(1)} fusion(bf16[2304,1024]{1,0:T(8,128)(2,1)} %bitcast.290, f32[2304]{0:T(1024)S(1)} %mul.466, bf16[1,1024,2048]{2,1,0:T(8,128)(2,1)S(1)} %copy-done.72), kind=kOutput, calls=%fused_computation.2 | convolution fusion | flops 9682550784 | bytes 18359296 | tf_op jit(solution)/shard_map/dot_general | solution.py:52
  493.2 8.2 convolution_convert_fusion
  501.5 15.6 %bitcast_convert_fusion.1 = bf16[2048,1024]{1,0:T(8,128)(2,1)} fusion(bf16[8,288,2048]{2,1,0:T(8,128)(2,1)} %get-tuple-element.28, bf16[8,288,1024]{2,1,0:T(8,128)(2,1)} %get-tuple-element.26.du_ref), kind=kOutput, calls=%fused_computation.6 | convolution fusion | flops 9665773568 | bytes 18350080 | tf_op jit(solution)/shard_map/rd,rf->df/dot_general | solution.py:816
  517.1 15.7 %bitcast_convert_fusion = bf16[1024,2048]{1,0:T(8,128)(2,1)} fusion(bf16[8,288,1024]{2,1,0:T(8,128)(2,1)S(1)} %bitcast.292, bf16[8,288,2048]{2,1,0:T(8,128)(2,1)} %get-tuple-element.33), kind=kOutput, calls=%fused_computation.5 | convolution fusion | flops 9665773568 | bytes 18350080 | tf_op jit(solution)/shard_map/rf,rd->fd/dot_general | solution.py:814
  532.8 12.1 %bitcast_convert_fusion.2 = bf16[2048,1024]{1,0:T(8,128)(2,1)} fusion(bf16[8,288,2048]{2,1,0:T(8,128)(2,1)S(1)} %bitcast.294, bf16[8,288,1024]{2,1,0:T(8,128)(2,1)S(1)} %bitcast.296), kind=kOutput, calls=%fused_computation.7 | convolution fusion | flops 9665773568 | bytes 18350080 | tf_op jit(solution)/shard_map/rd,rf->df/dot_general | solution.py:815
  547.8 3.9 convolution_convert_fusion.5
  553.0 6.0 convolution_convert_fusion.2
  560.3 5.8 multiply_reduce_fusion
  572.9 3.2 multiply_subtract_fusion.1
  579.8 4.4 fusion.35
  584.3 6.8 convolution_convert_fusion.3
  596.4 4.6 fusion.11
  603.1 5.5 convert_add_fusion
  608.5 3.4 copy-done.5
  612.0 3.4 collective-permute-start.6
  615.4 110.9 %qkv_gradient.1 = bf16[128,3072]{1,0:T(8,128)(2,1)} custom-call(bf16[2048,512]{1,0:T(8,128)(2,1)} %bitcast.272, bf16[512,3072]{1,0:T(8,128)(2,1)} %pad_maximum_fusion.grad_ref), custom_call_target="tpu_custom_call" | custom-call | flops 6442450944 | bytes 209715200 | tf_op jit(solution)/shard_map/qkv_gradient/pallas_call | solution.py:579
  728.6 4.3 collective-permute-start.7
  732.8 10.0 %fusion.53 = f32[512,2048]{1,0:T(8,128)S(1)} fusion(bf16[2048,3072]{1,0:T(8,128)(2,1)} %bitcast.250, bf16[512,1024]{1,0:T(8,128)(2,1)S(1)} %copy.233, bf16[512,1024]{1,0:T(8,128)(2,1)S(1)} %get-tuple-element.44, bf16[512,1024]{1,0:T(8,128)(2,1)} %copy-done.33), kind=kOutput, calls=%fused_computation.179 | convolution fusion | flops 6451888128 | bytes 19922944 | tf_op jit(solution)/shard_map/te,de->td/dot_general | solution.py:848
  744.0 88.3 %collective-permute-done.3 = bf16[128,3072]{1,0:T(8,128)(2,1)} collective-permute-done((bf16[128,3072]{1,0:T(8,128)(2,1)}, bf16[128,3072]{1,0:T(8,128)(2,1)}, u32[]{:S(2)}, u32[]{:S(2)}) %collective-permute-start.3) | collective-permute-done | bytes 786464 | tf_op jit(solution)/shard_map/ppermute | solution.py:683
  837.0 3.2 collective-permute-start.8
  841.3 10.4 %collective-permute-done.4 = bf16[256,2048]{1,0:T(8,128)(2,1)} collective-permute-done((bf16[256,2048]{1,0:T(8,128)(2,1)}, bf16[256,2048]{1,0:T(8,128)(2,1)}, u32[]{:S(2)}, u32[]{:S(2)}) %collective-permute-start.4) | collective-permute-done | bytes 1048608 | tf_op jit(solution)/shard_map/ppermute | solution.py:686
  851.7 5.0 collective-permute-start.10
  856.7 3.2 multiply_reduce_fusion.3
  860.6 4.0 all-to-all-start.1
  867.5 3.8 collective-permute-start.11
  874.0 3.7 reshape.437
  877.8 3.6 collective-permute-done.15
  883.5 3.5 collective-permute-start.12
  887.0 8.8 add_bitcast_fusion
  899.6 3.4 collective-permute-start.13
  903.0 8.9 add_bitcast_fusion.1
  914.9 8.9 add_bitcast_fusion.2
  925.8 6.5 add_bitcast_fusion.3
  (297 shorter events, 98.2 us)
Async XLA Ops:
  7.2 137.1 %copy-start = (s32[1,512]{1,0:T(1,128)S(1)}, s32[1,512]{1,0:T(1,128)}, u32[]{:S(2)}) copy-start(s32[1,512]{1,0:T(1,128)} %param.19) | copy-start | bytes 6148
  7.2 205.1 %all-gather.4.cloned.1.call-start = ((), (), s32[]{:S(2)}) async-start(), calls=%async_computation.3 | async-start | bytes 8912896 | tf_op jit(solution)/shard_map/all_gather | solution.py:725
  7.9 255.6 %all-gather.6.cloned.1.call-start = ((), (), s32[]{:S(2)}) async-start(), calls=%async_computation.5 | async-start | bytes 17825792 | tf_op jit(solution)/shard_map/all_gather | solution.py:731
  17.8 120.0 %copy-start.25 = (bf16[1,256,2048]{2,1,0:T(8,128)(2,1)S(1)}, bf16[1,256,2048]{2,1,0:T(8,128)(2,1)}, u32[]{:S(2)}) copy-start(bf16[1,256,2048]{2,1,0:T(8,128)(2,1)} %param.12) | copy-start | bytes 3145732
  17.8 121.6 %copy-start.71 = (bf16[272]{0:T(512)(128)(2,1)S(1)}, bf16[272]{0:T(512)(128)(2,1)}, u32[]{:S(2)}) copy-start(bf16[272]{0:T(512)(128)(2,1)} %param.15) | copy-start | bytes 1636
  17.8 121.6 %copy-start.69 = (f32[1,256,8]{1,2,0:T(8,128)S(1)}, f32[1,256,8]{1,2,0:T(8,128)}, u32[]{:S(2)}) copy-start(f32[1,256,8]{1,2,0:T(8,128)} %param.21) | copy-start | bytes 24580
  17.8 121.6 %copy-start.70 = (s32[1,256,8]{1,2,0:T(8,128)S(1)}, s32[1,256,8]{1,2,0:T(8,128)}, u32[]{:S(2)}) copy-start(s32[1,256,8]{1,2,0:T(8,128)} %param.20) | copy-start | bytes 24580
  137.8 37.1 %collective-permute-start = (bf16[256,2048]{1,0:T(8,128)(2,1)S(1)}, bf16[256,2048]{1,0:T(8,128)(2,1)S(1)}, u32[]{:S(2)}, u32[]{:S(2)}) collective-permute-start(bf16[256,2048]{1,0:T(8,128)(2,1)S(1)} %bitcast.252), channel_id=1, source_target_pairs={{16,0},{0,16},{17,1},{1,17},{18,2},{2,18},{19,3},{3,19},{20,4},{4,... | collective-permute-start | bytes 3145736 | tf_op jit(solution)/shard_map/ppermute | solution.py:683
  140.1 31.8 %all-to-all-start = ((f32[16,1,528]{2,1,0:T(1,128)}), f32[16,1,528]{2,1,0:T(1,128)S(1)}, u32[]{:S(2)}, u32[]{:S(2)}) async-start(f32[16,1,528]{2,1,0:T(1,128)} %all_to_all.14), calls=%async_computation | async-start | bytes 81920 | tf_op jit(solution)/shard_map/all_to_all | solution.py:712
  143.9 781.0 %reduce-scatter.2.cloned.1.call-start = ((), (), s32[]{:S(2)}) async-start(), calls=%async_computation.4 | async-start | bytes 17825792 | tf_op jit(solution)/shard_map/reduce_scatter | solution.py:799
  148.0 58.6 %copy-start.28 = (pred[512,512]{0,1:T(8,128)(4,1)}, pred[512,512]{0,1:T(8,128)(4,1)S(1)}, u32[]{:S(2)}) copy-start(pred[512,512]{0,1:T(8,128)(4,1)S(1)} %broadcast_compare_fusion) | copy-start | bytes 786436
  172.0 48.0 %copy-start.57 = (f32[16,256]{1,0:T(8,128)}, f32[16,256]{1,0:T(8,128)S(1)}, u32[]{:S(2)}) copy-start(f32[16,256]{1,0:T(8,128)S(1)} %slice.165.weight_ref) | copy-start | bytes 49156
  172.2 47.7 %copy-start.45 = (s32[16,256]{1,0:T(8,128)}, s32[16,256]{1,0:T(8,128)S(1)}, u32[]{:S(2)}) copy-start(s32[16,256]{1,0:T(8,128)S(1)} %fusion.17.slot_ref) | copy-start | bytes 49156
  174.2 23.1 %copy-start.65 = (f32[128]{0:T(128)}, f32[128]{0:T(128)S(1)}, u32[]{:S(2)}) copy-start(f32[128]{0:T(128)S(1)} %get-tuple-element.76) | copy-start | bytes 1540
  174.2 23.1 %copy-start.67 = (f32[128]{0:T(128)}, f32[128]{0:T(128)S(1)}, u32[]{:S(2)}) copy-start(f32[128]{0:T(128)S(1)} %get-tuple-element.77) | copy-start | bytes 1540
  174.8 47.5 %copy-start.55 = (f32[2048]{0:T(1024)}, f32[2048]{0:T(1024)S(1)}, u32[]{:S(2)}) copy-start(f32[2048]{0:T(1024)S(1)} %get-tuple-element.75) | copy-start | bytes 24580
  174.8 302.7 %copy-start.51 = (f32[2048]{0:T(1024)}, f32[2048]{0:T(1024)S(1)}, u32[]{:S(2)}) copy-start(f32[2048]{0:T(1024)S(1)} %get-tuple-element.74) | copy-start | bytes 24580
  175.4 47.0 %copy-start.62 = (f32[512]{0:T(512)}, f32[512]{0:T(512)S(1)}, u32[]{:S(2)}) copy-start(f32[512]{0:T(512)S(1)} %add_rsqrt_fusion.2) | copy-start | bytes 6148
  197.3 24.3 %copy-start.49 = (f32[512,8]{0,1:T(8,128)}, f32[512,8]{0,1:T(8,128)S(1)}, u32[]{:S(2)}) copy-start(f32[512,8]{0,1:T(8,128)S(1)} %add_rsqrt_fusion) | copy-start | bytes 49156
  197.3 23.4 %copy-start.47 = (f32[512,8]{0,1:T(8,128)}, f32[512,8]{0,1:T(8,128)S(1)}, u32[]{:S(2)}) copy-start(f32[512,8]{0,1:T(8,128)S(1)} %add_rsqrt_fusion.1) | copy-start | bytes 49156
  219.9 25.8 %collective-permute-start.1 = (bf16[256,2048]{1,0:T(8,128)(2,1)}, bf16[256,2048]{1,0:T(8,128)(2,1)}, u32[]{:S(2)}, u32[]{:S(2)}) collective-permute-start(bf16[256,2048]{1,0:T(8,128)(2,1)} %slice.225), channel_id=1, source_target_pairs={{0,16},{16,0},{1,17},{17,1},{2,18},{18,2},{3,19},{19,3},{4,20},{20... | collective-permute-start | bytes 3145736 | tf_op jit(solution)/shard_map/ppermute | solution.py:686
  228.7 17.0 %copy-start.14 = (f32[512,2048]{1,0:T(8,128)S(1)}, f32[512,2048]{1,0:T(8,128)}, u32[]{:S(2)}) copy-start(f32[512,2048]{1,0:T(8,128)} %copy-done.13) | copy-start | bytes 12582916
  247.5 230.1 %copy-start.3 = (f32[256,2048]{1,0:T(8,128)}, f32[256,2048]{1,0:T(8,128)S(1)}, u32[]{:S(2)}) copy-start(f32[256,2048]{1,0:T(8,128)S(1)} %get-tuple-element.43) | copy-start | bytes 6291460
  247.5 230.1 %copy-start.58 = (f32[256]{0:T(256)}, f32[256]{0:T(256)S(1)}, u32[]{:S(2)}) copy-start(f32[256]{0:T(256)S(1)} %add_rsqrt_fusion.3) | copy-start | bytes 3076
  479.3 68.5 %collective-permute-start.2 = (bf16[256,2048]{1,0:T(8,128)(2,1)}, bf16[256,2048]{1,0:T(8,128)(2,1)}, u32[]{:S(2)}, u32[]{:S(2)}) collective-permute-start(bf16[256,2048]{1,0:T(8,128)(2,1)} %fusion.52), channel_id=1, source_target_pairs={{16,0},{0,16},{17,1},{1,17},{18,2},{2,18},{19,3},{3,19},{20,4},{4,... | collective-permute-start | bytes 3145736 | tf_op jit(solution)/shard_map/ppermute | solution.py:683
  501.4 31.3 %slice-start.5 = ((s8[9437184]{0:T(1024)(128)(4,1)}), s8[4194304]{0:T(1024)(128)(4,1)S(1)}, s32[]{:S(2)}) async-start(s8[9437184]{0:T(1024)(128)(4,1)} %bitcast.293), calls=%async_computation.11 | async-start | bytes 8388608
  501.4 31.3 %slice-start.6 = ((s8[9437184]{0:T(1024)(128)(4,1)}), s8[4194304]{0:T(1024)(128)(4,1)S(1)}, s32[]{:S(2)}) async-start(s8[9437184]{0:T(1024)(128)(4,1)} %bitcast.293), calls=%async_computation.12 | async-start | bytes 8388608
  501.5 31.3 %slice-start.8 = ((s8[4718592]{0:T(1024)(128)(4,1)}), s8[4194304]{0:T(1024)(128)(4,1)S(1)}, s32[]{:S(2)}) async-start(s8[4718592]{0:T(1024)(128)(4,1)} %bitcast.295), calls=%async_computation.14 | async-start | bytes 8388608
  544.9 337.0 %collective-permute-start.18 = (bf16[1024,2048]{1,0:T(8,128)(2,1)}, bf16[1024,2048]{1,0:T(8,128)(2,1)}, u32[]{:S(2)}, u32[]{:S(2)}) collective-permute-start(bf16[1024,2048]{1,0:T(8,128)(2,1)} %bitcast_convert_fusion), channel_id=1, source_target_pairs={{16,0},{0,16},{17,1},{1,17},{18,2},{2,18},{19,3},{3,19},{20,4},{4,... | collective-permute-start | bytes 12582920 | tf_op jit(solution)/shard_map/ppermute | solution.py:683
  545.8 336.1 %collective-permute-start.17 = (bf16[2048,1024]{1,0:T(8,128)(2,1)}, bf16[2048,1024]{1,0:T(8,128)(2,1)}, u32[]{:S(2)}, u32[]{:S(2)}) collective-permute-start(bf16[2048,1024]{1,0:T(8,128)(2,1)} %bitcast_convert_fusion.1), channel_id=1, source_target_pairs={{16,0},{0,16},{17,1},{1,17},{18,2},{2,18},{19,3},{3,19},{20,4},{4,... | collective-permute-start | bytes 12582920 | tf_op jit(solution)/shard_map/ppermute | solution.py:683
  547.0 335.0 %collective-permute-start.16 = (bf16[2048,1024]{1,0:T(8,128)(2,1)}, bf16[2048,1024]{1,0:T(8,128)(2,1)}, u32[]{:S(2)}, u32[]{:S(2)}) collective-permute-start(bf16[2048,1024]{1,0:T(8,128)(2,1)} %bitcast_convert_fusion.2), channel_id=1, source_target_pairs={{16,0},{0,16},{17,1},{1,17},{18,2},{2,18},{19,3},{3,19},{20,4},{4,... | collective-permute-start | bytes 12582920 | tf_op jit(solution)/shard_map/ppermute | solution.py:683
  559.0 44.0 %collective-permute-start.5 = (bf16[1024,2048]{1,0:T(8,128)(2,1)}, bf16[1024,2048]{1,0:T(8,128)(2,1)}, u32[]{:S(2)}, u32[]{:S(2)}) collective-permute-start(bf16[1024,2048]{1,0:T(8,128)(2,1)} %convolution_convert_fusion.2), channel_id=1, source_target_pairs={{1,0},{3,2},{5,4},{7,6},{9,8},{11,10},{13,12},{15,14},{16,17},{18,... | collective-permute-start | bytes 12582920 | tf_op jit(solution)/shard_map/ppermute | solution.py:639
  612.0 114.4 %collective-permute-start.6 = (bf16[64,2048]{1,0:T(8,128)(2,1)S(1)}, bf16[64,2048]{1,0:T(8,128)(2,1)S(1)}, u32[]{:S(2)}, u32[]{:S(2)}) collective-permute-start(bf16[64,2048]{1,0:T(8,128)(2,1)S(1)} %get-tuple-element.68), channel_id=1, source_target_pairs={{0,4},{2,0},{4,8},{6,2},{8,12},{10,6},{12,14},{14,10},{17,21},{19,... | collective-permute-start | bytes 786440 | tf_op jit(solution)/shard_map/ppermute | solution.py:639
  726.4 105.9 %collective-permute-start.3 = (bf16[128,3072]{1,0:T(8,128)(2,1)}, bf16[128,3072]{1,0:T(8,128)(2,1)}, u32[]{:S(2)}, u32[]{:S(2)}) collective-permute-start(bf16[128,3072]{1,0:T(8,128)(2,1)} %qkv_gradient.1), channel_id=1, source_target_pairs={{16,0},{0,16},{17,1},{1,17},{18,2},{2,18},{19,3},{3,19},{20,4},{4,... | collective-permute-start | bytes 2359304 | tf_op jit(solution)/shard_map/ppermute | solution.py:683
  728.6 106.1 %collective-permute-start.7 = (bf16[128,2048]{1,0:T(8,128)(2,1)}, bf16[128,2048]{1,0:T(8,128)(2,1)}, u32[]{:S(2)}, u32[]{:S(2)}) collective-permute-start(bf16[128,2048]{1,0:T(8,128)(2,1)} %fusion.25), channel_id=1, source_target_pairs={{0,4},{2,0},{4,8},{6,2},{8,12},{10,6},{12,14},{14,10},{17,21},{19,... | collective-permute-start | bytes 1572872 | tf_op jit(solution)/shard_map/ppermute | solution.py:639
  742.8 91.9 %copy-start.30 = (f32[512,2048]{1,0:T(8,128)}, f32[512,2048]{1,0:T(8,128)S(1)}, u32[]{:S(2)}) copy-start(f32[512,2048]{1,0:T(8,128)S(1)} %fusion.53) | copy-start | bytes 12582916
  742.8 90.4 %copy-start.43 = (bf16[128,3072]{1,0:T(8,128)(2,1)S(1)}, bf16[128,3072]{1,0:T(8,128)(2,1)}, u32[]{:S(2)}) copy-start(bf16[128,3072]{1,0:T(8,128)(2,1)} %qkv_gradient.1) | copy-start | bytes 2359300
  832.3 19.4 %collective-permute-start.4 = (bf16[256,2048]{1,0:T(8,128)(2,1)}, bf16[256,2048]{1,0:T(8,128)(2,1)}, u32[]{:S(2)}, u32[]{:S(2)}) collective-permute-start(bf16[256,2048]{1,0:T(8,128)(2,1)} %slice.224), channel_id=1, source_target_pairs={{0,16},{16,0},{1,17},{17,1},{2,18},{18,2},{3,19},{19,3},{4,20},{20... | collective-permute-start | bytes 3145736 | tf_op jit(solution)/shard_map/ppermute | solution.py:686
  837.0 27.6 %collective-permute-start.8 = (bf16[128,2048]{1,0:T(8,128)(2,1)}, bf16[128,2048]{1,0:T(8,128)(2,1)}, u32[]{:S(2)}, u32[]{:S(2)}) collective-permute-start(bf16[128,2048]{1,0:T(8,128)(2,1)} %fusion.26), channel_id=1, source_target_pairs={{0,4},{2,0},{4,8},{6,2},{8,12},{10,6},{12,14},{14,10},{17,21},{19,... | collective-permute-start | bytes 1572872 | tf_op jit(solution)/shard_map/ppermute | solution.py:639
  840.4 16.3 %copy-start.56 = (f32[2048]{0:T(1024)S(1)}, f32[2048]{0:T(1024)}, u32[]{:S(2)}) copy-start(f32[2048]{0:T(1024)} %copy-done.55) | copy-start | bytes 24580
  851.7 12.9 %collective-permute-start.10 = (bf16[64,2048]{1,0:T(8,128)(2,1)S(1)}, bf16[64,2048]{1,0:T(8,128)(2,1)S(1)}, u32[]{:S(2)}, u32[]{:S(2)}) collective-permute-start(bf16[64,2048]{1,0:T(8,128)(2,1)S(1)} %get-tuple-element.69), channel_id=1, source_target_pairs={{0,2},{2,6},{4,0},{6,10},{8,4},{10,14},{12,8},{14,12},{17,19},{19,... | collective-permute-start | bytes 786440 | tf_op jit(solution)/shard_map/ppermute | solution.py:639
  860.6 17.1 %all-to-all-start.1 = ((f32[16,1,272]{2,1,0:T(1,128)}), f32[16,1,272]{2,1,0:T(1,128)S(1)}, u32[]{:S(2)}, u32[]{:S(2)}) async-start(f32[16,1,272]{2,1,0:T(1,128)} %all_to_all.17), calls=%async_computation.2 | async-start | bytes 49152 | tf_op jit(solution)/shard_map/all_to_all | solution.py:878
  867.5 14.5 %collective-permute-start.11 = (bf16[128,2048]{1,0:T(8,128)(2,1)}, bf16[128,2048]{1,0:T(8,128)(2,1)}, u32[]{:S(2)}, u32[]{:S(2)}) collective-permute-start(bf16[128,2048]{1,0:T(8,128)(2,1)} %get-tuple-element.47), channel_id=1, source_target_pairs={{0,2},{2,6},{4,0},{6,10},{8,4},{10,14},{12,8},{14,12},{17,19},{19,... | collective-permute-start | bytes 1572872 | tf_op jit(solution)/shard_map/ppermute | solution.py:639
  877.7 3.6 collective-permute-start.15
  883.5 14.8 %collective-permute-start.12 = (bf16[128,2048]{1,0:T(8,128)(2,1)S(1)}, bf16[128,2048]{1,0:T(8,128)(2,1)S(1)}, u32[]{:S(2)}, u32[]{:S(2)}) collective-permute-start(bf16[128,2048]{1,0:T(8,128)(2,1)S(1)} %fusion.23), channel_id=1, source_target_pairs={{0,2},{2,6},{4,0},{6,10},{8,4},{10,14},{12,8},{14,12},{17,19},{19,... | collective-permute-start | bytes 1572872 | tf_op jit(solution)/shard_map/ppermute | solution.py:639
  895.8 16.1 %collective-permute-start.9 = (bf16[128,2048]{1,0:T(8,128)(2,1)S(1)}, bf16[128,2048]{1,0:T(8,128)(2,1)S(1)}, u32[]{:S(2)}, u32[]{:S(2)}) collective-permute-start(bf16[128,2048]{1,0:T(8,128)(2,1)S(1)} %copy-done.44), channel_id=1, source_target_pairs={{0,4},{2,0},{4,8},{6,2},{8,12},{10,6},{12,14},{14,10},{17,21},{19,... | collective-permute-start | bytes 1572872 | tf_op jit(solution)/shard_map/ppermute | solution.py:639
  899.6 12.2 %collective-permute-start.13 = (bf16[128,2048]{1,0:T(8,128)(2,1)S(1)}, bf16[128,2048]{1,0:T(8,128)(2,1)S(1)}, u32[]{:S(2)}, u32[]{:S(2)}) collective-permute-start(bf16[128,2048]{1,0:T(8,128)(2,1)S(1)} %fusion.24), channel_id=1, source_target_pairs={{0,2},{2,6},{4,0},{6,10},{8,4},{10,14},{12,8},{14,12},{17,19},{19,... | collective-permute-start | bytes 1572872 | tf_op jit(solution)/shard_map/ppermute | solution.py:639
  913.3 10.6 %collective-permute-start.14 = (bf16[128,2048]{1,0:T(8,128)(2,1)S(1)}, bf16[128,2048]{1,0:T(8,128)(2,1)S(1)}, u32[]{:S(2)}, u32[]{:S(2)}) collective-permute-start(bf16[128,2048]{1,0:T(8,128)(2,1)S(1)} %fusion.29), channel_id=1, source_target_pairs={{0,16},{2,18},{4,20},{6,22},{8,24},{10,26},{12,28},{14,30},{17,1},... | collective-permute-start | bytes 1572872 | tf_op jit(solution)/shard_map/ppermute | solution.py:639
  (59 other events, 300.0 us)
Sparse Core Ops, SparseCore 0:
  10.2 115.4 all-gather.3
  137.9 125.5 all-gather.5
  501.5 211.9 reduce-scatter.1

commit v3 on v2

--- a/solution.py
+++ b/solution.py
@@ -29,23 +29,6 @@
     scaled = grad_out * gain_vec
     grad_in = inverse * (scaled - normed * jnp.mean(scaled * normed, axis=-1, keepdims=True))
     return (grad_in, grad_out * normed)
-
-
-def rotate(values, positions, direction):
-    half_size = values.shape[-1] // 2
-    frequency = rope_base ** (-2.0 * jnp.arange(half_size, dtype=jnp.float32) / values.shape[-1])
-    angles = positions[:, None] * frequency[None, :]
-    cosine_table = jnp.cos(angles)[:, None, :]
-    sine_table = direction * jnp.sin(angles)[:, None, :]
-    first_half = values[..., :half_size]
-    second_half = values[..., half_size:]
-    return jnp.concatenate(
-        [
-            first_half * cosine_table - second_half * sine_table,
-            second_half * cosine_table + first_half * sine_table,
-        ],
-        axis=-1,
-    )
 
 
 def dot32(a, b):
@@ -154,11 +137,16 @@
     def device(self, d):
         return 2 * self.chip(d) + self.core
 
-    def meet(self):
+    def meet(self, reps=1):
         barrier = pltpu.get_barrier_semaphore()
         for dev in (self.ahead, self.back, self.flip):
             pl.semaphore_signal(barrier, inc=1, device_id={"grp": dev}, device_id_type=MESH)
-        pl.semaphore_wait(barrier, 3)
+        rep = lax.axis_index("rep")
+        for k in range(1, reps):
+            pl.semaphore_signal(
+                barrier, inc=1, device_id={"rep": (rep + k) % reps}, device_id_type=MESH
+            )
+        pl.semaphore_wait(barrier, 2 + reps)
 
     def copy(self, src, dst, send_sem, recv_sem, dev):
         return pltpu.make_async_remote_copy(
@@ -182,40 +170,48 @@
         for c in self.started:
             c.wait_send()
 
-    def gather(self, own, slot, up, down, side, use):
-        half, rows = self.half, own.shape[0]
-        cut = rows // 2
-        self.send(own, slot(self.me), up, 0, self.ahead)
-        self.send(own, slot(self.me), down, 0, self.back)
-        self.send(own, slot(self.me), side, 0, self.flip)
+    def gather(self, items, use):
+        half = self.half
+
+        def parts(ref):
+            cut = ref.shape[0] // 2
+            return ref.at[pl.ds(0, cut)], ref.at[pl.ds(cut, ref.shape[0] - cut)]
+
+        for own, slot, up, down, side in items:
+            self.send(own, slot(self.me), up, 0, self.ahead)
+            self.send(own, slot(self.me), down, 0, self.back)
+            self.send(own, slot(self.me), side, 0, self.flip)
+        yield
 
         def ready(d):
             dev = self.device(d)
-            self.wait(slot(dev + 1 - 2 * self.core), side, d % self.chips)
+            for _, slot, _, _, side in items:
+                self.wait(slot(dev + 1 - 2 * self.core), side, d % self.chips)
             use(d)
 
+        ready(0)
         for s in range(1, half):
             last = s == half - 1
-            a, b = slot(self.device(-s)), slot(self.device(s))
-            self.wait(a, up, s - 1)
-            part = a.at[pl.ds(0, cut)] if last else a
-            self.send(part, part, up, s, self.ahead)
-            self.send(a, a, side, -s % self.chips, self.flip)
-            self.wait(b, down, s - 1)
-            part = b.at[pl.ds(cut, rows - cut)] if last else b
-            self.send(part, part, down, s, self.back)
-            self.send(b, b, side, s, self.flip)
-            for d in sorted({1 - s, s - 1}):
+            for _, slot, up, down, side in items:
+                a, b = slot(self.device(-s)), slot(self.device(s))
+                self.wait(a, up, s - 1)
+                part = parts(a)[0] if last else a
+                self.send(part, part, up, s, self.ahead)
+                self.send(a, a, side, -s % self.chips, self.flip)
+                self.wait(b, down, s - 1)
+                part = parts(b)[1] if last else b
+                self.send(part, part, down, s, self.back)
+                self.send(b, b, side, s, self.flip)
+            for d in (-s, s):
                 ready(d)
-        far = slot(self.device(half))
-        self.wait(far.at[pl.ds(0, cut)], up, half - 1)
-        self.wait(far.at[pl.ds(cut, rows - cut)], down, half - 1)
-        self.send(far, far, side, half, self.flip)
-        for d in sorted({1 - half, half - 1}):
-            ready(d)
+            yield
+        for _, slot, up, down, side in items:
+            far = slot(self.device(half))
+            low, high = parts(far)
+            self.wait(low, up, half - 1)
+            self.wait(high, down, half - 1)
+            self.send(far, far, side, half, self.flip)
         ready(half)
-        self.drain()
-
 
     def scatter(self, rows, produce, mine, out, came, far, up_in, down_in, up, down, side, finish):
         half, chips = self.half, self.chips
@@ -238,7 +234,7 @@
 
             lax.fori_loop(0, (last - first) // strip, step, 0)
 
-        for d in (half, half - 1, 1 - half):
+        for d in (half, half - 1):
             make(d)
         self.wait(came.at[half], side, half)
 
@@ -249,6 +245,8 @@
         low, high = pl.ds(0, cut), pl.ds(cut, rows - cut)
         self.send(far.at[low], up_in.at[0, low], up, 0, self.ahead)
         self.send(far.at[high], down_in.at[0, high], down, 0, self.back)
+        make(1 - half)
+        yield
         for s in range(half - 1, 0, -1):
             i = half - s
             for d in sorted({s - 1, 1 - s}):
@@ -277,6 +275,7 @@
                     strips(0, cut, fresh)
                     strips(cut, rows, onto)
                 self.send(buf.at[i - 1], buf.at[i], sems, i, target)
+            yield
         self.wait(came.at[0], side, 0)
         self.wait(up_in.at[half - 1], up, half - 1)
         self.wait(down_in.at[half - 1], down, half - 1)
@@ -290,6 +289,11 @@
             )
 
         strips(0, rows, total)
+
+    def turn(self, *rings):
+        rings = list(rings)
+        while rings:
+            rings = [r for r in rings if next(r, self) is not self]
         self.drain()
 
 
@@ -309,12 +313,13 @@
     return lax.dot_general(a, b, (((1,), (1,)), ((), ())), preferred_element_type=F32)
 
 
+def dot_tn(a, b):
+    return lax.dot_general(a, b, (((0,), (0,)), ((), ())), preferred_element_type=F32)
+
+
 def tiles(count, width, body):
-    def step(i, carry):
-        body(pl.ds(pl.multiple_of(i * width, width), width))
-        return carry
-
-    lax.fori_loop(0, count, step, 0)
+    for i in range(count):
+        body(pl.ds(i * width, width))
 
 
 def experts_kernel(
@@ -385,7 +390,7 @@
                 xs_b[p, rows, at] = dot32(pick, held[dev, :, at]).astype(BF)
                 de_b[p, rows, at] = (scale * dot32(pick, dy[p, k, :, at])).astype(BF)
 
-            tiles(width // 512, 512, choose)
+            tiles(width // 1024, 1024, choose)
 
         def hidden(at):
             gpre = dot32(xs_b[p], wg[:, at])
@@ -396,11 +401,11 @@
             dg_b[p, :, at] = (dact * upre * sig * (1.0 + gpre * (1.0 - sig))).astype(BF)
             du_b[p, :, at] = (dact * gpre * sig).astype(BF)
 
-        tiles(ff // 256, 256, hidden)
+        tiles(ff // 512, 512, hidden)
         for c in out_copies(i):
             c.start()
 
-    hops.gather(h2_ref, lambda dev: held.at[dev], up, down, side, use)
+    hops.turn(hops.gather([(h2_ref, lambda dev: held.at[dev], up, down, side)], use))
     for i in (chips - 2, chips - 1):
         for c in out_copies(i):
             c.wait()
@@ -489,7 +494,7 @@
         def back(at):
             drow[:, at] = (dot_nt(dg[p], wg[at, :]) + dot_nt(du[p], wu[at, :])).astype(BF)
 
-        tiles(width // 256, 256, back)
+        tiles(width // 512, 512, back)
         chip = hops.chip(d)
         lanes = lax.broadcasted_iota(jnp.int32, (tok, cap), 1)
 
@@ -505,13 +510,13 @@
             same_ref[:, at] = dot32(same_pick, drow[same_rows, at])
             other_ref[:, at] = dot32(other_pick, drow[other_rows, at]).astype(BF)
 
-        tiles(width // 512, 512, spread)
+        tiles(width // 1024, 1024, spread)
 
     def finish(value, at):
         total_ref[at, :] = value
 
-    hops.scatter(
-        tok, produce, mine, out, came, far, up_in, down_in, up, down, side, finish
+    hops.turn(
+        hops.scatter(tok, produce, mine, out, came, far, up_in, down_in, up, down, side, finish)
     )
 
 
@@ -546,123 +551,446 @@
     )(dg, du, slot, wg, wu)
 
 
-def qkv_gradient_kernel(
-    chips, h1_ref, grad_ref, total_ref, mine, out, came, far, up_in, down_in, up, down, side
+def turned(v, cosine, sine):
+    return v * cosine + pltpu.roll(v, HD // 2, 1) * sine
+
+
+def head_of(proj, at, gain, cosine, sine):
+    value = proj[:, at]
+    inverse = lax.rsqrt(jnp.mean(value * value, axis=-1, keepdims=True) + epsilon)
+    hat = value * inverse
+    return hat, inverse, turned(hat * gain, cosine, sine).astype(BF)
+
+
+def softmax_rows(queries, keys, docs_q, docs_k):
+    raw = dot_nt(queries, keys) * HD ** (-0.5)
+    raw = jnp.where(docs_q == docs_k, raw, -1e30)
+    grown = jnp.exp(raw - jnp.max(raw, axis=-1, keepdims=True))
+    return grown * (1.0 / jnp.sum(grown, axis=-1, keepdims=True))
+
+
+def columns_of(block, head, heads):
+    return pl.ds(pl.multiple_of((block * heads + head) * HD, HD), HD)
+
+
+def attention_kernel(
+    chips, reps, heads,
+    cot_ref, seq_ref, ga_ref, gf_ref, gq_ref, gk_ref, cos_ref, sin_ref, dc_ref, dr_ref, wq_hbm, wo_hbm,
+    dy_ref, h1_ref, proj_ref, ob_ref, mid_ref, h2_ref,
+    wq, wo, give, came, up, down, side, rep_sem, own_sem,
 ):
     hops = Hops(chips)
-    shard, width = total_ref.shape
-    hops.meet()
-
-    def produce(d, same_ref, other_ref):
-        first = 2 * hops.chip(d) * shard
-        rows = pl.ds(pl.multiple_of(first, 2 * shard), 2 * shard)
-
-        def block(at):
-            value = dot32(h1_ref[rows, :], grad_ref[:, at])
-            same_ref[:, at] = value[:shard]
-            other_ref[:, at] = value[shard:].astype(BF)
-
-        tiles(width // 512, 512, block)
-
-    def finish(value, at):
-        total_ref[at, :] = value.astype(BF)
-
-    hops.scatter(
-        shard, produce, mine, out, came, far, up_in, down_in, up, down, side, finish
-    )
-
-
-def qkv_gradient(chips, h1_t, grad, collective_id):
-    shard = h1_t.shape[0] // (2 * chips)
-    width = grad.shape[1]
+    rep = lax.axis_index("rep")
+    seq_len, width = seq_ref.shape
+    tok = mid_ref.shape[0]
+    block = min(256, seq_len)
+    loads = [
+        pltpu.make_async_copy(a, b, own_sem.at[i])
+        for i, (a, b) in enumerate(((wq_hbm, wq), (wo_hbm, wo), (cot_ref, dy_ref.at[hops.me])))
+    ]
+    hops.meet(reps)
+    ring = hops.gather([(cot_ref, lambda dev: dy_ref.at[dev], up, down, side)], lambda d: None)
+    next(ring)
+    for c in loads:
+        c.start()
+
+    def normed(i, carry):
+        rows = pl.ds(pl.multiple_of(i * 64, 64), 64)
+        v = seq_ref[rows, :].astype(F32)
+        v = v * lax.rsqrt(jnp.mean(v * v, axis=-1, keepdims=True) + epsilon)
+        h1_ref[rows, :] = (v * ga_ref[...]).astype(BF)
+        return carry
+
+    lax.fori_loop(0, seq_len // 64, normed, 0)
+    loads[0].wait()
+    total = 3 * heads * HD
+    step = 512 if total % 512 == 0 else HD
+    for i in range(total // step):
+        at = pl.ds(i * step, step)
+        proj_ref[:, at] = dot32(h1_ref[...], wq[:, at])
+
+    def one(head, carry):
+        _, _, q_b = head_of(
+            proj_ref, columns_of(0, head, heads), gq_ref[...], cos_ref[...], sin_ref[...]
+        )
+        _, _, k_b = head_of(
+            proj_ref, columns_of(1, head, heads), gk_ref[...], cos_ref[...], sin_ref[...]
+        )
+        v_b = proj_ref[:, columns_of(2, head, heads)].astype(BF)
+        for i in range(seq_len // block):
+            rows = slice(i * block, (i + 1) * block)
+            probs = softmax_rows(q_b[rows], k_b, dc_ref[rows, :], dr_ref[...])
+            ob_ref[rows, columns_of(0, head, heads)] = dot32(probs.astype(BF), v_b).astype(BF)
+        return carry
+
+    lax.fori_loop(0, heads // 2, one, 0)
+    next(ring)
+    lax.fori_loop(heads // 2, heads, one, 0)
+    loads[1].wait()
+    swaps = []
+    for k in range(1, reps):
+        for i in range(width // 512):
+            at = pl.ds(i * 512, 512)
+            give[k - 1, :, at] = dot32(ob_ref[pl.ds(k * tok, tok), :], wo[:, at]).astype(BF)
+        c = pltpu.make_async_remote_copy(
+            src_ref=give.at[k - 1],
+            dst_ref=came.at[k - 1],
+            send_sem=rep_sem.at[0, k - 1],
+            recv_sem=rep_sem.at[1, k - 1],
+            device_id={"rep": (rep + k) % reps},
+            device_id_type=MESH,
+        )
+        c.start()
+        swaps.append(c)
+    for i in range(width // 512):
+        at = pl.ds(i * 512, 512)
+        mid_ref[:, at] = dot32(ob_ref[pl.ds(0, tok), :], wo[:, at])
+    next(ring)
+    for c in swaps:
+        c.wait()
+
+    def second(i, carry):
+        rows = pl.ds(pl.multiple_of(i * 64, 64), 64)
+        v = seq_ref[rows, :].astype(F32) + mid_ref[rows, :]
+        for k in range(1, reps):
+            v = v + came[k - 1, rows, :].astype(F32)
+        mid_ref[rows, :] = v
+        v = v * lax.rsqrt(jnp.mean(v * v, axis=-1, keepdims=True) + epsilon)
+        h2_ref[rows, :] = (v * gf_ref[...]).astype(BF)
+        return carry
+
+    lax.fori_loop(0, tok // 64, second, 0)
+    loads[2].wait()
+    hops.turn(ring)
+
+
+def attention(chips, reps, cot, seq, ga, gf, gq, gk, cosine, sine, docs, w_qkv, w_out, collective_id):
+    seq_len, width = seq.shape
+    tok = cot.shape[0]
+    heads = w_out.shape[0] // HD
+    anywhere = pl.BlockSpec(memory_space=pl.ANY)
     vmem = pl.BlockSpec(memory_space=pltpu.VMEM)
     return pl.pallas_call(
-        functools.partial(qkv_gradient_kernel, chips),
-        out_shape=jax.ShapeDtypeStruct((shard, width), BF),
-        in_specs=[vmem, vmem],
-        out_specs=vmem,
-        scratch_shapes=[*scatter_scratch(chips, shard, width), *ring_sems(chips)],
+        functools.partial(attention_kernel, chips, reps, heads),
+        out_shape=(
+            jax.ShapeDtypeStruct((2 * chips, tok, width), BF),
+            jax.ShapeDtypeStruct((seq_len, width), BF),
+            jax.ShapeDtypeStruct((seq_len, 3 * heads * HD), F32),
+            jax.ShapeDtypeStruct((seq_len, heads * HD), BF),
+            jax.ShapeDtypeStruct((tok, width), F32),
+            jax.ShapeDtypeStruct((tok, width), BF),
+        ),
+        in_specs=[anywhere] + [vmem] * 9 + [anywhere] * 2,
+        out_specs=(anywhere,) + (vmem,) * 5,
+        scratch_shapes=[
+            pltpu.VMEM(w_qkv.shape, BF),
+            pltpu.VMEM(w_out.shape, BF),
+            pltpu.VMEM((reps - 1, tok, width), BF),
+            pltpu.VMEM((reps - 1, tok, width), BF),
+            *ring_sems(chips),
+            DMA((2, reps - 1)),
+            DMA((3,)),
+        ],
         compiler_params=pltpu.CompilerParams(
             collective_id=collective_id, has_side_effects=True, vmem_limit_bytes=VMEM_LIMIT
         ),
         cost_estimate=pl.CostEstimate(
-            flops=2 * h1_t.size * width, transcendentals=0, bytes_accessed=200 << 20
-        ),
-        name="qkv_gradient",
-    )(h1_t, grad)
-
-
-def gather_kernel(chips, own_ref, all_ref, up, down, side, local):
-    hops = Hops(chips)
-    hops.meet()
-    mine = pltpu.make_async_copy(own_ref, all_ref.at[hops.me], local)
-    mine.start()
-    hops.gather(own_ref, lambda dev: all_ref.at[dev], up, down, side, lambda d: None)
-    mine.wait()
+            flops=2 * seq_len * w_qkv.size, transcendentals=0, bytes_accessed=100 << 20
+        ),
+        name="attention",
+    )(cot, seq, ga, gf, gq, gk, cosine, sine, docs[:, None], docs[None, :], w_qkv, w_out)
+
+
+def attention_back_kernel(
+    heads,
+    proj_ref, mid_ref, wo_ref, gq_ref, gk_ref, cos_ref, sin_ref, dc_ref, dr_ref,
+    grad_ref, qt_ref, kt_ref,
+    dob, dk, dv,
+):
+    seq_len = proj_ref.shape[0]
+    block = min(256, seq_len)
+    scale = HD ** (-0.5)
+    for i in range(heads * HD // 512):
+        at = pl.ds(i * 512, 512)
+        dob[:, at] = dot_nt(mid_ref[...], wo_ref[at, :]).astype(BF)
+    qt_ref[...] = jnp.zeros_like(qt_ref)
+    kt_ref[...] = jnp.zeros_like(kt_ref)
+
+    def unturned(grad, hat, inverse, gain, rows):
+        grad = turned(grad, cos_ref[rows, :], -sin_ref[rows, :])
+        scaled = grad * gain
+        pre = inverse * (scaled - hat * jnp.mean(scaled * hat, axis=-1, keepdims=True))
+        return pre.astype(BF), jnp.sum(grad * hat, axis=0, keepdims=True)
+
+    def one(head, carry):
+        q_at, k_at, v_at = (columns_of(b, head, heads) for b in range(3))
+        q_hat, q_inv, q_b = head_of(proj_ref, q_at, gq_ref[...], cos_ref[...], sin_ref[...])
+        k_hat, k_inv, k_b = head_of(proj_ref, k_at, gk_ref[...], cos_ref[...], sin_ref[...])
+        v_b = proj_ref[:, v_at].astype(BF)
+        for i in range(seq_len // block):
+            rows = slice(i * block, (i + 1) * block)
+            probs = softmax_rows(q_b[rows], k_b, dc_ref[rows, :], dr_ref[...])
+            grad_o = dob[rows, columns_of(0, head, heads)]
+            grad_p = dot_nt(grad_o, v_b)
+            grad_s = (
+                probs * (grad_p - jnp.sum(probs * grad_p, axis=-1, keepdims=True))
+            ).astype(BF)
+            dv_part = dot_tn(probs.astype(BF), grad_o)
+            dk_part = dot_tn(grad_s, q_b[rows])
+            if i == 0:
+                dv[...] = dv_part
+                dk[...] = dk_part
+            else:
+                dv[...] += dv_part
+                dk[...] += dk_part
+            pre, terms = unturned(
+                dot32(grad_s, k_b) * scale, q_hat[rows], q_inv[rows], gq_ref[...], rows
+            )
+            grad_ref[rows, q_at] = pre
+            qt_ref[...] += terms
+        pre, terms = unturned(dk[...] * scale, k_hat, k_inv, gk_ref[...], slice(0, seq_len))
+        grad_ref[:, k_at] = pre
+        kt_ref[...] += terms
+        grad_ref[:, v_at] = dv[...].astype(BF)
+        return carry
+
+    lax.fori_loop(0, heads, one, 0)
+
+
+def attention_back(proj, mid, w_out, gq, gk, cosine, sine, docs):
+    seq_len = proj.shape[0]
+    heads = w_out.shape[0] // HD
+    vmem = pl.BlockSpec(memory_space=pltpu.VMEM)
+    return pl.pallas_call(
+        functools.partial(attention_back_kernel, heads),
+        out_shape=(
+            jax.ShapeDtypeStruct(proj.shape, BF),
+            jax.ShapeDtypeStruct((1, HD), F32),
+            jax.ShapeDtypeStruct((1, HD), F32),
+        ),
+        in_specs=[vmem] * 9,
+        out_specs=(vmem,) * 3,
+        scratch_shapes=[
+            pltpu.VMEM((seq_len, heads * HD), BF),
+            pltpu.VMEM((seq_len, HD), F32),
+            pltpu.VMEM((seq_len, HD), F32),
+        ],
+        compiler_params=pltpu.CompilerParams(vmem_limit_bytes=VMEM_LIMIT),
+        cost_estimate=pl.CostEstimate(
+            flops=20 * heads * seq_len * seq_len * HD, transcendentals=0, bytes_accessed=20 << 20
+        ),
+        name="attention_back",
+    )(proj, mid, w_out, gq, gk, cosine, sine, docs[:, None], docs[None, :])
 
 
 def ring_sems(chips):
     return [DMA((2, chips // 2)), DMA((2, chips // 2)), DMA((2, chips))]
 
 
-def ring_gather(chips, own, collective_id, name):
+def dense_gradients_kernel(
+    chips, split_out, h1_ref, grad_ref, ob_ref, mid_ref, gains_ref, qkv_ref, out_ref, gain_ref, *scratch
+):
+    hops = Hops(chips)
+    scratches = [scratch[9 * i : 9 * i + 9] for i in range(3)]
+    hops.meet()
+
+    first = hops.core == 0
+
+    def product(left_ref, right_ref, rows, width):
+        def produce(d, same_ref, other_ref):
+            columns = pl.ds(pl.multiple_of(2 * rows * hops.chip(d), 2 * rows), 2 * rows)
+            left = left_ref[:, columns]
+
+            def block(at):
+                value = dot_tn(left, right_ref[:, at])
+                low, high = value[:rows], value[rows:]
+                same_ref[:, at] = jnp.where(first, low, high)
+                other_ref[:, at] = jnp.where(first, high, low).astype(BF)
+
+            tiles(width // 512, 512, block)
+
+        return produce
+
+    def small(d, same_ref, other_ref):
+        dev = hops.device(d)
+        same_ref[...] = gains_ref[dev]
+        other_ref[...] = gains_ref[dev + 1 - 2 * hops.core].astype(BF)
+
+    def into(ref):
+        def finish(value, at):
+            ref[at, :] = value.astype(ref.dtype)
+
+        return finish
+
+    def ring(produce, ref, bufs):
+        return hops.scatter(ref.shape[0], produce, *bufs, into(ref))
+
+    rings = [ring(product(h1_ref, grad_ref, *qkv_ref.shape), qkv_ref, scratches[0])]
+    if split_out:
+        rings.append(ring(product(ob_ref, mid_ref, *out_ref.shape), out_ref, scratches[1]))
+    rings.append(ring(small, gain_ref, scratches[2]))
+    hops.turn(*rings)
+
+
+def dense_gradients(chips, split_out, h1, grad, ob, mid, gain_blocks, collective_id):
+    shard = h1.shape[1] // (2 * chips)
+    width = grad.shape[1]
+    half = ob.shape[1] // (2 * chips) if split_out else 32
+    vmem = pl.BlockSpec(memory_space=pltpu.VMEM)
+    shapes = ((shard, width), (half, D), gain_blocks.shape[1:])
+    scratch = []
+    for rows, columns in shapes:
+        scratch += [*scatter_scratch(chips, rows, columns), *ring_sems(chips)]
+    return pl.pallas_call(
+        functools.partial(dense_gradients_kernel, chips, split_out),
+        out_shape=tuple(
+            jax.ShapeDtypeStruct(shape, kind)
+            for shape, kind in zip(shapes, (BF, BF, F32), strict=True)
+        ),
+        in_specs=[vmem] * 5,
+        out_specs=(vmem,) * 3,
+        scratch_shapes=scratch,
+        compiler_params=pltpu.CompilerParams(
+            collective_id=collective_id, has_side_effects=True, vmem_limit_bytes=VMEM_LIMIT
+        ),
+        cost_estimate=pl.CostEstimate(
+            flops=2 * h1.size * width, transcendentals=0, bytes_accessed=200 << 20
+        ),
+        name="dense_gradients",
+    )(h1, grad, ob, mid, gain_blocks)
+
+
+def start_kernel(
+    chips, reps, heads, split_out,
+    tok_ref, small_ref, wq_ref, wo_ref,
+    seq_ref, smalls_ref, full_ref, out_ref,
+    own_q, own_o, *sems,
+):
+    hops = Hops(chips)
+    rep = lax.axis_index("rep")
+    up, down, side, up_s, down_s, side_s, up_o, down_o, side_o, rep_sem, col_sem, own_sem, half_sem = sems
+    pieces = []
+    for i in range(3 * heads):
+        q, j = i // heads, i % heads
+        at = pl.multiple_of(((q * heads + j) * reps + rep) * HD, HD)
+        pieces.append(
+            pltpu.make_async_copy(
+                wq_ref.at[:, pl.ds(at, HD)], own_q.at[:, pl.ds(i * HD, HD)], col_sem.at[i]
+            )
+        )
+        pieces[-1].start()
+    hops.meet(reps)
+    swaps = []
+    for k in range(1, reps):
+        c = pltpu.make_async_remote_copy(
+            src_ref=tok_ref,
+            dst_ref=seq_ref.at[reps - k],
+            send_sem=rep_sem.at[0, reps - k],
+            recv_sem=rep_sem.at[1, reps - k],
+            device_id={"rep": (rep + k) % reps},
+            device_id_type=MESH,
+        )
+        c.start()
+        swaps.append(c)
+    locals_ = [
+        pltpu.make_async_copy(tok_ref, seq_ref.at[0], own_sem.at[0]),
+        pltpu.make_async_copy(small_ref, smalls_ref.at[hops.me], own_sem.at[1]),
+    ]
+    for c in locals_:
+        c.start()
+    for c in pieces:
+        c.wait()
+    mine = pltpu.make_async_copy(own_q, full_ref.at[hops.me], own_sem.at[2])
+    mine.start()
+    items = [
+        (own_q, lambda dev: full_ref.at[dev], up, down, side),
+        (small_ref, lambda dev: smalls_ref.at[dev], up_s, down_s, side_s),
+    ]
+    if split_out:
+        rows = own_o.shape[0]
+        kept = wo_ref.at[pl.ds(pl.multiple_of(hops.core * rows, rows), rows)]
+        given = wo_ref.at[pl.ds(pl.multiple_of((1 - hops.core) * rows, rows), rows)]
+        give = hops.copy(given, own_o, half_sem.at[0], half_sem.at[1], hops.flip)
+
+        @pl.when(hops.core == rep)
+        def _():
+            give.start()
+            keep = pltpu.make_async_copy(kept, own_o, half_sem.at[2])
+            keep.start()
+            keep.wait()
+            give.wait_send()
+
+        @pl.when(hops.core != rep)
+        def _():
+            give.wait_recv()
+
+        def slot(dev):
+            return out_ref.at[dev // 2, pl.ds(pl.multiple_of(dev % 2 * rows, rows), rows)]
+
+        mine_o = pltpu.make_async_copy(own_o, slot(hops.me), half_sem.at[3])
+        mine_o.start()
+        items.append((own_o, slot, up_o, down_o, side_o))
+    hops.turn(hops.gather(items, lambda d: None))
+    for c in locals_:
+        c.wait()
+    mine.wait()
+    if split_out:
+        mine_o.wait()
+    for c in swaps:
+        c.wait()
+
+
+def start(chips, reps, heads, split_out, tok, small, w_qkv, w_out, collective_id):
     anywhere = pl.BlockSpec(memory_space=pl.ANY)
+    vmem = pl.BlockSpec(memory_space=pltpu.VMEM)
+    shard, wide = w_qkv.shape[0], 3 * heads * HD
+    half = w_out.shape[0] // 2
     return pl.pallas_call(
-        functools.partial(gather_kernel, chips),
-        out_shape=jax.ShapeDtypeStruct((2 * chips, *own.shape), own.dtype),
-        in_specs=[anywhere],
-        out_specs=anywhere,
-        scratch_shapes=[*ring_sems(chips), DMA],
+        functools.partial(start_kernel, chips, reps, heads, split_out),
+        out_shape=(
+            jax.ShapeDtypeStruct((reps, *tok.shape), BF),
+            jax.ShapeDtypeStruct((2 * chips, *small.shape), F32),
+            jax.ShapeDtypeStruct((2 * chips, shard, wide), BF),
+            jax.ShapeDtypeStruct((chips, 2 * half, D), BF),
+        ),
+        in_specs=[vmem, vmem, anywhere, anywhere],
+        out_specs=(anywhere,) * 4,
+        scratch_shapes=[
+            pltpu.VMEM((shard, wide), BF),
+            pltpu.VMEM((half, D), BF),
+            *ring_sems(chips),
+            *ring_sems(chips),
+            *ring_sems(chips),
+            DMA((2, max(reps, 2))),
+            DMA((3 * heads,)),
+            DMA((3,)),
+            DMA((4,)),
+        ],
         compiler_params=pltpu.CompilerParams(collective_id=collective_id, has_side_effects=True),
         cost_estimate=pl.CostEstimate(
-            flops=0, transcendentals=0, bytes_accessed=4 * chips * own.size * own.dtype.itemsize
-        ),
-        name=name,
-    )(own)
-
-
-def out_gradient(ring, grad, reps, heads, rel, rep, grp):
-    if reps != 2 or heads != ring.chips:
-        whole = lax.dynamic_update_slice(
-            jnp.zeros((heads, reps, HD, D), BF), grad.reshape(heads, 1, HD, D), (0, rep, 0, 0)
-        ).reshape(D, D)
-        part = lax.psum_scatter(whole, "grp", scatter_dimension=0, tiled=True)
-        return lax.psum(part, "rep").astype(F32)
+            flops=0, transcendentals=0, bytes_accessed=200 << 20
+        ),
+        name="start",
+    )(tok, small, w_qkv, w_out)
+
+
+def out_rows(ring, half, rep, grp):
     n = ring.devices
-    owners = [(r, 2 * chip + r) for r in range(2) for chip in range(ring.chips)]
-
-    def send(v, where):
-        pairs = []
-        for r, dev in owners:
-            src, dst = where(r, dev)
-            pairs.append((src[0] * n + src[1], dst[0] * n + dst[1]))
-        return lax.ppermute(v, ("rep", "grp"), pairs)
-
-    def hop(v, shift):
-        def to(r, dev):
-            chip = ring.cycle[(ring.place[dev // 2] + shift) % ring.chips]
-            return (r, dev), (r, 2 * chip + r)
-
-        return send(v, to)
-
-    other = send(grad, lambda r, dev: ((r, dev ^ 1), (r, dev)))
-    both = (grad.astype(F32) + other.astype(F32)).reshape(heads, HD, D)
-
-    def block(d):
-        return lax.dynamic_index_in_dim(both, rel[d, 0] // 2, 0, False)
-
-    far = block(ring.half).astype(BF)
-    rows = HD // 2
-    up, down = hop(far[:rows], 1), hop(far[rows:], -1)
-    zero = jnp.zeros_like(up)
-    up = jnp.concatenate([up, zero], axis=0)
-    down = jnp.concatenate([zero, down], axis=0)
-    for step in range(ring.half - 1, 0, -1):
-        up = hop((block(step) + up.astype(F32)).astype(BF), 1)
-        down = hop((block(-step % ring.chips) + down.astype(F32)).astype(BF), -1)
-    total = (block(0) + up.astype(F32) + down.astype(F32)).astype(BF)
-    mine = send(total, lambda r, dev: ((r, dev), (1 - r, dev)))
-    return jnp.where(grp % 2 == rep, total, mine).astype(F32)
+
+    def send(pairs):
+        pairs = [(a * n + b, c * n + d) for (a, b), (c, d) in pairs]
+        return lax.ppermute(half, ("rep", "grp"), pairs)
+
+    chips = range(ring.chips)
+    mate = send([((r, 2 * j + 1 - r), (r, 2 * j + r)) for r in range(2) for j in chips])
+    across = [
+        send([((r, 2 * j + c), (1 - r, 2 * j + r)) for r in range(2) for j in chips])
+        for c in range(2)
+    ]
+    core = grp % 2
+    first = jnp.where(core == rep, jnp.where(core == 0, half, mate), across[0])
+    second = jnp.where(core == rep, jnp.where(core == 0, mate, half), across[1])
+    return jnp.concatenate([first, second], axis=0).astype(F32)
 
 
 def per_device(
@@ -677,7 +1005,6 @@
     seq_len = segment_ids.shape[1]
     heads = HEADS // reps
     wide = heads * HD
-    score_scale = HD ** (-0.5)
 
     def from_rep(v, k):
         return lax.ppermute(v, "rep", [((s + k) % reps, s) for s in range(reps)])
@@ -696,72 +1023,69 @@
         return out
 
     own_b = tokens[0]
-    seq_b = rep_gather(own_b)
     gates_f = gate_weights[0]
     experts = jnp.arange(groups, dtype=jnp.int32)
     weight_of = jnp.sum(
         jnp.where(routes[0][None] == experts[:, None, None], gates_f[None], 0.0), axis=-1
     )
+    gain_rows = -(-gains.shape[0] // tok_rows)
+    small_rows = -(-(groups + gain_rows) // 16) * 16
     small = jnp.concatenate(
         [
             weight_of,
-            jnp.broadcast_to(gains.astype(F32)[None], (groups, gains.shape[0])),
+            jnp.pad(gains.astype(F32), (0, gain_rows * tok_rows - gains.shape[0])).reshape(
+                gain_rows, tok_rows
+            ),
+            jnp.zeros((small_rows - groups - gain_rows, tok_rows), F32),
         ],
-        axis=1,
-    )
-    small = lax.all_to_all(small, "grp", split_axis=0, concat_axis=0, tiled=True)
-    gains_f = small[:, tok_rows:].reshape(-1)
-    weight_in = small[:, :tok_rows]
+        axis=0,
+    )
+    split_out = reps == 2 and heads == ring.chips
+    seq_b, smalls, full_qkv, my_out = start(
+        ring.chips, reps, heads, split_out, own_b, small, w_qkv, w_out, 1
+    )
+    seq_b = seq_b.reshape(seq_len, D)
+    shard = full_qkv.shape[1]
+    full_qkv = full_qkv.reshape(D, 3 * wide)
+    if not split_out:
+        my_out = lax.all_gather(w_out, "grp", axis=0, tiled=True)
+        my_out = lax.dynamic_index_in_dim(
+            my_out.reshape(heads, reps, HD, D), rep, axis=1, keepdims=False
+        )
+    my_out = my_out.reshape(wide, D)
+    gains_f = smalls[:, groups : groups + gain_rows].reshape(groups, -1)
+    gains_f = gains_f[:, : gains.shape[0]].reshape(-1)
+    weight_in = lax.dynamic_index_in_dim(smalls, grp, 1, False)
     g_attn = gains_f[:D]
     g_ffn = gains_f[D : 2 * D]
     g_query = gains_f[2 * D : 2 * D + HD]
     g_key = gains_f[2 * D + HD :]
 
-    my_qkv = lax.dynamic_index_in_dim(
-        w_qkv.reshape(w_qkv.shape[0], 3, heads, reps, HD), rep, axis=3, keepdims=False
-    ).reshape(w_qkv.shape[0], 3 * wide)
-    shard = my_qkv.shape[0]
-    full_qkv = ring_gather(ring.chips, my_qkv, 1, "gather_qkv").reshape(D, 3 * wide)
-    full_out = lax.all_gather(w_out, "grp", axis=0, tiled=True)
-    my_out = lax.dynamic_index_in_dim(
-        full_out.reshape(heads, reps, HD, D), rep, axis=1, keepdims=False
-    ).reshape(wide, D)
-
-    cot_late, full_qkv = lax.optimization_barrier((cotangent[0], full_qkv))
-    dy_all = lax.all_gather(cot_late, "grp", axis=0, tiled=False)
-
-    seq_f = seq_b.astype(F32)
-    normed_one, hat_one, inv_one = rms_forward(seq_f, g_attn)
-    h1_b = normed_one.astype(BF)
-    projected = dot32(h1_b, full_qkv)
-    q_pre = projected[:, :wide].reshape(seq_len, heads, HD)
-    k_pre = projected[:, wide : 2 * wide].reshape(seq_len, heads, HD)
-    v_pre = projected[:, 2 * wide :]
-    q_normed, q_hat, q_inv = rms_forward(q_pre, g_query)
-    k_normed, k_hat, k_inv = rms_forward(k_pre, g_key)
     order = jnp.concatenate(
         [((rep + k) % reps) * tok_rows + jnp.arange(tok_rows, dtype=jnp.int32) for k in range(reps)]
     )
-    positions = order.astype(F32)
-    q_b = rotate(q_normed, positions, 1.0).astype(BF)
-    k_b = rotate(k_normed, positions, 1.0).astype(BF)
-    v_b = v_pre.astype(BF).reshape(seq_len, heads, HD)
+    frequency = rope_base ** (-2.0 * jnp.arange(HD // 2, dtype=F32) / HD)
+    angles = order.astype(F32)[:, None] * frequency[None, :]
+    cosine = jnp.concatenate([jnp.cos(angles)] * 2, axis=1)
+    sine = jnp.concatenate([-jnp.sin(angles), jnp.sin(angles)], axis=1)
     docs = segment_ids[0][order]
-    same_doc = (docs[:, None] == docs[None, :])[None]
-    scores = jnp.where(
-        same_doc,
-        jnp.einsum("qhd,khd->hqk", q_b, k_b, preferred_element_type=F32) * score_scale,
-        -1e30,
-    )
-    row_max = jnp.max(scores, axis=-1, keepdims=True)
-    log_total = row_max + jnp.log(jnp.sum(jnp.exp(scores - row_max), axis=-1, keepdims=True))
-    probs_f = jnp.exp(scores - log_total)
-    probs_b = probs_f.astype(BF)
-    attended = jnp.einsum("hqk,khd->qhd", probs_b, v_b, preferred_element_type=F32)
-    attended_b = attended.reshape(seq_len, wide).astype(BF)
-    mid_rows = own_b.astype(F32) + rep_scatter(dot32(attended_b, my_out))
-    normed_two, hat_two, inv_two = rms_forward(mid_rows, g_ffn)
-    h2_b = normed_two.astype(BF)
+    g_query, g_key = g_query[None], g_key[None]
+    dy_all, h1_b, projected, attended_b, mid_rows, h2_b = attention(
+        ring.chips,
+        reps,
+        cotangent[0],
+        seq_b,
+        g_attn[None],
+        g_ffn[None],
+        g_query,
+        g_key,
+        cosine,
+        sine,
+        docs,
+        full_qkv,
+        my_out,
+        5,
+    )
 
     chips = ring.chips
     entries = tok_rows * TOP
@@ -775,7 +1099,32 @@
     rows_in, grads_in, acts, grad_gates, grad_ups = expert_rows(
         chips, capacity, h2_b, dy_all, slot, weight_in, w_gate[0], w_up[0], w_down[0], 2
     )
+    all_rows = rows_in.reshape(-1, D)
+    all_grads = grads_in.reshape(-1, D)
+    all_acts = acts.reshape(groups * capacity, -1)
+    all_gates = grad_gates.reshape(groups * capacity, -1)
+    all_ups = grad_ups.reshape(groups * capacity, -1)
+
+    def rep_send(v):
+        v = v.astype(BF)
+        came = [[] for _ in range(1, reps)]
+        for part in jnp.split(v, 2):
+            for k in range(1, reps):
+                came[k - 1].append(from_rep(part, k))
+        return v, came
+
+    def rep_sum(sent, after):
+        (v, came), _ = lax.optimization_barrier((sent, after))
+        return v.astype(F32) + sum(jnp.concatenate(c, axis=0).astype(F32) for c in came)
+
+    grad_wdown = rep_send(jnp.einsum("rf,rd->fd", all_acts, all_grads, preferred_element_type=F32))
+    grad_wgate = rep_send(jnp.einsum("rd,rf->df", all_rows, all_gates, preferred_element_type=F32))
+    grad_wup = rep_send(jnp.einsum("rd,rf->df", all_rows, all_ups, preferred_element_type=F32))
+
     cuts = 1 if chips <= 8 else chips // 8
+    (grad_gates, grad_ups), _ = lax.optimization_barrier(
+        ((grad_gates, grad_ups), (grad_wdown[0], grad_wgate[0], grad_wup[0]))
+    )
     grad_h2 = jnp.concatenate(
         [
             rows_back(chips, capacity, grad_gates, grad_ups, slot[:, :, None], wg, wu, 8 + i)
@@ -786,76 +1135,60 @@
         axis=1,
     )
 
+
+    grad_out = cotangent[0].astype(F32)
+    _, hat_two, inv_two = rms_forward(mid_rows, g_ffn)
+    grad_mid_norm, ffn_terms = rms_backward(grad_h2, hat_two, inv_two, g_ffn)
+    grad_mid = grad_out + grad_mid_norm
+    grad_mid_b = grad_mid.astype(BF)
     pick = (slot[:, None, :] == jnp.arange(capacity, dtype=jnp.int32)[None, :, None]).astype(BF)
     row_weight = jnp.sum(pick.astype(F32) * weight_in[:, None, :], axis=-1)
-    all_rows = rows_in.reshape(-1, D)
-    all_grads = grads_in.reshape(-1, D)
-    all_acts = acts.reshape(groups * capacity, -1)
-    all_gates = grad_gates.reshape(groups * capacity, -1)
-    all_ups = grad_ups.reshape(groups * capacity, -1)
-    eout = dot32(all_acts, w_down[0]).astype(BF).astype(F32)
+    acts_late, _ = lax.optimization_barrier((all_acts, grad_mid_b))
+    eout = dot32(acts_late, w_down[0]).astype(BF).astype(F32)
     eout = (row_weight.reshape(-1, 1) * eout).astype(BF).reshape(groups, capacity, D)
     out_all = jnp.einsum("gct,gcd->gtd", pick, eout, preferred_element_type=F32).astype(BF)
     out_sum = lax.psum_scatter(
         out_all.reshape(groups * tok_rows, D), "grp", scatter_dimension=0, tiled=True
     )
 
-    def rep_send(v):
-        v = v.astype(BF)
-        return [v] + [from_rep(v, k) for k in range(1, reps)]
-
-    def rep_sum(parts, after):
-        parts, _ = lax.optimization_barrier((parts, after))
-        out = parts[0].astype(F32)
-        for part in parts[1:]:
-            out = out + part.astype(F32)
-        return out
-
-    grad_wdown = rep_send(jnp.einsum("rf,rd->fd", all_acts, all_grads, preferred_element_type=F32))
-    grad_wgate = rep_send(jnp.einsum("rd,rf->df", all_rows, all_gates, preferred_element_type=F32))
-    grad_wup = rep_send(jnp.einsum("rd,rf->df", all_rows, all_ups, preferred_element_type=F32))
-
-    grad_out = cotangent[0].astype(F32)
-    grad_mid_norm, ffn_terms = rms_backward(grad_h2, hat_two, inv_two, g_ffn)
-    grad_mid = grad_out + grad_mid_norm
-    grad_branch_b = rep_gather(grad_mid.astype(BF))
-    grad_wout = jnp.einsum("td,te->de", attended_b, grad_branch_b, preferred_element_type=F32)
-    grad_attn_b = (
-        jnp.einsum("te,de->td", grad_branch_b, my_out, preferred_element_type=F32)
-        .astype(BF)
-        .reshape(seq_len, heads, HD)
-    )
-    grad_probs = jnp.einsum("qhd,khd->hqk", grad_attn_b, v_b, preferred_element_type=F32)
-    grad_vals = jnp.einsum("hqk,qhd->khd", probs_b, grad_attn_b, preferred_element_type=F32)
-    grad_scores = (
-        probs_f * (grad_probs - jnp.sum(probs_f * grad_probs, axis=-1, keepdims=True))
-    ).astype(BF)
-    grad_q = jnp.einsum("hqk,khd->qhd", grad_scores, k_b, preferred_element_type=F32) * score_scale
-    grad_k = jnp.einsum("hqk,qhd->khd", grad_scores, q_b, preferred_element_type=F32) * score_scale
-    grad_qn = rotate(grad_q, positions, -1.0)
-    grad_kn = rotate(grad_k, positions, -1.0)
-    grad_q_pre, query_terms = rms_backward(grad_qn, q_hat, q_inv, g_query)
-    grad_k_pre, key_terms = rms_backward(grad_kn, k_hat, k_inv, g_key)
-    grad_proj = jnp.concatenate(
+    grad_branch_b = rep_gather(grad_mid_b)
+    grad_proj, query_terms, key_terms = attention_back(
+        projected, grad_branch_b, my_out, g_query, g_key, cosine, sine, docs
+    )
+    _, hat_one, inv_one = rms_forward(seq_b.astype(F32), g_attn)
+    grad_h1_part = jnp.einsum("te,de->td", grad_proj, full_qkv, preferred_element_type=F32)
+    attn_terms = grad_h1_part * hat_one
+    grad_h1 = rep_scatter(grad_h1_part)
+    grad_rows_one, _ = rms_backward(grad_h1, hat_one[:tok_rows], inv_one[:tok_rows], g_attn)
+    grad_tokens = grad_mid + grad_rows_one
+    grad_gains = jnp.concatenate(
         [
-            grad_q_pre.reshape(seq_len, wide),
-            grad_k_pre.reshape(seq_len, wide),
-            grad_vals.reshape(seq_len, wide),
-        ],
-        axis=1,
-    ).astype(BF)
-    grad_h1 = rep_scatter(
-        jnp.einsum("te,de->td", grad_proj, full_qkv, preferred_element_type=F32)
-    )
-    grad_rows_one, attn_terms = rms_backward(
-        grad_h1, hat_one[:tok_rows], inv_one[:tok_rows], g_attn
-    )
-    grad_tokens = grad_mid + grad_rows_one
-
-    h1_t = h1_b.T.reshape(chips, 2, shard, seq_len)
-    h1_t = jnp.where(grp % 2 == 0, h1_t, h1_t[:, ::-1]).reshape(D, seq_len)
-    shard_qkv = qkv_gradient(chips, h1_t, grad_proj, 4)
-    grad_wdown = rep_sum(grad_wdown, grad_proj)
+            jnp.sum(attn_terms, axis=0),
+            jnp.sum(ffn_terms, axis=0),
+            query_terms[0],
+            key_terms[0],
+        ]
+    )
+
+    grad_wdown = rep_sum(grad_wdown, grad_h2)
+    (grad_proj, grad_wdown), _ = lax.optimization_barrier(
+        ((grad_proj, grad_wdown), grad_h1_part)
+    )
+    gain_size = gains.shape[0]
+    gain_blocks = jnp.pad(
+        grad_gains.reshape(groups, gain_size), ((0, 0), (0, 4096 - gain_size))
+    ).reshape(groups, 32, 128)
+    shard_qkv, half_out, total = dense_gradients(
+        chips,
+        split_out,
+        h1_b,
+        grad_proj,
+        attended_b,
+        grad_branch_b,
+        gain_blocks,
+        4,
+    )
+    total = total.reshape(-1)[:gain_size]
     qkv_all = [shard_qkv] + [from_rep(shard_qkv, k) for k in range(1, reps)]
     columns = jnp.stack(qkv_all, axis=0).reshape(reps, shard, 3, heads, HD)
     columns = columns[(jnp.arange(reps) - rep) % reps]
@@ -865,23 +1198,21 @@
     grad_wup = rep_sum(grad_wup, shard_qkv)
     result = mid_rows + lax.optimization_barrier((out_sum, shard_qkv))[0].astype(F32)
 
-    shard_out = out_gradient(ring, grad_wout.astype(BF), reps, heads, rel, rep, grp)
-
-    grad_gains = jnp.concatenate(
-        [
-            jnp.sum(attn_terms, axis=0),
-            jnp.sum(ffn_terms, axis=0),
-            jnp.sum(query_terms, axis=(0, 1)),
-            jnp.sum(key_terms, axis=(0, 1)),
-        ]
-    )
-    pieces = lax.all_to_all(
-        grad_gains.reshape(groups, -1), "grp", split_axis=0, concat_axis=0, tiled=True
-    )
-    shard_gains = jnp.sum(pieces, axis=0)
-    total = shard_gains
+    if split_out:
+        shard_out = out_rows(ring, half_out, rep, grp)
+    else:
+        grad_wout = dot_tn(attended_b, grad_branch_b)
+        whole = lax.dynamic_update_slice(
+            jnp.zeros((heads, reps, HD, D), BF),
+            grad_wout.astype(BF).reshape(heads, 1, HD, D),
+            (0, rep, 0, 0),
+        ).reshape(D, D)
+        shard_out = lax.psum(
+            lax.psum_scatter(whole, "grp", scatter_dimension=0, tiled=True), "rep"
+        ).astype(F32)
+    own_gains = total
     for k in range(1, reps):
-        total = total + from_rep(shard_gains, k)
+        total = total + from_rep(own_gains, k)
     return (
         result[None],
         grad_tokens[None],

time: 947 us -> 945 us (level)
  starting transfers between devices: 47 us -> 148 us
  Pallas kernels: 442 us -> 542 us
  waiting for transfers between devices: 133 us -> 62.5 us
  other arithmetic: 99.9 us -> 46.5 us
  matrix products: 118 us -> 82.8 us
  local copies, waits for them, and re-layouts: 62.4 us -> 39.4 us
  between operations: 36.2 us -> 14.8 us
    ppermute x7 -> x9, starting transfers between devices: 6.12 us -> 140 us  [from_rep(): return lax.ppermute(v, 'rep', [((s + k) % reps, s) for s in range(reps)])]
    pallas_call x2 -> x4, Pallas kernels: 231 us -> 349 us  [the longest x1 125 us: dense_gradients(): pl.pallas_call(functools.partial(dense_gradients_kernel, chips, split_out...]
    dot_general x8 -> x0, matrix products: 32.4 us -> none  [the longest x1 6.8 us: per_device(): jnp.einsum('hqk,qhd->khd', probs_b, grad_attn_b, preferred_element_type=F32)]
    ppermute x7 -> x9, waiting for transfers between devices: 91.9 us -> 62.4 us  [from_rep(): return lax.ppermute(v, 'rep', [((s + k) % reps, s) for s in range(reps)])]
    ppermute x2 -> x1, waiting for transfers between devices: 25.5 us -> 0.01 us  [to_rep(): return lax.ppermute(v, 'rep', [(s, (s + k) % reps) for s in range(reps)])]
    ppermute x10 -> x3, starting transfers between devices: 31.9 us -> 6.88 us  [send(): return lax.ppermute(half, ('rep', 'grp'), pairs)]
    unnamed x173 -> x59, local copies, waits for them, and re-layouts: 21.4 us -> 1.29 us
    convert_element_type x11 -> x3, other arithmetic: 18.3 us -> 2.75 us  [the longest x1 1.67 us: per_device(): grad_mid_b = grad_mid.astype(BF)]
  transfers between devices with their start and end apart: 24 -> 14, of which waited for: 5 -> 4; matrix products, arithmetic and copies ran while one was open for 27% -> 8% of each run, Pallas kernels for 25% -> 17%
where the time goes in v3:
time: 945 us; the launch traced here: 936 us
  Pallas kernels  542 us (57%)
  starting transfers between devices  148 us (16%)
  matrix products  82.8 us (9%)
  waiting for transfers between devices  62.5 us (7%)
  other arithmetic  46.5 us (5%)
  local copies, waits for them, and re-layouts  39.4 us (4%)
  between operations  14.8 us (2%)
    ppermute x9, starting transfers between devices, from_rep(): return lax.ppermute(v, 'rep', [((s + k) % reps, s) for s in range(reps)])  140 us
    pallas_call x1, Pallas kernels, dense_gradients(): pl.pallas_call(functools.partial(dense_gradients_kernel, chips, split_out...  125 us
    pallas_call x1, Pallas kernels, rows_back(): pl.pallas_call(functools.partial(rows_back_kernel, chips, cap), out_shape...  97.9 us
    pallas_call x1, Pallas kernels, attention(): pl.pallas_call(functools.partial(attention_kernel, chips, reps, heads), o...  96.6 us
    pallas_call x1, Pallas kernels, expert_rows(): pl.pallas_call(functools.partial(experts_kernel, chips, cap), out_shape=(...  94.7 us
    pallas_call x1, Pallas kernels, start(): pl.pallas_call(functools.partial(start_kernel, chips, reps, heads, split_...  92.4 us
    ppermute x9, waiting for transfers between devices, from_rep(): return lax.ppermute(v, 'rep', [((s + k) % reps, s) for s in range(reps)])  62.4 us
    pallas_call x1, Pallas kernels, attention_back(): pl.pallas_call(functools.partial(attention_back_kernel, heads), out_shape...  35.4 us
  transfers between devices with their start and end apart: 14, of which 4 were waited for; matrix products, arithmetic and copies ran while one was open for 8% of the time, Pallas kernels for 17%

profile of v3, /device:TPU:0, one launch (start us, length us, event | category | flops | bytes accessed | tf_op | source)
XLA Modules:
  0.0 935.9 jit_solution(12729980210457507726)
XLA Ops:
  9.5 92.4 %start.1 = (bf16[2,256,2048]{2,1,0:T(8,128)(2,1)}, f32[16,32,256]{2,1,0:T(8,128)}, bf16[16,128,3072]{2,1,0:T(8,128)(2,1)}, bf16[8,128,2048]{2,1,0:T(8,128)(2,1)}) custom-call(bf16[256,2048]{1,0:T(8,128)(2,1)} %bitcast.100, f32[32,256]{1,0:T(8,128)} %maximum_maximum_fusion.small_ref, bf16[128,6144]{1,0:T(8,128)(2,1)} %wq_ref.1, bf16[128,2048]{1,0:T(8,128)(2,1)} %wo_ref.1), custom_call_target="tpu_custom_call" | custom-call | bytes 209715200 | tf_op jit(solution)/shard_map/start/pallas_call | solution.py:948
  104.1 0.9 constant_dynamic-slice_fusion
  105.3 1.0 fusion.5
  107.1 3.5 gather_fusion
  113.0 96.6 %attention.1 = (bf16[16,256,2048]{2,1,0:T(8,128)(2,1)}, bf16[512,2048]{1,0:T(8,128)(2,1)}, f32[512,3072]{1,0:T(8,128)}, bf16[512,1024]{1,0:T(8,128)(2,1)}, f32[2...) custom-call(bf16[256,2048]{1,0:T(8,128)(2,1)} %bitcast.96, bf16[512,2048]{1,0:T(8,128)(2,1)} %bitcast.99, f32[1,2048]{1,0:T(1,128)} %bitcast.108, ...), custom_call_target="tpu_custom_call" | custom-call | flops 6442450944 | bytes 104857600 | tf_op jit(solution)/shard_map/attention/pallas_call | solution.py:673
  209.6 94.7 %experts.1 = (bf16[8,288,2048]{2,1,0:T(8,128)(2,1)}, bf16[8,288,2048]{2,1,0:T(8,128)(2,1)}, bf16[8,288,1024]{2,1,0:T(8,128)(2,1)}, bf16[8,288,1024]{2,1,0:T(8,128)(2,1)}, bf16[8,288,1024]{2,1,0:T(8,128)(2,1)}) custom-call(bf16[256,2048]{1,0:T(8,128)(2,1)} %get-tuple-element.49.h2_ref, bf16[16,256,2048]{2,1,0:T(8,128)(2,1)} %get-tuple-element.50.dy_ref, ...), custom_call_target="tpu_custom_call" | custom-call | flops 28991029248 | bytes 209715200 | tf_op jit(solution)/shard_map/experts/pallas_call | solution.py:421
  304.4 16.0 %bitcast_convert_fusion = bf16[2048,1024]{1,0:T(8,128)(2,1)} fusion(bf16[8,288,2048]{2,1,0:T(8,128)(2,1)} %get-tuple-element.55, bf16[8,288,1024]{2,1,0:T(8,128)(2,1)} %get-tuple-element.57.du_ref), kind=kOutput, calls=%fused_computation.5 | convolution fusion | flops 9665773568 | bytes 18350080 | tf_op jit(solution)/shard_map/rd,rf->df/dot_general | solution.py:1122
  320.4 12.2 %bitcast_convert_fusion.1 = bf16[2048,1024]{1,0:T(8,128)(2,1)} fusion(bf16[8,288,2048]{2,1,0:T(8,128)(2,1)S(1)} %copy-done.19, bf16[8,288,1024]{2,1,0:T(8,128)(2,1)S(1)} %copy-done.20), kind=kOutput, calls=%fused_computation.6 | convolution fusion | flops 9665773568 | bytes 18350080 | tf_op jit(solution)/shard_map/rd,rf->df/dot_general | solution.py:1121
  332.6 12.3 %bitcast_convert_fusion.2 = bf16[1024,2048]{1,0:T(8,128)(2,1)} fusion(bf16[8,288,1024]{2,1,0:T(8,128)(2,1)S(1)} %bitcast.136, bf16[8,288,2048]{2,1,0:T(8,128)(2,1)S(1)} %bitcast.138), kind=kOutput, calls=%fused_computation.7 | convolution fusion | flops 9665773568 | bytes 18350080 | tf_op jit(solution)/shard_map/rf,rd->fd/dot_general | solution.py:1120
  345.0 2.0 copy.29.slot_ref
  347.2 97.9 %rows_back.1 = f32[256,2048]{1,0:T(8,128)} custom-call(bf16[8,288,1024]{2,1,0:T(8,128)(2,1)} %get-tuple-element.56.dg_ref, bf16[8,288,1024]{2,1,0:T(8,128)(2,1)} %get-tuple-element.57.du_ref, s32[16,256,1]{2,1,0:T(8,128)} %copy.29.slot_ref, bf16[2048,1024]{1,0:T(8,128)(2,1)} %bitcast.128, bf16[2048,1024]{1,0:T(8,128)(2,1)} %bitcast.130), custom_call_target="tpu_custom_call" | custom-call | flops 28991029248 | bytes 209715200 | tf_op jit(solution)/shard_map/rows_back/pallas_call | solution.py:528
  445.1 2.4 multiply_reduce_fusion.4
  447.6 1.7 fusion.13
  449.3 15.5 %multiply_convert_fusion = bf16[2304,2048]{1,0:T(8,128)(2,1)} fusion(bf16[2304,1024]{1,0:T(8,128)(2,1)} %bitcast.134, f32[2304]{0:T(1024)S(1)} %mul.130, bf16[1,1024,2048]{2,1,0:T(8,128)(2,1)} %param.17), kind=kOutput, calls=%fused_computation.2 | convolution fusion | flops 9682550784 | bytes 18359296 | tf_op jit(solution)/shard_map/dot_general | solution.py:35
  464.8 11.8 %convolution_convert_fusion = bf16[16,256,2048]{2,1,0:T(8,128)(2,1)} fusion(bf16[16,144,2048]{2,1,0:T(8,128)(2,1)} %bitcast.94, s32[16,256]{1,0:T(8,128)S(1)} %copy-done.11), kind=kOutput, calls=%fused_computation.3 | convolution fusion | flops 2424897536 | bytes 26230784 | tf_op jit(solution)/shard_map/gct,gcd->gtd/dot_general | solution.py:1149
  476.7 1.6 collective-permute-start
  478.3 4.8 fusion.16
  483.9 1.2 collective-permute-start.2
  485.1 2.7 fusion.14
  489.3 13.7 %collective-permute-done = bf16[256,2048]{1,0:T(8,128)(2,1)S(1)} collective-permute-done((bf16[256,2048]{1,0:T(8,128)(2,1)}, bf16[256,2048]{1,0:T(8,128)(2,1)S(1)}, u32[]{:S(2)}, u32[]{:S(2)}) %collective-permute-start) | collective-permute-done | bytes 1048608 | tf_op jit(solution)/shard_map/ppermute | solution.py:1010
  503.0 1.6 pad_maximum_fusion.mid_ref
  504.5 35.4 %attention_back.1 = (bf16[512,3072]{1,0:T(8,128)(2,1)}, f32[1,128]{1,0:T(1,128)}, f32[1,128]{1,0:T(1,128)}) custom-call(f32[512,3072]{1,0:T(8,128)} %get-tuple-element.60.proj_ref, bf16[512,2048]{1,0:T(8,128)(2,1)} %pad_maximum_fusion.mid_ref, bf16[1024,2048]{1,0:T(8,128)(2,1)} %bitcast.133, f32[1,128]{1,0:T(1,128)} %get-tuple-element.95.gq_ref, ...), custom_call_target="tpu_custom_call" | custom-call | flops 5368709120 | bytes 20971520 | tf_op jit(solution)/shard_map/attention_back/pallas_call | solution.py:764
  540.0 14.8 %convert_multiply_fusion = (f32[512,2048]{1,0:T(8,128)}, f32[2048]{0:T(1024)S(1)}, f32[512,2048]{1,0:T(8,128)}) fusion(f32[512]{0:T(512)S(1)} %bitcast.120, bf16[2,256,2048]{2,1,0:T(8,128)(2,1)} %get-tuple-element.44, bf16[512,3072]{1,0:T(8,128)(2,1)} %get-tuple-element.65.grad_ref, bf16[2048,3072]{1,0:T(8,128)(2,1)} %bitcast.126), kind=kOutput, calls=%fused_computation.13 | convolution fusion | flops 6446643200 | bytes 26224640 | tf_op jit(solution)/shard_map/te,de->td/dot_general | solution.py:1159
  555.7 2.7 slice.75
  558.4 1.6 collective-permute-start.4
  560.0 33.0 %collective-permute-done.2 = bf16[512,2048]{1,0:T(8,128)(2,1)} collective-permute-done((bf16[512,2048]{1,0:T(8,128)(2,1)}, bf16[512,2048]{1,0:T(8,128)(2,1)}, u32[]{:S(2)}, u32[]{:S(2)}) %collective-permute-start.2) | collective-permute-done | bytes 2097184 | tf_op jit(solution)/shard_map/ppermute | solution.py:1010
  593.0 6.7 convert_add_fusion
  599.7 124.7 %dense_gradients.1 = (bf16[128,3072]{1,0:T(8,128)(2,1)}, bf16[64,2048]{1,0:T(8,128)(2,1)}, f32[32,128]{1,0:T(8,128)}) custom-call(bf16[512,2048]{1,0:T(8,128)(2,1)} %get-tuple-element.59.h1_ref, bf16[512,3072]{1,0:T(8,128)(2,1)} %get-tuple-element.65.grad_ref, bf16[512,1024]{1,0:T(8,128)(2,1)} %get-tuple-element.66.ob_ref, ...), custom_call_target="tpu_custom_call" | custom-call | flops 6442450944 | bytes 209715200 | tf_op jit(solution)/shard_map/dense_gradients/pallas_call | solution.py:844
  724.4 1.4 collective-permute-start.5
  725.8 4.8 collective-permute-start.6
  730.6 4.7 fusion.15
  736.6 1.5 collective-permute-start.12
  738.1 1.5 collective-permute-done.8
  740.1 1.4 collective-permute-start.9
  742.3 3.0 multiply_reduce_fusion.3
  745.5 131.1 %collective-permute-start.3 = (bf16[128,3072]{1,0:T(8,128)(2,1)S(1)}, bf16[128,3072]{1,0:T(8,128)(2,1)S(1)}, u32[]{:S(2)}, u32[]{:S(2)}) collective-permute-start(bf16[128,3072]{1,0:T(8,128)(2,1)S(1)} %copy-done.9), channel_id=1, source_target_pairs={{16,0},{0,16},{17,1},{1,17},{18,2},{2,18},{19,3},{3,19},{20,4},{4,... | collective-permute-start | bytes 2359304 | tf_op jit(solution)/shard_map/ppermute | solution.py:1010
  876.5 1.3 slice_add_fusion.1
  877.8 1.1 select_select_fusion.1
  878.9 1.1 maximum_convert_fusion
  879.9 14.2 %collective-permute-done.3 = bf16[128,3072]{1,0:T(8,128)(2,1)S(1)} collective-permute-done((bf16[128,3072]{1,0:T(8,128)(2,1)S(1)}, bf16[128,3072]{1,0:T(8,128)(2,1)S(1)}, u32[]{:S(2)}, u32[]{:S(2)}) %collective-permute-start.3) | collective-permute-done | bytes 786464 | tf_op jit(solution)/shard_map/ppermute | solution.py:1010
  894.3 1.3 pad_maximum_fusion.1
  895.6 3.3 gather_fusion.1
  898.9 1.6 convert_bitcast_fusion
  900.5 4.1 copy.31
  904.6 5.5 reshape.260
  910.1 6.5 add_bitcast_fusion
  916.6 5.7 add_bitcast_fusion.1
  922.3 6.5 add_bitcast_fusion.2
  (112 shorter events, 14.3 us)
Async XLA Ops:
  7.2 100.0 %copy-start = (s32[1,512]{1,0:T(1,128)S(1)}, s32[1,512]{1,0:T(1,128)}, u32[]{:S(2)}) copy-start(s32[1,512]{1,0:T(1,128)} %param.18) | copy-start | bytes 6148
  7.2 915.1 %reduce-scatter.2.cloned.1.call-start = ((), (), s32[]{:S(2)}) async-start(), calls=%async_computation.1 | async-start | bytes 17825792 | tf_op jit(solution)/shard_map/reduce_scatter | solution.py:1150
  105.2 104.4 %copy-start.10 = (s32[16,256]{1,0:T(8,128)}, s32[16,256]{1,0:T(8,128)S(1)}, u32[]{:S(2)}) copy-start(s32[16,256]{1,0:T(8,128)S(1)} %fusion.4.slot_ref) | copy-start | bytes 49156
  105.2 104.4 %copy-start.15 = (f32[16,1,256]{2,0,1:T(8,128)}, f32[16,1,256]{2,0,1:T(8,128)S(1)}, u32[]{:S(2)}) copy-start(f32[16,1,256]{2,0,1:T(8,128)S(1)} %copy.45) | copy-start | bytes 49156
  110.7 2.3 copy-start.16
  304.3 16.1 %copy-start.19 = (bf16[8,288,2048]{2,1,0:T(8,128)(2,1)S(1)}, bf16[8,288,2048]{2,1,0:T(8,128)(2,1)}, u32[]{:S(2)}) copy-start(bf16[8,288,2048]{2,1,0:T(8,128)(2,1)} %get-tuple-element.55) | copy-start | bytes 28311556
  304.3 16.0 %copy-start.20 = (bf16[8,288,1024]{2,1,0:T(8,128)(2,1)S(1)}, bf16[8,288,1024]{2,1,0:T(8,128)(2,1)}, u32[]{:S(2)}) copy-start(bf16[8,288,1024]{2,1,0:T(8,128)(2,1)} %get-tuple-element.56.dg_ref) | copy-start | bytes 14155780
  304.4 28.2 %slice-start = ((s8[4718592]{0:T(1024)(128)(4,1)}), s8[4194304]{0:T(1024)(128)(4,1)S(1)}, s32[]{:S(2)}) async-start(s8[4718592]{0:T(1024)(128)(4,1)} %bitcast.135), calls=%async_computation.2 | async-start | bytes 8388608
  304.4 28.2 %slice-start.2 = ((s8[9437184]{0:T(1024)(128)(4,1)}), s8[4194304]{0:T(1024)(128)(4,1)S(1)}, s32[]{:S(2)}) async-start(s8[9437184]{0:T(1024)(128)(4,1)} %bitcast.137), calls=%async_computation.4 | async-start | bytes 8388608
  304.4 28.2 %slice-start.3 = ((s8[9437184]{0:T(1024)(128)(4,1)}), s8[4194304]{0:T(1024)(128)(4,1)S(1)}, s32[]{:S(2)}) async-start(s8[9437184]{0:T(1024)(128)(4,1)} %bitcast.137), calls=%async_computation.5 | async-start | bytes 8388608
  320.4 12.2 %slice-start.1 = ((s8[4718592]{0:T(1024)(128)(4,1)}), s8[524288]{0:T(1024)(128)(4,1)S(1)}, s32[]{:S(2)}) async-start(s8[4718592]{0:T(1024)(128)(4,1)} %bitcast.135), calls=%async_computation.3 | async-start | bytes 1048576
  320.4 12.2 %slice-start.4 = ((s8[9437184]{0:T(1024)(128)(4,1)}), s8[1048576]{0:T(1024)(128)(4,1)S(1)}, s32[]{:S(2)}) async-start(s8[9437184]{0:T(1024)(128)(4,1)} %bitcast.137), calls=%async_computation.6 | async-start | bytes 2097152
  332.6 12.4 %copy-start.11 = (s32[16,256]{1,0:T(8,128)S(1)}, s32[16,256]{1,0:T(8,128)}, u32[]{:S(2)}) copy-start(s32[16,256]{1,0:T(8,128)} %copy-done.10) | copy-start | bytes 49156
  345.0 2.0 copy-start.2
  347.2 97.9 %copy-start.13 = (f32[2048]{0:T(1024)S(1)}, f32[2048]{0:T(1024)}, u32[]{:S(2)}) copy-start(f32[2048]{0:T(1024)} %get-tuple-element.96) | copy-start | bytes 24580
  445.1 2.4 copy-start.3
  445.1 2.5 copy-start.6
  476.7 8.5 copy-start.5
  476.7 26.3 %collective-permute-start = (bf16[256,2048]{1,0:T(8,128)(2,1)}, bf16[256,2048]{1,0:T(8,128)(2,1)S(1)}, u32[]{:S(2)}, u32[]{:S(2)}) collective-permute-start(bf16[256,2048]{1,0:T(8,128)(2,1)} %fusion.13), channel_id=1, source_target_pairs={{16,0},{0,16},{17,1},{1,17},{18,2},{2,18},{19,3},{3,19},{20,4},{4,... | collective-permute-start | bytes 3145736 | tf_op jit(solution)/shard_map/ppermute | solution.py:1010
  483.1 76.9 %collective-permute-start.1 = (bf16[512,2048]{1,0:T(8,128)(2,1)}, bf16[512,2048]{1,0:T(8,128)(2,1)}, u32[]{:S(2)}, u32[]{:S(2)}) collective-permute-start(bf16[512,2048]{1,0:T(8,128)(2,1)} %get-tuple-element.87), channel_id=1, source_target_pairs={{16,0},{0,16},{17,1},{1,17},{18,2},{2,18},{19,3},{3,19},{20,4},{4,... | collective-permute-start | bytes 6291464 | tf_op jit(solution)/shard_map/ppermute | solution.py:1010
  483.9 4.8 copy-start.8
  483.9 19.0 %copy-start.7 = (bf16[256,2048]{1,0:T(8,128)(2,1)S(1)}, bf16[256,2048]{1,0:T(8,128)(2,1)}, u32[]{:S(2)}) copy-start(bf16[256,2048]{1,0:T(8,128)(2,1)} %fusion.13) | copy-start | bytes 3145732
  483.9 109.0 %collective-permute-start.2 = (bf16[512,2048]{1,0:T(8,128)(2,1)}, bf16[512,2048]{1,0:T(8,128)(2,1)}, u32[]{:S(2)}, u32[]{:S(2)}) collective-permute-start(bf16[512,2048]{1,0:T(8,128)(2,1)} %get-tuple-element.86), channel_id=1, source_target_pairs={{16,0},{0,16},{17,1},{1,17},{18,2},{2,18},{19,3},{3,19},{20,4},{4,... | collective-permute-start | bytes 6291464 | tf_op jit(solution)/shard_map/ppermute | solution.py:1010
  487.8 422.2 %collective-permute-start.11 = (bf16[1024,1024]{1,0:T(8,128)(2,1)}, bf16[1024,1024]{1,0:T(8,128)(2,1)}, u32[]{:S(2)}, u32[]{:S(2)}) collective-permute-start(bf16[1024,1024]{1,0:T(8,128)(2,1)} %get-tuple-element.83), channel_id=1, source_target_pairs={{16,0},{0,16},{17,1},{1,17},{18,2},{2,18},{19,3},{3,19},{20,4},{4,... | collective-permute-start | bytes 6291464 | tf_op jit(solution)/shard_map/ppermute | solution.py:1010
  540.0 14.8 %copy-start.17 = (f32[1,128]{1,0:T(1,128)S(1)}, f32[1,128]{1,0:T(1,128)}, u32[]{:S(2)}) copy-start(f32[1,128]{1,0:T(1,128)} %get-tuple-element.67) | copy-start | bytes 1540
  540.0 14.8 %copy-start.18 = (f32[1,128]{1,0:T(1,128)S(1)}, f32[1,128]{1,0:T(1,128)}, u32[]{:S(2)}) copy-start(f32[1,128]{1,0:T(1,128)} %get-tuple-element.68) | copy-start | bytes 1540
  558.4 178.2 %collective-permute-start.4 = (bf16[256,2048]{1,0:T(8,128)(2,1)}, bf16[256,2048]{1,0:T(8,128)(2,1)}, u32[]{:S(2)}, u32[]{:S(2)}) collective-permute-start(bf16[256,2048]{1,0:T(8,128)(2,1)} %slice.75), channel_id=1, source_target_pairs={{0,16},{16,0},{1,17},{17,1},{2,18},{18,2},{3,19},{19,3},{4,20},{20... | collective-permute-start | bytes 3145736 | tf_op jit(solution)/shard_map/ppermute | solution.py:1013
  724.4 17.2 %copy-start.12 = (bf16[64,2048]{1,0:T(8,128)(2,1)S(1)}, bf16[64,2048]{1,0:T(8,128)(2,1)}, u32[]{:S(2)}) copy-start(bf16[64,2048]{1,0:T(8,128)(2,1)} %get-tuple-element.71) | copy-start | bytes 786436
  724.4 17.9 %copy-start.14 = (f32[2048]{0:T(1024)S(1)}, f32[2048]{0:T(1024)}, u32[]{:S(2)}) copy-start(f32[2048]{0:T(1024)} %get-tuple-element.97) | copy-start | bytes 24580
  724.4 15.8 %collective-permute-start.5 = (bf16[64,2048]{1,0:T(8,128)(2,1)}, bf16[64,2048]{1,0:T(8,128)(2,1)}, u32[]{:S(2)}, u32[]{:S(2)}) collective-permute-start(bf16[64,2048]{1,0:T(8,128)(2,1)} %get-tuple-element.71), channel_id=1, source_target_pairs={{1,0},{3,2},{5,4},{7,6},{9,8},{11,10},{13,12},{15,14},{16,17},{18,... | collective-permute-start | bytes 786440 | tf_op jit(solution)/shard_map/ppermute | solution.py:982
  725.8 15.8 %collective-permute-start.6 = (bf16[64,2048]{1,0:T(8,128)(2,1)}, bf16[64,2048]{1,0:T(8,128)(2,1)}, u32[]{:S(2)}, u32[]{:S(2)}) collective-permute-start(bf16[64,2048]{1,0:T(8,128)(2,1)} %get-tuple-element.71), channel_id=1, source_target_pairs={{0,16},{2,18},{4,20},{6,22},{8,24},{10,26},{12,28},{14,30},{16,1},... | collective-permute-start | bytes 786440 | tf_op jit(solution)/shard_map/ppermute | solution.py:982
  735.9 3.6 collective-permute-start.8
  736.6 8.7 copy-start.9
  736.6 173.5 %collective-permute-start.12 = (bf16[1024,1024]{1,0:T(8,128)(2,1)}, bf16[1024,1024]{1,0:T(8,128)(2,1)}, u32[]{:S(2)}, u32[]{:S(2)}) collective-permute-start(bf16[1024,1024]{1,0:T(8,128)(2,1)} %get-tuple-element.82), channel_id=1, source_target_pairs={{16,0},{0,16},{17,1},{1,17},{18,2},{2,18},{19,3},{3,19},{20,4},{4,... | collective-permute-start | bytes 6291464 | tf_op jit(solution)/shard_map/ppermute | solution.py:1010
  739.5 170.5 %collective-permute-start.10 = (bf16[1024,1024]{1,0:T(8,128)(2,1)}, bf16[1024,1024]{1,0:T(8,128)(2,1)}, u32[]{:S(2)}, u32[]{:S(2)}) collective-permute-start(bf16[1024,1024]{1,0:T(8,128)(2,1)} %get-tuple-element.84), channel_id=1, source_target_pairs={{16,0},{0,16},{17,1},{1,17},{18,2},{2,18},{19,3},{3,19},{20,4},{4,... | collective-permute-start | bytes 6291464 | tf_op jit(solution)/shard_map/ppermute | solution.py:1010
  740.1 170.0 %collective-permute-start.9 = (bf16[1024,1024]{1,0:T(8,128)(2,1)}, bf16[1024,1024]{1,0:T(8,128)(2,1)}, u32[]{:S(2)}, u32[]{:S(2)}) collective-permute-start(bf16[1024,1024]{1,0:T(8,128)(2,1)} %get-tuple-element.85), channel_id=1, source_target_pairs={{16,0},{0,16},{17,1},{1,17},{18,2},{2,18},{19,3},{3,19},{20,4},{4,... | collective-permute-start | bytes 6291464 | tf_op jit(solution)/shard_map/ppermute | solution.py:1010
  741.6 3.9 collective-permute-start.7
  745.5 148.7 %collective-permute-start.3 = (bf16[128,3072]{1,0:T(8,128)(2,1)S(1)}, bf16[128,3072]{1,0:T(8,128)(2,1)S(1)}, u32[]{:S(2)}, u32[]{:S(2)}) collective-permute-start(bf16[128,3072]{1,0:T(8,128)(2,1)S(1)} %copy-done.9), channel_id=1, source_target_pairs={{16,0},{0,16},{17,1},{1,17},{18,2},{2,18},{19,3},{3,19},{20,4},{4,... | collective-permute-start | bytes 2359304 | tf_op jit(solution)/shard_map/ppermute | solution.py:1010
  910.1 6.5 copy-start.4
  922.3 6.5 copy-start.1
Sparse Core Ops, SparseCore 0:
  476.8 207.0 reduce-scatter.1

commit v4 on v3

--- a/solution.py
+++ b/solution.py
@@ -450,6 +450,177 @@
     )(h2, dy_all, slot, weight, wg, wu, wd)
 
 
+def column_of(table, dev):
+    lanes = lax.broadcasted_iota(jnp.int32, table.shape, 1)
+    return jnp.sum(jnp.where(lanes == dev, table[...], 0.0), axis=1, keepdims=True)
+
+
+def returned(hops, d, cap, tok, slot_ref, rows_ref, same_ref, other_ref, weight_ref=None):
+    chip = hops.chip(d)
+    lanes = lax.broadcasted_iota(jnp.int32, (tok, cap), 1).astype(F32)
+    for k, ref in ((hops.core, same_ref), (1 - hops.core, other_ref)):
+        pick = (column_of(slot_ref, 2 * chip + k) == lanes).astype(F32).astype(BF)
+        rows = pl.ds(pl.multiple_of(k * cap, 16), cap)
+        weight = None if weight_ref is None else column_of(weight_ref, 2 * chip + k)
+
+        def spread(at, pick=pick, rows=rows, ref=ref, weight=weight):
+            value = dot32(pick, rows_ref[rows, at])
+            if weight is not None:
+                value = weight * value
+            ref[:, at] = value.astype(ref.dtype)
+
+        tiles(rows_ref.shape[1] // 1024, 1024, spread)
+
+
+def scatter_order(half):
+    order = [half, half - 1, 1 - half]
+    for s in range(half - 2, 0, -1):
+        order += [-s, s]
+    return order + [0]
+
+
+def outputs_kernel(
+    chips, cap,
+    act_ref, xs_ref, de_ref, dg_ref, du_ref, slot_ref, weight_ref, wd_hbm,
+    total_ref, down_ref, came_ref, gate_ref, up_ref,
+    wd, left, right, made_d, made, act, rows_b, mine, out, came, far, up_in, down_in,
+    up, down, side, w_sem, act_sem, left_sem, right_sem, made_sem, down_sem, rep_sem,
+):
+    hops = Hops(chips)
+    replica = lax.axis_index("rep")
+    tok, width = total_ref.shape
+    order = scatter_order(chips // 2)
+    number = {d: i for i, d in enumerate(order)}
+    strip = right.shape[2]
+    count = width // strip
+
+    def act_copy(i):
+        rows = pl.ds(pl.multiple_of(hops.chip(order[i]) * (2 * cap), 2 * cap), 2 * cap)
+        return pltpu.make_async_copy(act_ref.at[rows], act.at[i % 2], act_sem.at[i % 2])
+
+    jobs = [
+        (thin, wide, result, i)
+        for thin, wide, result in (
+            (act_ref, de_ref, down_ref),
+            (dg_ref, xs_ref, gate_ref),
+            (du_ref, xs_ref, up_ref),
+        )
+        for i in range(count)
+    ]
+    done, stored, sent = [], {}, []
+
+    def right_copy(n):
+        at = pl.ds(jobs[n][3] * strip, strip)
+        return pltpu.make_async_copy(jobs[n][1].at[:, at], right.at[n % 2], right_sem.at[n % 2])
+
+    def job():
+        n = len(done)
+        if n == len(jobs):
+            return
+        done.append(n)
+        thin, _, result, i = jobs[n]
+        if i == 0:
+            fresh = pltpu.make_async_copy(thin, left, left_sem)
+            fresh.start()
+            fresh.wait()
+        right_copy(n).wait()
+        if n + 1 < len(jobs):
+            right_copy(n + 1).start()
+        at = pl.ds(i * strip, strip)
+        if n < count:
+            made_d[i] = dot_tn(left[...], right[n % 2]).astype(BF)
+            stored[n] = pltpu.make_async_copy(made_d.at[i], result.at[:, at], down_sem.at[i])
+            c = pltpu.make_async_remote_copy(
+                src_ref=made_d.at[i],
+                dst_ref=came_ref.at[:, at],
+                send_sem=rep_sem.at[0, i],
+                recv_sem=rep_sem.at[1, i],
+                device_id={"rep": 1 - replica},
+                device_id_type=MESH,
+            )
+            c.start()
+            sent.append(c)
+        else:
+            if n - 2 >= count:
+                stored.pop(n - 2).wait()
+            made[n % 2] = dot_tn(right[n % 2], left[...]).astype(BF)
+            stored[n] = pltpu.make_async_copy(made.at[n % 2], result.at[at, :], made_sem.at[n % 2])
+        stored[n].start()
+
+    def produce(d, same_ref, other_ref):
+        i = number[d]
+        act_copy(i).wait()
+        if i + 1 < chips:
+            act_copy(i + 1).start()
+
+        def last(at):
+            rows_b[:, at] = dot32(act[i % 2], wd[:, at]).astype(BF)
+
+        tiles(width // 512, 512, last)
+        returned(hops, d, cap, tok, slot_ref, rows_b, same_ref, other_ref, weight_ref)
+
+    def finish(value, at):
+        total_ref[at, :] = value
+
+    load = pltpu.make_async_copy(wd_hbm, wd, w_sem)
+    load.start()
+    act_copy(0).start()
+    right_copy(0).start()
+    hops.meet(2)
+    load.wait()
+    ring = hops.scatter(tok, produce, mine, out, came, far, up_in, down_in, up, down, side, finish)
+    share = -(-(len(jobs) - count) // (chips // 2 - 1))
+    for step in range(chips // 2):
+        next(ring)
+        for _ in range(share if step else count):
+            job()
+    hops.turn(ring)
+    for c in stored.values():
+        c.wait()
+    for c in sent:
+        c.wait()
+
+
+def outputs(chips, cap, act, xs, de, dg, du, slot_t, weight_t, wd, collective_id):
+    ff, width = wd.shape
+    tok = slot_t.shape[0]
+    strip = 512
+    anywhere = pl.BlockSpec(memory_space=pl.ANY)
+    vmem = pl.BlockSpec(memory_space=pltpu.VMEM)
+    tall, flat = jax.ShapeDtypeStruct((width, ff), BF), jax.ShapeDtypeStruct((ff, width), BF)
+    return pl.pallas_call(
+        functools.partial(outputs_kernel, chips, cap),
+        out_shape=(jax.ShapeDtypeStruct((tok, width), F32), flat, flat, tall, tall),
+        in_specs=[anywhere] * 5 + [vmem] * 2 + [anywhere],
+        out_specs=(vmem,) + (anywhere,) * 4,
+        scratch_shapes=[
+            pltpu.VMEM((ff, width), BF),
+            pltpu.VMEM((2 * chips * cap, ff), BF),
+            pltpu.VMEM((2, 2 * chips * cap, strip), BF),
+            pltpu.VMEM((width // strip, ff, strip), BF),
+            pltpu.VMEM((2, strip, ff), BF),
+            pltpu.VMEM((2, 2 * cap, ff), BF),
+            pltpu.VMEM((2 * cap, width), BF),
+            *scatter_scratch(chips, tok, width),
+            *ring_sems(chips),
+            DMA,
+            DMA((2,)),
+            DMA,
+            DMA((2,)),
+            DMA((2,)),
+            DMA((width // strip,)),
+            DMA((2, width // strip)),
+        ],
+        compiler_params=pltpu.CompilerParams(
+            collective_id=collective_id, has_side_effects=True, vmem_limit_bytes=63 << 20
+        ),
+        cost_estimate=pl.CostEstimate(
+            flops=2 * 2 * chips * cap * width * ff * 4, transcendentals=0, bytes_accessed=200 << 20
+        ),
+        name="outputs",
+    )(act, xs, de, dg, du, slot_t, weight_t, wd)
+
+
 def rows_back_kernel(
     chips, cap,
     dg_ref, du_ref, slot_ref, wg_hbm, wu_hbm, total_ref,
@@ -457,12 +628,8 @@
     up, down, side, w_sem, in_sem,
 ):
     hops = Hops(chips)
-    half = chips // 2
     tok, width = total_ref.shape
-    order = [half]
-    for s in range(half - 1, 0, -1):
-        order += [s, -s] if s == half - 1 else [-s, s]
-    order += [0]
+    order = scatter_order(chips // 2)
     number = {d: i for i, d in enumerate(order)}
     loads = [
         pltpu.make_async_copy(a, b, w_sem.at[i])
@@ -495,22 +662,7 @@
             drow[:, at] = (dot_nt(dg[p], wg[at, :]) + dot_nt(du[p], wu[at, :])).astype(BF)
 
         tiles(width // 512, 512, back)
-        chip = hops.chip(d)
-        lanes = lax.broadcasted_iota(jnp.int32, (tok, cap), 1)
-
-        def pick(k):
-            return (slot_ref[2 * chip + k] == lanes).astype(F32).astype(BF)
-
-        same, other = hops.core, 1 - hops.core
-        same_pick, other_pick = pick(same), pick(other)
-        same_rows = pl.ds(pl.multiple_of(same * cap, 16), cap)
-        other_rows = pl.ds(pl.multiple_of(other * cap, 16), cap)
-
-        def spread(at):
-            same_ref[:, at] = dot32(same_pick, drow[same_rows, at])
-            other_ref[:, at] = dot32(other_pick, drow[other_rows, at]).astype(BF)
-
-        tiles(width // 1024, 1024, spread)
+        returned(hops, d, cap, tok, slot_ref, drow, same_ref, other_ref)
 
     def finish(value, at):
         total_ref[at, :] = value
@@ -521,7 +673,7 @@
 
 
 def rows_back(chips, cap, dg, du, slot, wg, wu, collective_id):
-    tok = slot.shape[1]
+    tok = slot.shape[0]
     width, ff = wg.shape
     anywhere = pl.BlockSpec(memory_space=pl.ANY)
     vmem = pl.BlockSpec(memory_space=pltpu.VMEM)
@@ -792,9 +944,12 @@
 ):
     hops = Hops(chips)
     scratches = [scratch[9 * i : 9 * i + 9] for i in range(3)]
-    hops.meet()
-
+    hops.meet(2 if split_out else 1)
     first = hops.core == 0
+    if split_out:
+        q_sum, q_came, o_sum, o_came, o_give, o_got, g_sum, g_came, rep_sem, flip_sem = scratch[27:]
+    else:
+        q_sum, o_sum, g_sum = qkv_ref, out_ref, gain_ref
 
     def product(left_ref, right_ref, rows, width):
         def produce(d, same_ref, other_ref):
@@ -825,11 +980,49 @@
     def ring(produce, ref, bufs):
         return hops.scatter(ref.shape[0], produce, *bufs, into(ref))
 
-    rings = [ring(product(h1_ref, grad_ref, *qkv_ref.shape), qkv_ref, scratches[0])]
+    rings = [ring(product(h1_ref, grad_ref, *q_sum.shape), q_sum, scratches[0])]
     if split_out:
-        rings.append(ring(product(ob_ref, mid_ref, *out_ref.shape), out_ref, scratches[1]))
-    rings.append(ring(small, gain_ref, scratches[2]))
+        rings.insert(0, ring(product(ob_ref, mid_ref, *o_sum.shape), o_sum, scratches[1]))
+    rings.append(ring(small, g_sum, scratches[2]))
     hops.turn(*rings)
+    if not split_out:
+        return
+
+    replica = lax.axis_index("rep")
+    pairs = ((o_sum, o_came), (q_sum, q_came), (g_sum, g_came))
+    swaps = [
+        pltpu.make_async_remote_copy(
+            src_ref=src,
+            dst_ref=dst,
+            send_sem=rep_sem.at[0, i],
+            recv_sem=rep_sem.at[1, i],
+            device_id={"rep": 1 - replica},
+            device_id_type=MESH,
+        )
+        for i, (src, dst) in enumerate(pairs)
+    ]
+    for c in swaps:
+        c.start()
+    mine = hops.core == replica
+    swaps[0].wait()
+    o_give[...] = jnp.where(mine, o_came[...], o_sum[...])
+    give = hops.copy(o_give, o_got, flip_sem.at[0], flip_sem.at[1], hops.flip)
+    give.start()
+    keep = jnp.where(mine, o_sum[...], o_came[...])
+    swaps[2].wait()
+    gain_ref[...] = g_sum[...] + g_came[...]
+    swaps[1].wait()
+    _, wide = q_sum.shape
+    even = replica == 0
+    for i in range(wide // HD):
+        own, came = q_sum[:, pl.ds(i * HD, HD)], q_came[:, pl.ds(i * HD, HD)]
+        qkv_ref[:, pl.ds(2 * i * HD, HD)] = jnp.where(even, own, came).astype(F32)
+        qkv_ref[:, pl.ds((2 * i + 1) * HD, HD)] = jnp.where(even, came, own).astype(F32)
+    give.wait()
+    half = o_sum.shape[0]
+    got = o_got[...]
+    out_ref[pl.ds(0, half), :] = jnp.where(first, keep, got).astype(F32)
+    out_ref[pl.ds(half, half), :] = jnp.where(first, got, keep).astype(F32)
 
 
 def dense_gradients(chips, split_out, h1, grad, ob, mid, gain_blocks, collective_id):
@@ -841,11 +1034,15 @@
     scratch = []
     for rows, columns in shapes:
         scratch += [*scatter_scratch(chips, rows, columns), *ring_sems(chips)]
+    if split_out:
+        scratch += [pltpu.VMEM(shapes[0], BF)] * 2 + [pltpu.VMEM(shapes[1], BF)] * 4
+        scratch += [pltpu.VMEM(shapes[2], F32)] * 2 + [DMA((2, 3)), DMA((2,))]
+        shapes = ((shard, 2 * width), (2 * half, D), shapes[2])
+    kinds = (F32, F32, F32) if split_out else (BF, BF, F32)
     return pl.pallas_call(
         functools.partial(dense_gradients_kernel, chips, split_out),
         out_shape=tuple(
-            jax.ShapeDtypeStruct(shape, kind)
-            for shape, kind in zip(shapes, (BF, BF, F32), strict=True)
+            jax.ShapeDtypeStruct(shape, kind) for shape, kind in zip(shapes, kinds, strict=True)
         ),
         in_specs=[vmem] * 5,
         out_specs=(vmem,) * 3,
@@ -974,25 +1171,6 @@
     )(tok, small, w_qkv, w_out)
 
 
-def out_rows(ring, half, rep, grp):
-    n = ring.devices
-
-    def send(pairs):
-        pairs = [(a * n + b, c * n + d) for (a, b), (c, d) in pairs]
-        return lax.ppermute(half, ("rep", "grp"), pairs)
-
-    chips = range(ring.chips)
-    mate = send([((r, 2 * j + 1 - r), (r, 2 * j + r)) for r in range(2) for j in chips])
-    across = [
-        send([((r, 2 * j + c), (1 - r, 2 * j + r)) for r in range(2) for j in chips])
-        for c in range(2)
-    ]
-    core = grp % 2
-    first = jnp.where(core == rep, jnp.where(core == 0, half, mate), across[0])
-    second = jnp.where(core == rep, jnp.where(core == 0, mate, half), across[1])
-    return jnp.concatenate([first, second], axis=0).astype(F32)
-
-
 def per_device(
     tokens, w_qkv, w_out, gains, w_gate, w_up, w_down, segment_ids, routes, gate_weights, cotangent
 ):
@@ -1061,14 +1239,16 @@
     g_query = gains_f[2 * D : 2 * D + HD]
     g_key = gains_f[2 * D + HD :]
 
-    order = jnp.concatenate(
-        [((rep + k) % reps) * tok_rows + jnp.arange(tok_rows, dtype=jnp.int32) for k in range(reps)]
-    )
-    frequency = rope_base ** (-2.0 * jnp.arange(HD // 2, dtype=F32) / HD)
-    angles = order.astype(F32)[:, None] * frequency[None, :]
-    cosine = jnp.concatenate([jnp.cos(angles)] * 2, axis=1)
-    sine = jnp.concatenate([-jnp.sin(angles), jnp.sin(angles)], axis=1)
-    docs = segment_ids[0][order]
+    def this_first(table):
+        return lax.dynamic_slice_in_dim(
+            jnp.concatenate([table, table], axis=0), rep * tok_rows, seq_len, axis=0
+        )
+
+    frequency = np.float32(rope_base) ** (-2.0 * np.arange(HD // 2, dtype=np.float32) / HD)
+    angles = np.arange(seq_len, dtype=np.float32)[:, None] * frequency.astype(np.float32)[None, :]
+    cosine = this_first(jnp.asarray(np.concatenate([np.cos(angles)] * 2, axis=1)))
+    sine = this_first(jnp.asarray(np.concatenate([-np.sin(angles), np.sin(angles)], axis=1)))
+    docs = this_first(segment_ids[0])
     g_query, g_key = g_query[None], g_key[None]
     dy_all, h1_b, projected, attended_b, mid_rows, h2_b = attention(
         ring.chips,
@@ -1106,20 +1286,28 @@
     all_ups = grad_ups.reshape(groups * capacity, -1)
 
     def rep_send(v):
-        v = v.astype(BF)
-        came = [[] for _ in range(1, reps)]
-        for part in jnp.split(v, 2):
-            for k in range(1, reps):
-                came[k - 1].append(from_rep(part, k))
-        return v, came
+        return v, [from_rep(v, k) for k in range(1, reps)]
 
     def rep_sum(sent, after):
         (v, came), _ = lax.optimization_barrier((sent, after))
-        return v.astype(F32) + sum(jnp.concatenate(c, axis=0).astype(F32) for c in came)
-
-    grad_wdown = rep_send(jnp.einsum("rf,rd->fd", all_acts, all_grads, preferred_element_type=F32))
-    grad_wgate = rep_send(jnp.einsum("rd,rf->df", all_rows, all_gates, preferred_element_type=F32))
-    grad_wup = rep_send(jnp.einsum("rd,rf->df", all_rows, all_ups, preferred_element_type=F32))
+        return v.astype(F32) + sum(c.astype(F32) for c in came)
+
+    slot_t, weight_t = slot.astype(F32).T, weight_in.T
+    together = split_out and chips <= 8
+    if together:
+        out_sum, own_down, came_down, grad_wgate, grad_wup = outputs(
+            chips, capacity, all_acts, all_rows, all_grads, all_gates, all_ups,
+            slot_t, weight_t, w_down[0], 6,
+        )
+        grad_wdown = (own_down, [came_down])
+    else:
+        grad_wdown = rep_send(
+            jnp.einsum("rf,rd->fd", all_acts, all_grads, preferred_element_type=F32).astype(BF)
+        )
+        grad_wgate = jnp.einsum("rd,rf->df", all_rows, all_gates, preferred_element_type=F32).astype(BF)
+        grad_wup = jnp.einsum("rd,rf->df", all_rows, all_ups, preferred_element_type=F32).astype(BF)
+    grad_wgate = rep_send(grad_wgate)
+    grad_wup = rep_send(grad_wup)
 
     cuts = 1 if chips <= 8 else chips // 8
     (grad_gates, grad_ups), _ = lax.optimization_barrier(
@@ -1127,7 +1315,7 @@
     )
     grad_h2 = jnp.concatenate(
         [
-            rows_back(chips, capacity, grad_gates, grad_ups, slot[:, :, None], wg, wu, 8 + i)
+            rows_back(chips, capacity, grad_gates, grad_ups, slot_t, wg, wu, 8 + i)
             for i, (wg, wu) in enumerate(
                 zip(jnp.split(w_gate[0], cuts), jnp.split(w_up[0], cuts), strict=True)
             )
@@ -1141,17 +1329,23 @@
     grad_mid_norm, ffn_terms = rms_backward(grad_h2, hat_two, inv_two, g_ffn)
     grad_mid = grad_out + grad_mid_norm
     grad_mid_b = grad_mid.astype(BF)
-    pick = (slot[:, None, :] == jnp.arange(capacity, dtype=jnp.int32)[None, :, None]).astype(BF)
-    row_weight = jnp.sum(pick.astype(F32) * weight_in[:, None, :], axis=-1)
-    acts_late, _ = lax.optimization_barrier((all_acts, grad_mid_b))
-    eout = dot32(acts_late, w_down[0]).astype(BF).astype(F32)
-    eout = (row_weight.reshape(-1, 1) * eout).astype(BF).reshape(groups, capacity, D)
-    out_all = jnp.einsum("gct,gcd->gtd", pick, eout, preferred_element_type=F32).astype(BF)
-    out_sum = lax.psum_scatter(
-        out_all.reshape(groups * tok_rows, D), "grp", scatter_dimension=0, tiled=True
-    )
-
+    if not together:
+        pick = (slot[:, None, :] == jnp.arange(capacity, dtype=jnp.int32)[None, :, None]).astype(BF)
+        row_weight = jnp.sum(pick.astype(F32) * weight_in[:, None, :], axis=-1)
+        acts_late, _ = lax.optimization_barrier((all_acts, grad_mid_b))
+        eout = dot32(acts_late, w_down[0]).astype(BF).astype(F32)
+        eout = (row_weight.reshape(-1, 1) * eout).astype(BF).reshape(groups, capacity, D)
+        out_all = jnp.einsum("gct,gcd->gtd", pick, eout, preferred_element_type=F32).astype(BF)
+        out_sum = lax.psum_scatter(
+            out_all.reshape(groups * tok_rows, D), "grp", scatter_dimension=0, tiled=True
+        )
+    result = mid_rows + lax.optimization_barrier((out_sum, grad_mid_b))[0].astype(F32)
+    grad_wdown = rep_sum(grad_wdown, grad_mid_b)
+    grad_wgate = rep_sum(grad_wgate, grad_mid_b)
     grad_branch_b = rep_gather(grad_mid_b)
+    (grad_branch_b, result, grad_wdown, grad_wgate), _ = lax.optimization_barrier(
+        ((grad_branch_b, result, grad_wdown, grad_wgate), grad_mid_b)
+    )
     grad_proj, query_terms, key_terms = attention_back(
         projected, grad_branch_b, my_out, g_query, g_key, cosine, sine, docs
     )
@@ -1170,10 +1364,6 @@
         ]
     )
 
-    grad_wdown = rep_sum(grad_wdown, grad_h2)
-    (grad_proj, grad_wdown), _ = lax.optimization_barrier(
-        ((grad_proj, grad_wdown), grad_h1_part)
-    )
     gain_size = gains.shape[0]
     gain_blocks = jnp.pad(
         grad_gains.reshape(groups, gain_size), ((0, 0), (0, 4096 - gain_size))
@@ -1189,18 +1379,15 @@
         4,
     )
     total = total.reshape(-1)[:gain_size]
-    qkv_all = [shard_qkv] + [from_rep(shard_qkv, k) for k in range(1, reps)]
-    columns = jnp.stack(qkv_all, axis=0).reshape(reps, shard, 3, heads, HD)
-    columns = columns[(jnp.arange(reps) - rep) % reps]
-    shard_qkv = columns.transpose(1, 2, 3, 0, 4).reshape(shard, 3 * D).astype(F32)
-
-    grad_wgate = rep_sum(grad_wgate, shard_qkv)
     grad_wup = rep_sum(grad_wup, shard_qkv)
-    result = mid_rows + lax.optimization_barrier((out_sum, shard_qkv))[0].astype(F32)
 
     if split_out:
-        shard_out = out_rows(ring, half_out, rep, grp)
+        shard_out = half_out
     else:
+        qkv_all = [shard_qkv] + [from_rep(shard_qkv, k) for k in range(1, reps)]
+        columns = jnp.stack(qkv_all, axis=0).reshape(reps, shard, 3, heads, HD)
+        columns = columns[(jnp.arange(reps) - rep) % reps]
+        shard_qkv = columns.transpose(1, 2, 3, 0, 4).reshape(shard, 3 * D).astype(F32)
         grad_wout = dot_tn(attended_b, grad_branch_b)
         whole = lax.dynamic_update_slice(
             jnp.zeros((heads, reps, HD, D), BF),
@@ -1210,9 +1397,9 @@
         shard_out = lax.psum(
             lax.psum_scatter(whole, "grp", scatter_dimension=0, tiled=True), "rep"
         ).astype(F32)
-    own_gains = total
-    for k in range(1, reps):
-        total = total + from_rep(own_gains, k)
+        own_gains = total
+        for k in range(1, reps):
+            total = total + from_rep(own_gains, k)
     return (
         result[None],
         grad_tokens[None],

time: 945 us -> 815 us (0.86)
  starting transfers between devices: 148 us -> 5.18 us
  Pallas kernels: 542 us -> 641 us
  matrix products: 82.8 us -> 14.7 us
  waiting for transfers between devices: 62.5 us -> 91.1 us
  local copies, waits for them, and re-layouts: 39.4 us -> 18.2 us
  between operations: 14.8 us -> 1.33 us
  other arithmetic: 46.5 us -> 35.6 us
    ppermute x9 -> x3, starting transfers between devices: 140 us -> 3.46 us  [from_rep(): return lax.ppermute(v, 'rep', [((s + k) % reps, s) for s in range(reps)])]
    pallas_call x0 -> x1, Pallas kernels: none -> 109 us  [outputs(): pl.pallas_call(functools.partial(outputs_kernel, chips, cap), out_shape=(...]
    dot_general x4 -> x0, matrix products: 52.3 us -> none  [the longest x1 16 us: per_device(): jnp.einsum('rd,rf->df', all_rows, all_ups, preferred_element_type=F32)]
    ppermute x9 -> x3, waiting for transfers between devices: 62.4 us -> 91.1 us  [from_rep(): return lax.ppermute(v, 'rep', [((s + k) % reps, s) for s in range(reps)])]
    dot_general x2 -> x1, matrix products: 15.6 us -> 0.19 us  [dot32(): return jnp.dot(a, b, preferred_element_type=F32)]
    split x3 -> x0, local copies, waits for them, and re-layouts: 12.2 us -> none  [rep_send(): jnp.split(v, 2)]
  transfers between devices with their start and end apart: 14 -> 4, of which waited for: 4 -> 1; matrix products, arithmetic and copies ran while one was open for 8% -> 6% of each run, Pallas kernels for 17% -> 31%
where the time goes in v4:
time: 815 us; the launch traced here: 807 us
  Pallas kernels  641 us (79%)
  waiting for transfers between devices  91.1 us (11%)
  other arithmetic  35.6 us (4%)
  local copies, waits for them, and re-layouts  18.2 us (2%)
  matrix products  14.7 us (2%)
    pallas_call x1, Pallas kernels, dense_gradients(): pl.pallas_call(functools.partial(dense_gradients_kernel, chips, split_out...  116 us
    pallas_call x1, Pallas kernels, outputs(): pl.pallas_call(functools.partial(outputs_kernel, chips, cap), out_shape=(...  109 us
    pallas_call x1, Pallas kernels, rows_back(): pl.pallas_call(functools.partial(rows_back_kernel, chips, cap), out_shape...  97.4 us
    pallas_call x1, Pallas kernels, attention(): pl.pallas_call(functools.partial(attention_kernel, chips, reps, heads), o...  96.5 us
    pallas_call x1, Pallas kernels, expert_rows(): pl.pallas_call(functools.partial(experts_kernel, chips, cap), out_shape=(...  94.6 us
    pallas_call x1, Pallas kernels, start(): pl.pallas_call(functools.partial(start_kernel, chips, reps, heads, split_...  92.5 us
    ppermute x3, waiting for transfers between devices, from_rep(): return lax.ppermute(v, 'rep', [((s + k) % reps, s) for s in range(reps)])  91.1 us
    pallas_call x1, Pallas kernels, attention_back(): pl.pallas_call(functools.partial(attention_back_kernel, heads), out_shape...  35.4 us
  transfers between devices with their start and end apart: 4, of which 1 were waited for; matrix products, arithmetic and copies ran while one was open for 6% of the time, Pallas kernels for 31%

profile of v4, /device:TPU:0, one launch (start us, length us, event | category | flops | bytes accessed | tf_op | source)
XLA Modules:
  0.0 807.4 jit_solution(12990207486773928905)
XLA Ops:
  0.6 0.7 pad_convert_fusion
  1.3 0.8 select_reduce_fusion
  2.2 0.7 maximum_maximum_fusion.small_ref
  2.9 92.5 %start.1 = (bf16[2,256,2048]{2,1,0:T(8,128)(2,1)}, f32[16,32,256]{2,1,0:T(8,128)}, bf16[16,128,3072]{2,1,0:T(8,128)(2,1)}, bf16[8,128,2048]{2,1,0:T(8,128)(2,1)}) custom-call(bf16[256,2048]{1,0:T(8,128)(2,1)} %bitcast.71, f32[32,256]{1,0:T(8,128)} %maximum_maximum_fusion.small_ref, bf16[128,6144]{1,0:T(8,128)(2,1)} %wq_ref.1, bf16[128,2048]{1,0:T(8,128)(2,1)} %wo_ref.1), custom_call_target="tpu_custom_call" | custom-call | bytes 209715200 | tf_op jit(solution)/shard_map/start/pallas_call | solution.py:1145
  95.4 0.9 slice.37
  96.4 0.6 fusion.7
  97.0 0.6 slice_bitcast_fusion
  97.6 0.9 constant_dynamic-slice_fusion
  98.5 0.1 copy.42
  98.6 0.6 copy.53
  99.3 0.2 fusion.2
  99.5 0.7 copy.44.slot_ref
  100.2 0.7 convert_bitcast_fusion.slot_ref
  100.9 0.8 copy.41.dc_ref
  101.8 0.8 constant_dynamic-slice_fusion.1
  102.6 96.5 %attention.1 = (bf16[16,256,2048]{2,1,0:T(8,128)(2,1)}, bf16[512,2048]{1,0:T(8,128)(2,1)}, f32[512,3072]{1,0:T(8,128)}, bf16[512,1024]{1,0:T(8,128)(2,1)}, f32[2...) custom-call(bf16[256,2048]{1,0:T(8,128)(2,1)} %bitcast.68, bf16[512,2048]{1,0:T(8,128)(2,1)} %bitcast.70, f32[1,2048]{1,0:T(1,128)} %bitcast.77, ...), custom_call_target="tpu_custom_call" | custom-call | flops 6442450944 | bytes 104857600 | tf_op jit(solution)/shard_map/attention/pallas_call | solution.py:825
  199.1 94.6 %experts.1 = (bf16[8,288,2048]{2,1,0:T(8,128)(2,1)}, bf16[8,288,2048]{2,1,0:T(8,128)(2,1)}, bf16[8,288,1024]{2,1,0:T(8,128)(2,1)}, bf16[8,288,1024]{2,1,0:T(8,128)(2,1)}, bf16[8,288,1024]{2,1,0:T(8,128)(2,1)}) custom-call(bf16[256,2048]{1,0:T(8,128)(2,1)} %get-tuple-element.52.h2_ref, bf16[16,256,2048]{2,1,0:T(8,128)(2,1)} %get-tuple-element.53.dy_ref, ...), custom_call_target="tpu_custom_call" | custom-call | flops 28991029248 | bytes 209715200 | tf_op jit(solution)/shard_map/experts/pallas_call | solution.py:421
  293.8 108.9 %outputs.1 = (f32[256,2048]{1,0:T(8,128)}, bf16[1024,2048]{1,0:T(8,128)(2,1)}, bf16[1024,2048]{1,0:T(8,128)(2,1)}, bf16[2048,1024]{1,0:T(8,128)(2,1)}, bf16[2048,1024]{1,0:T(8,128)(2,1)}) custom-call(bf16[2304,1024]{1,0:T(8,128)(2,1)} %bitcast.104, bf16[2304,2048]{1,0:T(8,128)(2,1)} %bitcast.100, bf16[2304,2048]{1,0:T(8,128)(2,1)} %bitcast.101, ...), custom_call_target="tpu_custom_call" | custom-call | flops 38654705664 | bytes 209715200 | tf_op jit(solution)/shard_map/outputs/pallas_call | solution.py:591
  402.7 1.8 collective-permute-start.1
  404.5 0.3 collective-permute-start.3
  404.8 97.4 %rows_back.1 = f32[256,2048]{1,0:T(8,128)} custom-call(bf16[8,288,1024]{2,1,0:T(8,128)(2,1)} %get-tuple-element.62.dg_ref, bf16[8,288,1024]{2,1,0:T(8,128)(2,1)} %get-tuple-element.63.du_ref, f32[256,16]{1,0:T(8,128)} %convert_bitcast_fusion.slot_ref, bf16[2048,1024]{1,0:T(8,128)(2,1)} %bitcast.95, bf16[2048,1024]{1,0:T(8,128)(2,1)} %bitcast.97), custom_call_target="tpu_custom_call" | custom-call | flops 28991029248 | bytes 209715200 | tf_op jit(solution)/shard_map/rows_back/pallas_call | solution.py:680
  502.2 0.2 multiply_reduce_fusion.5
  502.5 1.3 copy-done.1
  503.8 0.6 multiply_reduce_fusion.2
  504.4 0.6 copy-done.4
  505.0 0.7 fusion.6
  505.7 1.4 collective-permute-start
  507.1 1.6 add.68
  508.7 0.5 multiply_reduce_fusion.1
  509.2 0.8 copy-done.7
  510.0 1.2 copy-done.8
  511.3 5.3 convert_add_fusion.1
  516.6 91.1 %collective-permute-done = bf16[256,2048]{1,0:T(8,128)(2,1)S(1)} collective-permute-done((bf16[256,2048]{1,0:T(8,128)(2,1)S(1)}, bf16[256,2048]{1,0:T(8,128)(2,1)S(1)}, u32[]{:S(2)}, u32[]{:S(2)}) %collective-permute-start) | collective-permute-done | bytes 1048608 | tf_op jit(solution)/shard_map/ppermute | solution.py:1188
  607.7 1.5 pad_maximum_fusion.mid_ref
  609.1 7.6 convert_add_fusion
  616.7 35.4 %attention_back.1 = (bf16[512,3072]{1,0:T(8,128)(2,1)}, f32[1,128]{1,0:T(1,128)}, f32[1,128]{1,0:T(1,128)}) custom-call(f32[512,3072]{1,0:T(8,128)} %get-tuple-element.72.proj_ref, bf16[512,2048]{1,0:T(8,128)(2,1)} %pad_maximum_fusion.mid_ref, bf16[1024,2048]{1,0:T(8,128)(2,1)} %bitcast.99, f32[1,128]{1,0:T(1,128)} %get-tuple-element.91.gq_ref, ...), custom_call_target="tpu_custom_call" | custom-call | flops 5368709120 | bytes 20971520 | tf_op jit(solution)/shard_map/attention_back/pallas_call | solution.py:916
  652.1 14.5 %multiply_reduce_fusion = (f32[2048]{0:T(1024)S(1)}, f32[512,2048]{1,0:T(8,128)}, f32[512,2048]{1,0:T(8,128)}) fusion(f32[512]{0:T(512)S(1)} %bitcast.86, bf16[2,256,2048]{2,1,0:T(8,128)(2,1)} %get-tuple-element.47, bf16[512,3072]{1,0:T(8,128)(2,1)} %get-tuple-element.74.grad_ref, bf16[2048,3072]{1,0:T(8,128)(2,1)} %bitcast.91), kind=kOutput, calls=%fused_computation.3 | convolution fusion | flops 6446643200 | bytes 26224640 | tf_op jit(solution)/shard_map/te,de->td/dot_general | solution.py:1353
  666.8 0.8 copy.51
  667.5 2.7 slice.70
  670.3 1.7 collective-permute-start.2
  672.0 115.8 %dense_gradients.1 = (f32[128,6144]{1,0:T(8,128)}, f32[128,2048]{1,0:T(8,128)}, f32[32,128]{1,0:T(8,128)}) custom-call(bf16[512,2048]{1,0:T(8,128)(2,1)} %get-tuple-element.75.h1_ref, bf16[512,3072]{1,0:T(8,128)(2,1)} %get-tuple-element.74.grad_ref, bf16[512,1024]{1,0:T(8,128)(2,1)} %get-tuple-element.76.ob_ref, bf16[512,2048]{1,0:T(8,128)(2,1)} %pad_maximum_fusion.mid_ref, ...), custom_call_target="tpu_custom_call" | custom-call | flops 6442450944 | bytes 209715200 | tf_op jit(solution)/shard_map/dense_gradients/pallas_call | solution.py:1042
  787.8 1.3 slice.57
  789.1 9.1 %add_bitcast_fusion = f32[1,2048,1024]{2,1,0:T(8,128)} fusion(bf16[2048,1024]{1,0:T(8,128)(2,1)} %collective-permute-done.3, bf16[2048,1024]{1,0:T(8,128)(2,1)} %get-tuple-element.83), kind=kLoop, calls=%fused_computation | loop fusion | flops 6291456 | bytes 16777216 | tf_op jit(solution)/shard_map/broadcast_in_dim | solution.py:1410
  798.2 1.8 multiply_reduce_fusion.3
  800.1 3.9 add_bitcast_fusion.1
  804.0 1.7 copy.56
  805.7 0.3 copy-done.12
  806.0 1.0 copy.57
  (59 shorter events, 0.5 us)
Async XLA Ops:
  2.9 98.0 %copy-start.19 = (s32[1,512]{1,0:T(1,128)S(1)}, s32[1,512]{1,0:T(1,128)}, u32[]{:S(2)}) copy-start(s32[1,512]{1,0:T(1,128)} %param.20) | copy-start | bytes 6148
  2.9 98.9 %copy-start.14 = (f32[1024,128]{1,0:T(8,128)S(1)}, f32[1024,128]{1,0:T(8,128)}, u32[]{:S(2)}) copy-start(f32[1024,128]{1,0:T(8,128)} %constant.59) | copy-start | bytes 1572868
  2.9 98.9 %copy-start.15 = (f32[1024,128]{1,0:T(8,128)S(1)}, f32[1024,128]{1,0:T(8,128)}, u32[]{:S(2)}) copy-start(f32[1024,128]{1,0:T(8,128)} %constant.60) | copy-start | bytes 1572868
  98.6 100.5 %copy-start.13 = (f32[16,1,256]{0,2,1:T(8,128)}, f32[16,1,256]{0,2,1:T(8,128)S(1)}, u32[]{:S(2)}) copy-start(f32[16,1,256]{0,2,1:T(8,128)S(1)} %copy.42) | copy-start | bytes 49156
  100.9 1.7 copy-start.18
  402.7 206.4 %collective-permute-start.1 = (bf16[2048,1024]{1,0:T(8,128)(2,1)}, bf16[2048,1024]{1,0:T(8,128)(2,1)}, u32[]{:S(2)}, u32[]{:S(2)}) collective-permute-start(bf16[2048,1024]{1,0:T(8,128)(2,1)} %get-tuple-element.69), channel_id=1, source_target_pairs={{16,0},{0,16},{17,1},{1,17},{18,2},{2,18},{19,3},{3,19},{20,4},{4,... | collective-permute-start | bytes 12582920 | tf_op jit(solution)/shard_map/ppermute | solution.py:1188
  404.5 383.3 %collective-permute-start.3 = (bf16[2048,1024]{1,0:T(8,128)(2,1)}, bf16[2048,1024]{1,0:T(8,128)(2,1)}, u32[]{:S(2)}, u32[]{:S(2)}) collective-permute-start(bf16[2048,1024]{1,0:T(8,128)(2,1)} %get-tuple-element.83), channel_id=1, source_target_pairs={{16,0},{0,16},{17,1},{1,17},{18,2},{2,18},{19,3},{3,19},{20,4},{4,... | collective-permute-start | bytes 12582920 | tf_op jit(solution)/shard_map/ppermute | solution.py:1188
  404.8 97.4 %copy-start = (f32[256,2048]{1,0:T(8,128)S(1)}, f32[256,2048]{1,0:T(8,128)}, u32[]{:S(2)}) copy-start(f32[256,2048]{1,0:T(8,128)} %get-tuple-element.51) | copy-start | bytes 6291460
  404.8 97.7 %copy-start.16 = (f32[2048]{0:T(1024)S(1)}, f32[2048]{0:T(1024)}, u32[]{:S(2)}) copy-start(f32[2048]{0:T(1024)} %get-tuple-element.92) | copy-start | bytes 24580
  502.2 1.6 copy-start.1
  503.8 1.2 copy-start.4
  505.0 2.0 copy-start.10
  505.0 3.7 copy-start.11
  505.7 102.0 %collective-permute-start = (bf16[256,2048]{1,0:T(8,128)(2,1)S(1)}, bf16[256,2048]{1,0:T(8,128)(2,1)S(1)}, u32[]{:S(2)}, u32[]{:S(2)}) collective-permute-start(bf16[256,2048]{1,0:T(8,128)(2,1)S(1)} %fusion.6), channel_id=1, source_target_pairs={{16,0},{0,16},{17,1},{1,17},{18,2},{2,18},{19,3},{3,19},{20,4},{4,... | collective-permute-start | bytes 3145736 | tf_op jit(solution)/shard_map/ppermute | solution.py:1188
  507.1 3.0 copy-start.7
  507.1 4.2 copy-start.8
  516.6 92.6 %copy-start.6 = (bf16[2048,1024]{1,0:T(8,128)(2,1)S(1)}, bf16[2048,1024]{1,0:T(8,128)(2,1)}, u32[]{:S(2)}) copy-start(bf16[2048,1024]{1,0:T(8,128)(2,1)} %get-tuple-element.69) | copy-start | bytes 12582916
  652.1 14.5 %copy-start.20 = (f32[1,128]{1,0:T(1,128)S(1)}, f32[1,128]{1,0:T(1,128)}, u32[]{:S(2)}) copy-start(f32[1,128]{1,0:T(1,128)} %get-tuple-element.77) | copy-start | bytes 1540
  652.1 14.5 %copy-start.21 = (f32[1,128]{1,0:T(1,128)S(1)}, f32[1,128]{1,0:T(1,128)}, u32[]{:S(2)}) copy-start(f32[1,128]{1,0:T(1,128)} %get-tuple-element.78) | copy-start | bytes 1540
  670.3 127.9 %collective-permute-start.2 = (bf16[256,2048]{1,0:T(8,128)(2,1)}, bf16[256,2048]{1,0:T(8,128)(2,1)}, u32[]{:S(2)}, u32[]{:S(2)}) collective-permute-start(bf16[256,2048]{1,0:T(8,128)(2,1)} %slice.70), channel_id=1, source_target_pairs={{0,16},{16,0},{1,17},{17,1},{2,18},{18,2},{3,19},{19,3},{4,20},{20... | collective-permute-start | bytes 3145736 | tf_op jit(solution)/shard_map/ppermute | solution.py:1191
  789.1 9.1 %copy-start.3 = (f32[512,2048]{1,0:T(8,128)S(1)}, f32[512,2048]{1,0:T(8,128)}, u32[]{:S(2)}) copy-start(f32[512,2048]{1,0:T(8,128)} %get-tuple-element.96) | copy-start | bytes 12582916
  789.1 9.1 %copy-start.5 = (f32[512,2048]{1,0:T(8,128)S(1)}, f32[512,2048]{1,0:T(8,128)}, u32[]{:S(2)}) copy-start(f32[512,2048]{1,0:T(8,128)} %get-tuple-element.89) | copy-start | bytes 12582916
  789.1 9.1 %copy-start.17 = (f32[2048]{0:T(1024)S(1)}, f32[2048]{0:T(1024)}, u32[]{:S(2)}) copy-start(f32[2048]{0:T(1024)} %get-tuple-element.93) | copy-start | bytes 24580
  798.2 1.9 copy-start.2
  800.1 3.9 copy-start.9
  804.0 2.0 copy-start.12

commit v5 on v4

--- a/solution.py
+++ b/solution.py
@@ -569,10 +569,11 @@
     hops.meet(2)
     load.wait()
     ring = hops.scatter(tok, produce, mine, out, came, far, up_in, down_in, up, down, side, finish)
-    share = -(-(len(jobs) - count) // (chips // 2 - 1))
+    job()
+    share = -(-(len(jobs) - 2) // (chips // 2 - 1))
     for step in range(chips // 2):
         next(ring)
-        for _ in range(share if step else count):
+        for _ in range(share if step else 1):
             job()
     hops.turn(ring)
     for c in stored.values():
@@ -728,8 +729,8 @@
 def attention_kernel(
     chips, reps, heads,
     cot_ref, seq_ref, ga_ref, gf_ref, gq_ref, gk_ref, cos_ref, sin_ref, dc_ref, dr_ref, wq_hbm, wo_hbm,
-    dy_ref, h1_ref, proj_ref, ob_ref, mid_ref, h2_ref,
-    wq, wo, give, came, up, down, side, rep_sem, own_sem,
+    dy_ref, h1_out, proj_out, ob_out, mid_ref, h2_ref,
+    wq, wo, give, came, h1_ref, proj_ref, ob_ref, up, down, side, rep_sem, own_sem, out_sem,
 ):
     hops = Hops(chips)
     rep = lax.axis_index("rep")
@@ -761,6 +762,13 @@
         at = pl.ds(i * step, step)
         proj_ref[:, at] = dot32(h1_ref[...], wq[:, at])
 
+    stores = [
+        pltpu.make_async_copy(a, b, out_sem.at[i])
+        for i, (a, b) in enumerate(((h1_ref, h1_out), (proj_ref, proj_out), (ob_ref, ob_out)))
+    ]
+    stores[0].start()
+    stores[1].start()
+
     def one(head, carry):
         _, _, q_b = head_of(
             proj_ref, columns_of(0, head, heads), gq_ref[...], cos_ref[...], sin_ref[...]
@@ -778,6 +786,7 @@
     lax.fori_loop(0, heads // 2, one, 0)
     next(ring)
     lax.fori_loop(heads // 2, heads, one, 0)
+    stores[2].start()
     loads[1].wait()
     swaps = []
     for k in range(1, reps):
@@ -814,6 +823,8 @@
     lax.fori_loop(0, tok // 64, second, 0)
     loads[2].wait()
     hops.turn(ring)
+    for c in stores:
+        c.wait()
 
 
 def attention(chips, reps, cot, seq, ga, gf, gq, gk, cosine, sine, docs, w_qkv, w_out, collective_id):
@@ -833,14 +844,18 @@
             jax.ShapeDtypeStruct((tok, width), BF),
         ),
         in_specs=[anywhere] + [vmem] * 9 + [anywhere] * 2,
-        out_specs=(anywhere,) + (vmem,) * 5,
+        out_specs=(anywhere,) * 4 + (vmem,) * 2,
         scratch_shapes=[
             pltpu.VMEM(w_qkv.shape, BF),
             pltpu.VMEM(w_out.shape, BF),
             pltpu.VMEM((reps - 1, tok, width), BF),
             pltpu.VMEM((reps - 1, tok, width), BF),
+            pltpu.VMEM((seq_len, width), BF),
+            pltpu.VMEM((seq_len, 3 * heads * HD), F32),
+            pltpu.VMEM((seq_len, heads * HD), BF),
             *ring_sems(chips),
             DMA((2, reps - 1)),
+            DMA((3,)),
             DMA((3,)),
         ],
         compiler_params=pltpu.CompilerParams(
@@ -943,15 +958,17 @@
     chips, split_out, h1_ref, grad_ref, ob_ref, mid_ref, gains_ref, qkv_ref, out_ref, gain_ref, *scratch
 ):
     hops = Hops(chips)
-    scratches = [scratch[9 * i : 9 * i + 9] for i in range(3)]
+    scratches = [scratch[9 * i : 9 * i + 9] for i in range(4)]
     hops.meet(2 if split_out else 1)
     first = hops.core == 0
     if split_out:
-        q_sum, q_came, o_sum, o_came, o_give, o_got, g_sum, g_came, rep_sem, flip_sem = scratch[27:]
+        q_sum, q_came, o_sum, o_came, o_give, o_got, g_sum, g_came, rep_sem, flip_sem = scratch[36:]
     else:
         q_sum, o_sum, g_sum = qkv_ref, out_ref, gain_ref
 
     def product(left_ref, right_ref, rows, width):
+        step = 512 if width % 512 == 0 else 256
+
         def produce(d, same_ref, other_ref):
             columns = pl.ds(pl.multiple_of(2 * rows * hops.chip(d), 2 * rows), 2 * rows)
             left = left_ref[:, columns]
@@ -962,7 +979,7 @@
                 same_ref[:, at] = jnp.where(first, low, high)
                 other_ref[:, at] = jnp.where(first, high, low).astype(BF)
 
-            tiles(width // 512, 512, block)
+            tiles(width // step, step, block)
 
         return produce
 
@@ -980,44 +997,55 @@
     def ring(produce, ref, bufs):
         return hops.scatter(ref.shape[0], produce, *bufs, into(ref))
 
-    rings = [ring(product(h1_ref, grad_ref, *q_sum.shape), q_sum, scratches[0])]
+    shard, wide = q_sum.shape
+    replica = lax.axis_index("rep")
+    halves = [pl.ds(0, wide // 2), pl.ds(wide // 2, wide // 2)]
     if split_out:
-        rings.insert(0, ring(product(ob_ref, mid_ref, *o_sum.shape), o_sum, scratches[1]))
-    rings.append(ring(small, g_sum, scratches[2]))
+        pairs = [(o_sum, o_came), *((q_sum.at[:, h], q_came.at[:, h]) for h in halves), (g_sum, g_came)]
+        swaps = [
+            pltpu.make_async_remote_copy(
+                src_ref=src,
+                dst_ref=dst,
+                send_sem=rep_sem.at[0, i],
+                recv_sem=rep_sem.at[1, i],
+                device_id={"rep": 1 - replica},
+                device_id_type=MESH,
+            )
+            for i, (src, dst) in enumerate(pairs)
+        ]
+
+    def then_swap(ring_steps, i):
+        yield from ring_steps
+        if split_out:
+            swaps[i].start()
+
+    rings = []
+    if split_out:
+        steps = ring(product(ob_ref, mid_ref, *o_sum.shape), o_sum, scratches[2])
+        rings.append(then_swap(steps, 0))
+    for i, h in enumerate(halves):
+        part = product(h1_ref, grad_ref.at[:, h], shard, wide // 2)
+        rings.append(then_swap(ring(part, q_sum.at[:, h], scratches[i]), 1 + i))
+    rings.append(then_swap(ring(small, g_sum, scratches[3]), 3))
     hops.turn(*rings)
     if not split_out:
         return
 
-    replica = lax.axis_index("rep")
-    pairs = ((o_sum, o_came), (q_sum, q_came), (g_sum, g_came))
-    swaps = [
-        pltpu.make_async_remote_copy(
-            src_ref=src,
-            dst_ref=dst,
-            send_sem=rep_sem.at[0, i],
-            recv_sem=rep_sem.at[1, i],
-            device_id={"rep": 1 - replica},
-            device_id_type=MESH,
-        )
-        for i, (src, dst) in enumerate(pairs)
-    ]
-    for c in swaps:
-        c.start()
     mine = hops.core == replica
     swaps[0].wait()
     o_give[...] = jnp.where(mine, o_came[...], o_sum[...])
     give = hops.copy(o_give, o_got, flip_sem.at[0], flip_sem.at[1], hops.flip)
     give.start()
     keep = jnp.where(mine, o_sum[...], o_came[...])
-    swaps[2].wait()
-    gain_ref[...] = g_sum[...] + g_came[...]
-    swaps[1].wait()
-    _, wide = q_sum.shape
     even = replica == 0
     for i in range(wide // HD):
+        if i * HD == 0 or i * HD == wide // 2:
+            swaps[1 + (i > 0)].wait()
         own, came = q_sum[:, pl.ds(i * HD, HD)], q_came[:, pl.ds(i * HD, HD)]
         qkv_ref[:, pl.ds(2 * i * HD, HD)] = jnp.where(even, own, came).astype(F32)
         qkv_ref[:, pl.ds((2 * i + 1) * HD, HD)] = jnp.where(even, came, own).astype(F32)
+    swaps[3].wait()
+    gain_ref[...] = g_sum[...] + g_came[...]
     give.wait()
     half = o_sum.shape[0]
     got = o_got[...]
@@ -1032,11 +1060,11 @@
     vmem = pl.BlockSpec(memory_space=pltpu.VMEM)
     shapes = ((shard, width), (half, D), gain_blocks.shape[1:])
     scratch = []
-    for rows, columns in shapes:
+    for rows, columns in ((shard, width // 2), (shard, width // 2), *shapes[1:]):
         scratch += [*scatter_scratch(chips, rows, columns), *ring_sems(chips)]
     if split_out:
         scratch += [pltpu.VMEM(shapes[0], BF)] * 2 + [pltpu.VMEM(shapes[1], BF)] * 4
-        scratch += [pltpu.VMEM(shapes[2], F32)] * 2 + [DMA((2, 3)), DMA((2,))]
+        scratch += [pltpu.VMEM(shapes[2], F32)] * 2 + [DMA((2, 4)), DMA((2,))]
         shapes = ((shard, 2 * width), (2 * half, D), shapes[2])
     kinds = (F32, F32, F32) if split_out else (BF, BF, F32)
     return pl.pallas_call(

time: 815 us -> 790 us (0.969)
  Pallas kernels: 641 us -> 617 us
    pallas_call x1, Pallas kernels: 116 us -> 101 us  [dense_gradients(): pl.pallas_call(functools.partial(dense_gradients_kernel, chips, split_out...]
  transfers between devices with their start and end apart: 4 -> 4, of which waited for: 1 -> 1; matrix products, arithmetic and copies ran while one was open for 6% -> 6% of each run, Pallas kernels for 31% -> 30%
where the time goes in v5:
time: 790 us; the launch traced here: 782 us
  Pallas kernels  617 us (78%)
  waiting for transfers between devices  91.3 us (12%)
  other arithmetic  35.6 us (5%)
  local copies, waits for them, and re-layouts  18.2 us (2%)
  matrix products  14.7 us (2%)
    pallas_call x1, Pallas kernels, outputs(): pl.pallas_call(functools.partial(outputs_kernel, chips, cap), out_shape=(...  103 us
    pallas_call x1, Pallas kernels, dense_gradients(): pl.pallas_call(functools.partial(dense_gradients_kernel, chips, split_out...  101 us
    pallas_call x1, Pallas kernels, rows_back(): pl.pallas_call(functools.partial(rows_back_kernel, chips, cap), out_shape...  96.3 us
    pallas_call x1, Pallas kernels, expert_rows(): pl.pallas_call(functools.partial(experts_kernel, chips, cap), out_shape=(...  94.6 us
    pallas_call x1, Pallas kernels, attention(): pl.pallas_call(functools.partial(attention_kernel, chips, reps, heads), o...  93.7 us
    pallas_call x1, Pallas kernels, start(): pl.pallas_call(functools.partial(start_kernel, chips, reps, heads, split_...  92.5 us
    ppermute x3, waiting for transfers between devices, from_rep(): return lax.ppermute(v, 'rep', [((s + k) % reps, s) for s in range(reps)])  91.3 us
    pallas_call x1, Pallas kernels, attention_back(): pl.pallas_call(functools.partial(attention_back_kernel, heads), out_shape...  35.4 us
  transfers between devices with their start and end apart: 4, of which 1 were waited for; matrix products, arithmetic and copies ran while one was open for 6% of the time, Pallas kernels for 30%

profile of v5, /device:TPU:0, one launch (start us, length us, event | category | flops | bytes accessed | tf_op | source)
XLA Modules:
  0.0 782.2 jit_solution(5422074735942004560)
XLA Ops:
  0.6 0.7 pad_convert_fusion
  1.3 0.8 select_reduce_fusion
  2.2 0.7 maximum_maximum_fusion.small_ref
  2.9 92.5 %start.1 = (bf16[2,256,2048]{2,1,0:T(8,128)(2,1)}, f32[16,32,256]{2,1,0:T(8,128)}, bf16[16,128,3072]{2,1,0:T(8,128)(2,1)}, bf16[8,128,2048]{2,1,0:T(8,128)(2,1)}) custom-call(bf16[256,2048]{1,0:T(8,128)(2,1)} %bitcast.71, f32[32,256]{1,0:T(8,128)} %maximum_maximum_fusion.small_ref, bf16[128,6144]{1,0:T(8,128)(2,1)} %wq_ref.1, bf16[128,2048]{1,0:T(8,128)(2,1)} %wo_ref.1), custom_call_target="tpu_custom_call" | custom-call | bytes 209715200 | tf_op jit(solution)/shard_map/start/pallas_call | solution.py:1173
  95.4 0.9 slice.37
  96.3 0.1 reshape.122
  96.4 0.6 fusion.7
  97.0 0.6 slice_bitcast_fusion
  97.6 0.9 constant_dynamic-slice_fusion
  98.5 0.1 copy.42
  98.6 0.6 copy.53
  99.3 0.2 fusion.2
  99.5 0.7 copy.44.slot_ref
  100.2 0.7 convert_bitcast_fusion.slot_ref
  100.9 0.8 copy.41.dc_ref
  101.8 0.8 constant_dynamic-slice_fusion.1
  102.6 93.7 %attention.1 = (bf16[16,256,2048]{2,1,0:T(8,128)(2,1)}, bf16[512,2048]{1,0:T(8,128)(2,1)}, f32[512,3072]{1,0:T(8,128)}, bf16[512,1024]{1,0:T(8,128)(2,1)}, f32[2...) custom-call(bf16[256,2048]{1,0:T(8,128)(2,1)} %bitcast.68, bf16[512,2048]{1,0:T(8,128)(2,1)} %bitcast.70, f32[1,2048]{1,0:T(1,128)} %bitcast.77, ...), custom_call_target="tpu_custom_call" | custom-call | flops 6442450944 | bytes 104857600 | tf_op jit(solution)/shard_map/attention/pallas_call | solution.py:836
  196.4 94.6 %experts.1 = (bf16[8,288,2048]{2,1,0:T(8,128)(2,1)}, bf16[8,288,2048]{2,1,0:T(8,128)(2,1)}, bf16[8,288,1024]{2,1,0:T(8,128)(2,1)}, bf16[8,288,1024]{2,1,0:T(8,128)(2,1)}, bf16[8,288,1024]{2,1,0:T(8,128)(2,1)}) custom-call(bf16[256,2048]{1,0:T(8,128)(2,1)} %get-tuple-element.52.h2_ref, bf16[16,256,2048]{2,1,0:T(8,128)(2,1)} %get-tuple-element.53.dy_ref, ...), custom_call_target="tpu_custom_call" | custom-call | flops 28991029248 | bytes 209715200 | tf_op jit(solution)/shard_map/experts/pallas_call | solution.py:421
  291.0 103.5 %outputs.1 = (f32[256,2048]{1,0:T(8,128)}, bf16[1024,2048]{1,0:T(8,128)(2,1)}, bf16[1024,2048]{1,0:T(8,128)(2,1)}, bf16[2048,1024]{1,0:T(8,128)(2,1)}, bf16[2048,1024]{1,0:T(8,128)(2,1)}) custom-call(bf16[2304,1024]{1,0:T(8,128)(2,1)} %bitcast.104, bf16[2304,2048]{1,0:T(8,128)(2,1)} %bitcast.100, bf16[2304,2048]{1,0:T(8,128)(2,1)} %bitcast.101, ...), custom_call_target="tpu_custom_call" | custom-call | flops 38654705664 | bytes 209715200 | tf_op jit(solution)/shard_map/outputs/pallas_call | solution.py:592
  394.5 2.0 collective-permute-start.3
  396.6 96.3 %rows_back.1 = f32[256,2048]{1,0:T(8,128)} custom-call(bf16[8,288,1024]{2,1,0:T(8,128)(2,1)} %get-tuple-element.62.dg_ref, bf16[8,288,1024]{2,1,0:T(8,128)(2,1)} %get-tuple-element.63.du_ref, f32[256,16]{1,0:T(8,128)} %convert_bitcast_fusion.slot_ref, bf16[2048,1024]{1,0:T(8,128)(2,1)} %bitcast.95, bf16[2048,1024]{1,0:T(8,128)(2,1)} %bitcast.97), custom_call_target="tpu_custom_call" | custom-call | flops 28991029248 | bytes 209715200 | tf_op jit(solution)/shard_map/rows_back/pallas_call | solution.py:681
  492.9 0.2 multiply_reduce_fusion.5
  493.1 1.3 copy-done.1
  494.5 0.6 multiply_reduce_fusion.2
  495.1 0.6 copy-done.4
  495.7 0.7 fusion.6
  496.4 1.2 collective-permute-start
  497.5 1.6 add.68
  499.2 0.5 multiply_reduce_fusion.1
  499.7 0.9 copy-done.7
  500.6 1.2 copy-done.8
  501.8 5.3 convert_add_fusion.1
  507.1 91.2 %collective-permute-done = bf16[256,2048]{1,0:T(8,128)(2,1)S(1)} collective-permute-done((bf16[256,2048]{1,0:T(8,128)(2,1)S(1)}, bf16[256,2048]{1,0:T(8,128)(2,1)S(1)}, u32[]{:S(2)}, u32[]{:S(2)}) %collective-permute-start) | collective-permute-done | bytes 1048608 | tf_op jit(solution)/shard_map/ppermute | solution.py:1216
  598.3 1.5 pad_maximum_fusion.mid_ref
  599.8 7.6 convert_add_fusion
  607.4 35.4 %attention_back.1 = (bf16[512,3072]{1,0:T(8,128)(2,1)}, f32[1,128]{1,0:T(1,128)}, f32[1,128]{1,0:T(1,128)}) custom-call(f32[512,3072]{1,0:T(8,128)} %get-tuple-element.72.proj_ref, bf16[512,2048]{1,0:T(8,128)(2,1)} %pad_maximum_fusion.mid_ref, bf16[1024,2048]{1,0:T(8,128)(2,1)} %bitcast.99, f32[1,128]{1,0:T(1,128)} %get-tuple-element.91.gq_ref, ...), custom_call_target="tpu_custom_call" | custom-call | flops 5368709120 | bytes 20971520 | tf_op jit(solution)/shard_map/attention_back/pallas_call | solution.py:931
  642.8 14.5 %multiply_reduce_fusion = (f32[2048]{0:T(1024)S(1)}, f32[512,2048]{1,0:T(8,128)}, f32[512,2048]{1,0:T(8,128)}) fusion(f32[512]{0:T(512)S(1)} %bitcast.86, bf16[2,256,2048]{2,1,0:T(8,128)(2,1)} %get-tuple-element.47, bf16[512,3072]{1,0:T(8,128)(2,1)} %get-tuple-element.74.grad_ref, bf16[2048,3072]{1,0:T(8,128)(2,1)} %bitcast.91), kind=kOutput, calls=%fused_computation.3 | convolution fusion | flops 6446643200 | bytes 26224640 | tf_op jit(solution)/shard_map/te,de->td/dot_general | solution.py:1381
  657.5 0.8 copy.51
  658.2 2.7 slice.70
  660.9 0.3 collective-permute-start.2
  661.2 101.4 %dense_gradients.1 = (f32[128,6144]{1,0:T(8,128)}, f32[128,2048]{1,0:T(8,128)}, f32[32,128]{1,0:T(8,128)}) custom-call(bf16[512,2048]{1,0:T(8,128)(2,1)} %get-tuple-element.75.h1_ref, bf16[512,3072]{1,0:T(8,128)(2,1)} %get-tuple-element.74.grad_ref, bf16[512,1024]{1,0:T(8,128)(2,1)} %get-tuple-element.76.ob_ref, bf16[512,2048]{1,0:T(8,128)(2,1)} %pad_maximum_fusion.mid_ref, ...), custom_call_target="tpu_custom_call" | custom-call | flops 6442450944 | bytes 209715200 | tf_op jit(solution)/shard_map/dense_gradients/pallas_call | solution.py:1070
  762.6 1.3 slice.57
  763.9 9.1 %add_bitcast_fusion = f32[1,2048,1024]{2,1,0:T(8,128)} fusion(bf16[2048,1024]{1,0:T(8,128)(2,1)} %collective-permute-done.3, bf16[2048,1024]{1,0:T(8,128)(2,1)} %get-tuple-element.83), kind=kLoop, calls=%fused_computation | loop fusion | flops 6291456 | bytes 16777216 | tf_op jit(solution)/shard_map/broadcast_in_dim | solution.py:1438
  773.0 1.8 multiply_reduce_fusion.3
  774.9 3.9 add_bitcast_fusion.1
  778.8 1.7 copy.56
  780.5 0.3 copy-done.12
  780.8 1.0 copy.57
  (59 shorter events, 0.5 us)
Async XLA Ops:
  2.9 98.0 %copy-start.19 = (s32[1,512]{1,0:T(1,128)S(1)}, s32[1,512]{1,0:T(1,128)}, u32[]{:S(2)}) copy-start(s32[1,512]{1,0:T(1,128)} %param.20) | copy-start | bytes 6148
  2.9 98.9 %copy-start.14 = (f32[1024,128]{1,0:T(8,128)S(1)}, f32[1024,128]{1,0:T(8,128)}, u32[]{:S(2)}) copy-start(f32[1024,128]{1,0:T(8,128)} %constant.59) | copy-start | bytes 1572868
  2.9 98.9 %copy-start.15 = (f32[1024,128]{1,0:T(8,128)S(1)}, f32[1024,128]{1,0:T(8,128)}, u32[]{:S(2)}) copy-start(f32[1024,128]{1,0:T(8,128)} %constant.60) | copy-start | bytes 1572868
  98.6 97.7 %copy-start.13 = (f32[16,1,256]{0,2,1:T(8,128)}, f32[16,1,256]{0,2,1:T(8,128)S(1)}, u32[]{:S(2)}) copy-start(f32[16,1,256]{0,2,1:T(8,128)S(1)} %copy.42) | copy-start | bytes 49156
  100.9 1.7 copy-start.18
  394.5 205.3 %collective-permute-start.1 = (bf16[2048,1024]{1,0:T(8,128)(2,1)}, bf16[2048,1024]{1,0:T(8,128)(2,1)}, u32[]{:S(2)}, u32[]{:S(2)}) collective-permute-start(bf16[2048,1024]{1,0:T(8,128)(2,1)} %get-tuple-element.69), channel_id=1, source_target_pairs={{16,0},{0,16},{17,1},{1,17},{18,2},{2,18},{19,3},{3,19},{20,4},{4,... | collective-permute-start | bytes 12582920 | tf_op jit(solution)/shard_map/ppermute | solution.py:1216
  394.5 368.1 %collective-permute-start.3 = (bf16[2048,1024]{1,0:T(8,128)(2,1)}, bf16[2048,1024]{1,0:T(8,128)(2,1)}, u32[]{:S(2)}, u32[]{:S(2)}) collective-permute-start(bf16[2048,1024]{1,0:T(8,128)(2,1)} %get-tuple-element.83), channel_id=1, source_target_pairs={{16,0},{0,16},{17,1},{1,17},{18,2},{2,18},{19,3},{3,19},{20,4},{4,... | collective-permute-start | bytes 12582920 | tf_op jit(solution)/shard_map/ppermute | solution.py:1216
  396.5 96.3 %copy-start = (f32[256,2048]{1,0:T(8,128)S(1)}, f32[256,2048]{1,0:T(8,128)}, u32[]{:S(2)}) copy-start(f32[256,2048]{1,0:T(8,128)} %get-tuple-element.51) | copy-start | bytes 6291460
  396.6 96.6 %copy-start.16 = (f32[2048]{0:T(1024)S(1)}, f32[2048]{0:T(1024)}, u32[]{:S(2)}) copy-start(f32[2048]{0:T(1024)} %get-tuple-element.92) | copy-start | bytes 24580
  492.9 1.6 copy-start.1
  494.5 1.2 copy-start.4
  495.7 1.8 copy-start.10
  495.7 3.5 copy-start.11
  496.4 102.0 %collective-permute-start = (bf16[256,2048]{1,0:T(8,128)(2,1)S(1)}, bf16[256,2048]{1,0:T(8,128)(2,1)S(1)}, u32[]{:S(2)}, u32[]{:S(2)}) collective-permute-start(bf16[256,2048]{1,0:T(8,128)(2,1)S(1)} %fusion.6), channel_id=1, source_target_pairs={{16,0},{0,16},{17,1},{1,17},{18,2},{2,18},{19,3},{3,19},{20,4},{4,... | collective-permute-start | bytes 3145736 | tf_op jit(solution)/shard_map/ppermute | solution.py:1216
  497.5 3.0 copy-start.7
  497.5 4.2 copy-start.8
  507.1 92.7 %copy-start.6 = (bf16[2048,1024]{1,0:T(8,128)(2,1)S(1)}, bf16[2048,1024]{1,0:T(8,128)(2,1)}, u32[]{:S(2)}) copy-start(bf16[2048,1024]{1,0:T(8,128)(2,1)} %get-tuple-element.69) | copy-start | bytes 12582916
  642.8 14.5 %copy-start.20 = (f32[1,128]{1,0:T(1,128)S(1)}, f32[1,128]{1,0:T(1,128)}, u32[]{:S(2)}) copy-start(f32[1,128]{1,0:T(1,128)} %get-tuple-element.77) | copy-start | bytes 1540
  642.8 14.5 %copy-start.21 = (f32[1,128]{1,0:T(1,128)S(1)}, f32[1,128]{1,0:T(1,128)}, u32[]{:S(2)}) copy-start(f32[1,128]{1,0:T(1,128)} %get-tuple-element.78) | copy-start | bytes 1540
  660.9 112.0 %collective-permute-start.2 = (bf16[256,2048]{1,0:T(8,128)(2,1)}, bf16[256,2048]{1,0:T(8,128)(2,1)}, u32[]{:S(2)}, u32[]{:S(2)}) collective-permute-start(bf16[256,2048]{1,0:T(8,128)(2,1)} %slice.70), channel_id=1, source_target_pairs={{0,16},{16,0},{1,17},{17,1},{2,18},{18,2},{3,19},{19,3},{4,20},{20... | collective-permute-start | bytes 3145736 | tf_op jit(solution)/shard_map/ppermute | solution.py:1219
  763.9 9.1 %copy-start.3 = (f32[512,2048]{1,0:T(8,128)S(1)}, f32[512,2048]{1,0:T(8,128)}, u32[]{:S(2)}) copy-start(f32[512,2048]{1,0:T(8,128)} %get-tuple-element.96) | copy-start | bytes 12582916
  763.9 9.1 %copy-start.5 = (f32[512,2048]{1,0:T(8,128)S(1)}, f32[512,2048]{1,0:T(8,128)}, u32[]{:S(2)}) copy-start(f32[512,2048]{1,0:T(8,128)} %get-tuple-element.89) | copy-start | bytes 12582916
  763.9 9.1 %copy-start.17 = (f32[2048]{0:T(1024)S(1)}, f32[2048]{0:T(1024)}, u32[]{:S(2)}) copy-start(f32[2048]{0:T(1024)} %get-tuple-element.93) | copy-start | bytes 24580
  773.0 1.9 copy-start.2
  774.9 3.9 copy-start.9
  778.8 2.0 copy-start.12

commit v6 on v5

--- a/solution.py
+++ b/solution.py
@@ -513,16 +513,17 @@
         at = pl.ds(jobs[n][3] * strip, strip)
         return pltpu.make_async_copy(jobs[n][1].at[:, at], right.at[n % 2], right_sem.at[n % 2])
 
+    def left_copy(n):
+        return pltpu.make_async_copy(jobs[n][0], left, left_sem)
+
     def job():
         n = len(done)
         if n == len(jobs):
             return
         done.append(n)
-        thin, _, result, i = jobs[n]
+        _, _, result, i = jobs[n]
         if i == 0:
-            fresh = pltpu.make_async_copy(thin, left, left_sem)
-            fresh.start()
-            fresh.wait()
+            left_copy(n).wait()
         right_copy(n).wait()
         if n + 1 < len(jobs):
             right_copy(n + 1).start()
@@ -546,6 +547,8 @@
             made[n % 2] = dot_tn(right[n % 2], left[...]).astype(BF)
             stored[n] = pltpu.make_async_copy(made.at[n % 2], result.at[at, :], made_sem.at[n % 2])
         stored[n].start()
+        if i == count - 1 and n + 1 < len(jobs):
+            left_copy(n + 1).start()
 
     def produce(d, same_ref, other_ref):
         i = number[d]
@@ -563,13 +566,14 @@
         total_ref[at, :] = value
 
     load = pltpu.make_async_copy(wd_hbm, wd, w_sem)
+    left_copy(0).start()
+    right_copy(0).start()
+    act_copy(0).start()
     load.start()
-    act_copy(0).start()
-    right_copy(0).start()
     hops.meet(2)
-    load.wait()
     ring = hops.scatter(tok, produce, mine, out, came, far, up_in, down_in, up, down, side, finish)
     job()
+    load.wait()
     share = -(-(len(jobs) - 2) // (chips // 2 - 1))
     for step in range(chips // 2):
         next(ring)
@@ -870,11 +874,13 @@
 
 def attention_back_kernel(
     heads,
-    proj_ref, mid_ref, wo_ref, gq_ref, gk_ref, cos_ref, sin_ref, dc_ref, dr_ref,
-    grad_ref, qt_ref, kt_ref,
-    dob, dk, dv,
+    proj_ref, mid_ref, wo_ref, seq_ref, gq_ref, gk_ref, cos_ref, sin_ref, dc_ref, dr_ref, wq_hbm,
+    grad_ref, qt_ref, kt_ref, own_ref, rest_ref, at_ref,
+    dob, dk, dv, wq, scale_b, w_sem,
 ):
     seq_len = proj_ref.shape[0]
+    load = pltpu.make_async_copy(wq_hbm, wq, w_sem)
+    load.start()
     block = min(256, seq_len)
     scale = HD ** (-0.5)
     for i in range(heads * HD // 512):
@@ -923,8 +929,26 @@
 
     lax.fori_loop(0, heads, one, 0)
 
-
-def attention_back(proj, mid, w_out, gq, gk, cosine, sine, docs):
+    tok = own_ref.shape[0]
+
+    def inverses(i, carry):
+        rows = pl.ds(pl.multiple_of(i * 64, 64), 64)
+        v = seq_ref[rows, :].astype(F32)
+        scale_b[rows, :] = lax.rsqrt(jnp.mean(v * v, axis=-1, keepdims=True) + epsilon)
+        return carry
+
+    lax.fori_loop(0, seq_len // 64, inverses, 0)
+    load.wait()
+    for i in range(wq.shape[0] // 256):
+        at = pl.ds(i * 256, 256)
+        part = dot_nt(grad_ref[...], wq[at, :])
+        own_ref[:, at] = part[:tok]
+        rest_ref[:, at] = part[tok:].astype(BF)
+        hat = seq_ref[:, at].astype(F32) * scale_b[...]
+        at_ref[:, at] = jnp.sum(part * hat, axis=0, keepdims=True)
+
+
+def attention_back(tok, proj, mid, w_out, seq, gq, gk, cosine, sine, docs, w_qkv):
     seq_len = proj.shape[0]
     heads = w_out.shape[0] // HD
     vmem = pl.BlockSpec(memory_space=pltpu.VMEM)
@@ -934,20 +958,26 @@
             jax.ShapeDtypeStruct(proj.shape, BF),
             jax.ShapeDtypeStruct((1, HD), F32),
             jax.ShapeDtypeStruct((1, HD), F32),
-        ),
-        in_specs=[vmem] * 9,
-        out_specs=(vmem,) * 3,
+            jax.ShapeDtypeStruct((tok, D), F32),
+            jax.ShapeDtypeStruct((seq_len - tok, D), BF),
+            jax.ShapeDtypeStruct((1, D), F32),
+        ),
+        in_specs=[vmem] * 10 + [pl.BlockSpec(memory_space=pl.ANY)],
+        out_specs=(vmem,) * 6,
         scratch_shapes=[
             pltpu.VMEM((seq_len, heads * HD), BF),
             pltpu.VMEM((seq_len, HD), F32),
             pltpu.VMEM((seq_len, HD), F32),
+            pltpu.VMEM(w_qkv.shape, BF),
+            pltpu.VMEM((seq_len, 1), F32),
+            DMA,
         ],
         compiler_params=pltpu.CompilerParams(vmem_limit_bytes=VMEM_LIMIT),
         cost_estimate=pl.CostEstimate(
             flops=20 * heads * seq_len * seq_len * HD, transcendentals=0, bytes_accessed=20 << 20
         ),
         name="attention_back",
-    )(proj, mid, w_out, gq, gk, cosine, sine, docs[:, None], docs[None, :])
+    )(proj, mid, w_out, seq, gq, gk, cosine, sine, docs[:, None], docs[None, :], w_qkv)
 
 
 def ring_sems(chips):
@@ -1221,13 +1251,6 @@
     def rep_gather(v):
         return jnp.concatenate([v] + [from_rep(v, k) for k in range(1, reps)], axis=0)
 
-    def rep_scatter(v):
-        parts = v.reshape(reps, tok_rows, v.shape[-1])
-        out = parts[0].astype(F32)
-        for k in range(1, reps):
-            out = out + to_rep(parts[k].astype(BF), k).astype(F32)
-        return out
-
     own_b = tokens[0]
     gates_f = gate_weights[0]
     experts = jnp.arange(groups, dtype=jnp.int32)
@@ -1374,18 +1397,19 @@
     (grad_branch_b, result, grad_wdown, grad_wgate), _ = lax.optimization_barrier(
         ((grad_branch_b, result, grad_wdown, grad_wgate), grad_mid_b)
     )
-    grad_proj, query_terms, key_terms = attention_back(
-        projected, grad_branch_b, my_out, g_query, g_key, cosine, sine, docs
-    )
-    _, hat_one, inv_one = rms_forward(seq_b.astype(F32), g_attn)
-    grad_h1_part = jnp.einsum("te,de->td", grad_proj, full_qkv, preferred_element_type=F32)
-    attn_terms = grad_h1_part * hat_one
-    grad_h1 = rep_scatter(grad_h1_part)
-    grad_rows_one, _ = rms_backward(grad_h1, hat_one[:tok_rows], inv_one[:tok_rows], g_attn)
+    grad_proj, query_terms, key_terms, grad_h1, rest, attn_terms = attention_back(
+        tok_rows, projected, grad_branch_b, my_out, seq_b, g_query, g_key, cosine, sine, docs,
+        full_qkv,
+    )
+    for k in range(1, reps):
+        part = rest[(k - 1) * tok_rows : k * tok_rows]
+        grad_h1 = grad_h1 + to_rep(part, k).astype(F32)
+    _, hat_one, inv_one = rms_forward(own_b.astype(F32), g_attn)
+    grad_rows_one, _ = rms_backward(grad_h1, hat_one, inv_one, g_attn)
     grad_tokens = grad_mid + grad_rows_one
     grad_gains = jnp.concatenate(
         [
-            jnp.sum(attn_terms, axis=0),
+            attn_terms[0],
             jnp.sum(ffn_terms, axis=0),
             query_terms[0],
             key_terms[0],

time: 790 us -> 782 us (0.990)
  matrix products: 14.7 us -> 0.19 us
  Pallas kernels: 617 us -> 626 us
    dot_general x1 -> x0, matrix products: 14.5 us -> none  [per_device(): jnp.einsum('te,de->td', grad_proj, full_qkv, preferred_element_type=F32)]
    pallas_call x1, Pallas kernels: 35.4 us -> 45.1 us  [attention_back(): pl.pallas_call(functools.partial(attention_back_kernel, heads), out_shape...]
  transfers between devices with their start and end apart: 4 -> 4, of which waited for: 1 -> 1; matrix products, arithmetic and copies ran while one was open for 6% -> 4% of each run, Pallas kernels for 30% -> 31%
where the time goes in v6:
time: 782 us; the launch traced here: 774 us
  Pallas kernels  626 us (80%)
  waiting for transfers between devices  90.4 us (12%)
  other arithmetic  39.6 us (5%)
  local copies, waits for them, and re-layouts  13.3 us (2%)
    pallas_call x1, Pallas kernels, outputs(): pl.pallas_call(functools.partial(outputs_kernel, chips, cap), out_shape=(...  102 us
    pallas_call x1, Pallas kernels, dense_gradients(): pl.pallas_call(functools.partial(dense_gradients_kernel, chips, split_out...  101 us
    pallas_call x1, Pallas kernels, rows_back(): pl.pallas_call(functools.partial(rows_back_kernel, chips, cap), out_shape...  96.4 us
    pallas_call x1, Pallas kernels, expert_rows(): pl.pallas_call(functools.partial(experts_kernel, chips, cap), out_shape=(...  94.6 us
    pallas_call x1, Pallas kernels, attention(): pl.pallas_call(functools.partial(attention_kernel, chips, reps, heads), o...  93.7 us
    pallas_call x1, Pallas kernels, start(): pl.pallas_call(functools.partial(start_kernel, chips, reps, heads, split_...  92.5 us
    ppermute x3, waiting for transfers between devices, from_rep(): return lax.ppermute(v, 'rep', [((s + k) % reps, s) for s in range(reps)])  90.4 us
    pallas_call x1, Pallas kernels, attention_back(): pl.pallas_call(functools.partial(attention_back_kernel, heads), out_shape...  45.1 us
  transfers between devices with their start and end apart: 4, of which 1 were waited for; matrix products, arithmetic and copies ran while one was open for 4% of the time, Pallas kernels for 31%

profile of v6, /device:TPU:0, one launch (start us, length us, event | category | flops | bytes accessed | tf_op | source)
XLA Modules:
  0.0 774.0 jit_solution(7150718906257545462)
XLA Ops:
  0.6 0.7 pad_convert_fusion
  1.3 0.8 select_reduce_fusion
  2.2 0.7 maximum_maximum_fusion.small_ref
  2.9 92.5 %start.1 = (bf16[2,256,2048]{2,1,0:T(8,128)(2,1)}, f32[16,32,256]{2,1,0:T(8,128)}, bf16[16,128,3072]{2,1,0:T(8,128)(2,1)}, bf16[8,128,2048]{2,1,0:T(8,128)(2,1)}) custom-call(bf16[256,2048]{1,0:T(8,128)(2,1)} %bitcast.61, f32[32,256]{1,0:T(8,128)} %maximum_maximum_fusion.small_ref, bf16[128,6144]{1,0:T(8,128)(2,1)} %wq_ref.1, bf16[128,2048]{1,0:T(8,128)(2,1)} %wo_ref.1), custom_call_target="tpu_custom_call" | custom-call | bytes 209715200 | tf_op jit(solution)/shard_map/start/pallas_call | solution.py:1203
  95.4 0.9 slice.21
  96.3 0.1 reshape.91
  96.4 0.6 fusion.13
  97.0 0.6 slice_bitcast_fusion
  97.6 0.9 constant_dynamic-slice_fusion
  98.5 0.1 copy.42
  98.6 0.6 copy.52
  99.3 0.2 fusion.9
  99.5 0.7 copy.44.slot_ref
  100.2 0.7 convert_bitcast_fusion.slot_ref
  100.8 0.1 dynamic_slice.15
  100.9 0.9 copy.41.dc_ref
  101.8 0.8 constant_dynamic-slice_fusion.1
  102.6 93.7 %attention.1 = (bf16[16,256,2048]{2,1,0:T(8,128)(2,1)}, bf16[512,2048]{1,0:T(8,128)(2,1)}, f32[512,3072]{1,0:T(8,128)}, bf16[512,1024]{1,0:T(8,128)(2,1)}, f32[2...) custom-call(bf16[256,2048]{1,0:T(8,128)(2,1)} %bitcast.68, bf16[512,2048]{1,0:T(8,128)(2,1)} %bitcast.69, f32[1,2048]{1,0:T(1,128)} %bitcast.77, ...), custom_call_target="tpu_custom_call" | custom-call | flops 6442450944 | bytes 104857600 | tf_op jit(solution)/shard_map/attention/pallas_call | solution.py:840
  196.4 94.6 %experts.1 = (bf16[8,288,2048]{2,1,0:T(8,128)(2,1)}, bf16[8,288,2048]{2,1,0:T(8,128)(2,1)}, bf16[8,288,1024]{2,1,0:T(8,128)(2,1)}, bf16[8,288,1024]{2,1,0:T(8,128)(2,1)}, bf16[8,288,1024]{2,1,0:T(8,128)(2,1)}) custom-call(bf16[256,2048]{1,0:T(8,128)(2,1)} %get-tuple-element.55.h2_ref, bf16[16,256,2048]{2,1,0:T(8,128)(2,1)} %get-tuple-element.56.dy_ref, ...), custom_call_target="tpu_custom_call" | custom-call | flops 28991029248 | bytes 209715200 | tf_op jit(solution)/shard_map/experts/pallas_call | solution.py:421
  291.0 101.8 %outputs.1 = (f32[256,2048]{1,0:T(8,128)}, bf16[1024,2048]{1,0:T(8,128)(2,1)}, bf16[1024,2048]{1,0:T(8,128)(2,1)}, bf16[2048,1024]{1,0:T(8,128)(2,1)}, bf16[2048,1024]{1,0:T(8,128)(2,1)}) custom-call(bf16[2304,1024]{1,0:T(8,128)(2,1)} %bitcast.99, bf16[2304,2048]{1,0:T(8,128)(2,1)} %bitcast.95, bf16[2304,2048]{1,0:T(8,128)(2,1)} %bitcast.96, ...), custom_call_target="tpu_custom_call" | custom-call | flops 38654705664 | bytes 209715200 | tf_op jit(solution)/shard_map/outputs/pallas_call | solution.py:596
  392.9 2.0 collective-permute-start.3
  394.9 1.8 multiply_reduce_fusion.2
  396.7 96.4 %rows_back.1 = f32[256,2048]{1,0:T(8,128)} custom-call(bf16[8,288,1024]{2,1,0:T(8,128)(2,1)} %get-tuple-element.65.dg_ref, bf16[8,288,1024]{2,1,0:T(8,128)(2,1)} %get-tuple-element.66.du_ref, f32[256,16]{1,0:T(8,128)} %convert_bitcast_fusion.slot_ref, bf16[2048,1024]{1,0:T(8,128)(2,1)} %bitcast.92, bf16[2048,1024]{1,0:T(8,128)(2,1)} %bitcast.94), custom_call_target="tpu_custom_call" | custom-call | flops 28991029248 | bytes 209715200 | tf_op jit(solution)/shard_map/rows_back/pallas_call | solution.py:685
  493.2 2.3 multiply_reduce_fusion
  495.5 0.1 copy-done.8
  495.7 0.7 fusion.12
  496.4 1.1 collective-permute-start
  497.5 1.6 add.55
  499.1 0.3 fusion.7
  499.4 1.6 copy-done.6
  501.0 5.3 convert_add_fusion.1
  506.3 90.4 %collective-permute-done = bf16[256,2048]{1,0:T(8,128)(2,1)S(1)} collective-permute-done((bf16[256,2048]{1,0:T(8,128)(2,1)S(1)}, bf16[256,2048]{1,0:T(8,128)(2,1)S(1)}, u32[]{:S(2)}, u32[]{:S(2)}) %collective-permute-start) | collective-permute-done | bytes 1048608 | tf_op jit(solution)/shard_map/ppermute | solution.py:1246
  596.7 1.5 pad_maximum_fusion.mid_ref
  598.1 7.6 convert_add_fusion
  605.7 45.1 %attention_back.1 = (bf16[512,3072]{1,0:T(8,128)(2,1)}, f32[1,128]{1,0:T(1,128)}, f32[1,128]{1,0:T(1,128)}, f32[256,2048]{1,0:T(8,128)}, bf16[256,2048]{1,0:T(8,128)(2,1)}, /*index=5*/f32[1,2048]{1,0:T(1,128)}) custom-call(f32[512,3072]{1,0:T(8,128)} %get-tuple-element.75.proj_ref, bf16[512,2048]{1,0:T(8,128)(2,1)} %pad_maximum_fusion.mid_ref, ...), custom_call_target="tpu_custom_call" | custom-call | flops 5368709120 | bytes 20971520 | tf_op jit(solution)/shard_map/attention_back/pallas_call | solution.py:955
  650.8 0.7 pad_maximum_fusion.1
  651.5 0.1 reshape.99
  651.6 0.8 copy.50
  652.4 0.3 collective-permute-start.2
  652.7 101.4 %dense_gradients.1 = (f32[128,6144]{1,0:T(8,128)}, f32[128,2048]{1,0:T(8,128)}, f32[32,128]{1,0:T(8,128)}) custom-call(bf16[512,2048]{1,0:T(8,128)(2,1)} %get-tuple-element.79.h1_ref, bf16[512,3072]{1,0:T(8,128)(2,1)} %get-tuple-element.80.grad_ref, bf16[512,1024]{1,0:T(8,128)(2,1)} %get-tuple-element.81.ob_ref, bf16[512,2048]{1,0:T(8,128)(2,1)} %pad_maximum_fusion.mid_ref, ...), custom_call_target="tpu_custom_call" | custom-call | flops 6442450944 | bytes 209715200 | tf_op jit(solution)/shard_map/dense_gradients/pallas_call | solution.py:1100
  754.1 1.3 slice.33
  755.4 9.0 %add_bitcast_fusion = f32[1,2048,1024]{2,1,0:T(8,128)} fusion(bf16[2048,1024]{1,0:T(8,128)(2,1)} %collective-permute-done.3, bf16[2048,1024]{1,0:T(8,128)(2,1)} %get-tuple-element.89), kind=kLoop, calls=%fused_computation | loop fusion | flops 6291456 | bytes 16777216 | tf_op jit(solution)/shard_map/broadcast_in_dim | solution.py:1462
  764.4 2.0 fusion.2
  766.4 0.1 copy-done.9
  766.5 4.1 fusion.6
  770.6 1.7 copy.55
  772.3 0.3 copy-done.12
  772.6 1.0 copy.56
  (51 shorter events, 0.3 us)
Async XLA Ops:
  2.9 98.0 %copy-start.19 = (s32[1,512]{1,0:T(1,128)S(1)}, s32[1,512]{1,0:T(1,128)}, u32[]{:S(2)}) copy-start(s32[1,512]{1,0:T(1,128)} %param.20) | copy-start | bytes 6148
  2.9 98.9 %copy-start.14 = (f32[1024,128]{1,0:T(8,128)S(1)}, f32[1024,128]{1,0:T(8,128)}, u32[]{:S(2)}) copy-start(f32[1024,128]{1,0:T(8,128)} %constant.57) | copy-start | bytes 1572868
  2.9 98.9 %copy-start.15 = (f32[1024,128]{1,0:T(8,128)S(1)}, f32[1024,128]{1,0:T(8,128)}, u32[]{:S(2)}) copy-start(f32[1024,128]{1,0:T(8,128)} %constant.58) | copy-start | bytes 1572868
  98.6 97.7 %copy-start.13 = (f32[16,1,256]{0,2,1:T(8,128)}, f32[16,1,256]{0,2,1:T(8,128)S(1)}, u32[]{:S(2)}) copy-start(f32[16,1,256]{0,2,1:T(8,128)S(1)} %copy.42) | copy-start | bytes 49156
  100.9 1.7 copy-start.18
  392.8 205.3 %collective-permute-start.1 = (bf16[2048,1024]{1,0:T(8,128)(2,1)}, bf16[2048,1024]{1,0:T(8,128)(2,1)}, u32[]{:S(2)}, u32[]{:S(2)}) collective-permute-start(bf16[2048,1024]{1,0:T(8,128)(2,1)} %get-tuple-element.72), channel_id=1, source_target_pairs={{16,0},{0,16},{17,1},{1,17},{18,2},{2,18},{19,3},{3,19},{20,4},{4,... | collective-permute-start | bytes 12582920 | tf_op jit(solution)/shard_map/ppermute | solution.py:1246
  392.9 361.2 %collective-permute-start.3 = (bf16[2048,1024]{1,0:T(8,128)(2,1)}, bf16[2048,1024]{1,0:T(8,128)(2,1)}, u32[]{:S(2)}, u32[]{:S(2)}) collective-permute-start(bf16[2048,1024]{1,0:T(8,128)(2,1)} %get-tuple-element.89), channel_id=1, source_target_pairs={{16,0},{0,16},{17,1},{1,17},{18,2},{2,18},{19,3},{3,19},{20,4},{4,... | collective-permute-start | bytes 12582920 | tf_op jit(solution)/shard_map/ppermute | solution.py:1246
  396.7 96.4 %copy-start = (f32[256,2048]{1,0:T(8,128)S(1)}, f32[256,2048]{1,0:T(8,128)}, u32[]{:S(2)}) copy-start(f32[256,2048]{1,0:T(8,128)} %get-tuple-element.54) | copy-start | bytes 6291460
  396.7 96.4 %copy-start.16 = (f32[2048]{0:T(1024)S(1)}, f32[2048]{0:T(1024)}, u32[]{:S(2)}) copy-start(f32[2048]{0:T(1024)} %get-tuple-element.96) | copy-start | bytes 24580
  493.2 2.3 copy-start.1
  493.2 2.5 copy-start.8
  495.7 1.8 copy-start.11
  495.7 3.7 copy-start.7
  496.4 100.3 %collective-permute-start = (bf16[256,2048]{1,0:T(8,128)(2,1)S(1)}, bf16[256,2048]{1,0:T(8,128)(2,1)S(1)}, u32[]{:S(2)}, u32[]{:S(2)}) collective-permute-start(bf16[256,2048]{1,0:T(8,128)(2,1)S(1)} %fusion.12), channel_id=1, source_target_pairs={{16,0},{0,16},{17,1},{1,17},{18,2},{2,18},{19,3},{3,19},{20,4},{4,... | collective-permute-start | bytes 3145736 | tf_op jit(solution)/shard_map/ppermute | solution.py:1246
  497.5 1.6 copy-start.3
  497.5 3.5 copy-start.6
  506.3 91.8 %copy-start.5 = (bf16[2048,1024]{1,0:T(8,128)(2,1)S(1)}, bf16[2048,1024]{1,0:T(8,128)(2,1)}, u32[]{:S(2)}) copy-start(bf16[2048,1024]{1,0:T(8,128)(2,1)} %get-tuple-element.72) | copy-start | bytes 12582916
  652.4 112.0 %collective-permute-start.2 = (bf16[256,2048]{1,0:T(8,128)(2,1)}, bf16[256,2048]{1,0:T(8,128)(2,1)}, u32[]{:S(2)}, u32[]{:S(2)}) collective-permute-start(bf16[256,2048]{1,0:T(8,128)(2,1)} %get-tuple-element.78), channel_id=1, source_target_pairs={{0,16},{16,0},{1,17},{17,1},{2,18},{18,2},{3,19},{19,3},{4,20},{20... | collective-permute-start | bytes 3145736 | tf_op jit(solution)/shard_map/ppermute | solution.py:1249
  755.4 9.0 %copy-start.4 = (f32[256,2048]{1,0:T(8,128)S(1)}, f32[256,2048]{1,0:T(8,128)}, u32[]{:S(2)}) copy-start(f32[256,2048]{1,0:T(8,128)} %get-tuple-element.77) | copy-start | bytes 6291460
  755.4 9.0 %copy-start.17 = (f32[2048]{0:T(1024)S(1)}, f32[2048]{0:T(1024)}, u32[]{:S(2)}) copy-start(f32[2048]{0:T(1024)} %get-tuple-element.97) | copy-start | bytes 24580
  764.4 2.0 copy-start.2
  764.4 2.2 copy-start.9
  766.5 4.1 copy-start.10
  770.6 2.0 copy-start.12

commit v7 on v6

--- a/solution.py
+++ b/solution.py
@@ -327,7 +327,7 @@
     h2_ref, dy_ref, slot_ref, weight_ref, wg_hbm, wu_hbm, wd_hbm,
     xs_ref, de_ref, act_ref, dg_ref, du_ref,
     held, dy, wg, wu, wd, xs_b, de_b, act_b, dg_b, du_b,
-    up, down, side, w_sem, dy_sem, own_sem, out_sem,
+    w_sem, dy_sem, own_sem, out_sem, *sems,
 ):
     hops = Hops(chips)
     half = chips // 2
@@ -405,7 +405,7 @@
         for c in out_copies(i):
             c.start()
 
-    hops.turn(hops.gather([(h2_ref, lambda dev: held.at[dev], up, down, side)], use))
+    hops.turn(hops.gather(in_halves(h2_ref, lambda dev: held.at[dev], sems), use))
     for i in (chips - 2, chips - 1):
         for c in out_copies(i):
             c.wait()
@@ -434,11 +434,12 @@
             pltpu.VMEM((2, 2 * cap, ff), BF),
             pltpu.VMEM((2, 2 * cap, ff), BF),
             pltpu.VMEM((2, 2 * cap, ff), BF),
-            *ring_sems(chips),
             DMA((3,)),
             DMA((2,)),
             DMA,
             DMA((2, 5)),
+            *ring_sems(chips),
+            *ring_sems(chips),
         ],
         compiler_params=pltpu.CompilerParams(
             collective_id=collective_id, has_side_effects=True, vmem_limit_bytes=VMEM_LIMIT
@@ -734,7 +735,7 @@
     chips, reps, heads,
     cot_ref, seq_ref, ga_ref, gf_ref, gq_ref, gk_ref, cos_ref, sin_ref, dc_ref, dr_ref, wq_hbm, wo_hbm,
     dy_ref, h1_out, proj_out, ob_out, mid_ref, h2_ref,
-    wq, wo, give, came, h1_ref, proj_ref, ob_ref, up, down, side, rep_sem, own_sem, out_sem,
+    wq, wo, give, came, h1_ref, proj_ref, ob_ref, rep_sem, own_sem, out_sem, *sems,
 ):
     hops = Hops(chips)
     rep = lax.axis_index("rep")
@@ -746,7 +747,7 @@
         for i, (a, b) in enumerate(((wq_hbm, wq), (wo_hbm, wo), (cot_ref, dy_ref.at[hops.me])))
     ]
     hops.meet(reps)
-    ring = hops.gather([(cot_ref, lambda dev: dy_ref.at[dev], up, down, side)], lambda d: None)
+    ring = hops.gather(in_halves(cot_ref, lambda dev: dy_ref.at[dev], sems), lambda d: None)
     next(ring)
     for c in loads:
         c.start()
@@ -857,10 +858,11 @@
             pltpu.VMEM((seq_len, width), BF),
             pltpu.VMEM((seq_len, 3 * heads * HD), F32),
             pltpu.VMEM((seq_len, heads * HD), BF),
-            *ring_sems(chips),
             DMA((2, reps - 1)),
             DMA((3,)),
             DMA((3,)),
+            *ring_sems(chips),
+            *ring_sems(chips),
         ],
         compiler_params=pltpu.CompilerParams(
             collective_id=collective_id, has_side_effects=True, vmem_limit_bytes=VMEM_LIMIT
@@ -980,6 +982,18 @@
     )(proj, mid, w_out, seq, gq, gk, cosine, sine, docs[:, None], docs[None, :], w_qkv)
 
 
+def in_halves(own, slot, sems):
+    cut = own.shape[0] // 2
+    return [
+        (
+            own.at[pl.ds(i * cut, cut)],
+            lambda dev, i=i: slot(dev).at[pl.ds(i * cut, cut)],
+            *sems[3 * i : 3 * i + 3],
+        )
+        for i in range(2)
+    ]
+
+
 def ring_sems(chips):
     return [DMA((2, chips // 2)), DMA((2, chips // 2)), DMA((2, chips))]
 
@@ -1123,7 +1137,8 @@
 ):
     hops = Hops(chips)
     rep = lax.axis_index("rep")
-    up, down, side, up_s, down_s, side_s, up_o, down_o, side_o, rep_sem, col_sem, own_sem, half_sem = sems
+    sems_q, sems_s, sems_o = sems[:6], sems[6:9], sems[9:12]
+    rep_sem, col_sem, own_sem, half_sem = sems[12:]
     pieces = []
     for i in range(3 * heads):
         q, j = i // heads, i % heads
@@ -1158,8 +1173,8 @@
     mine = pltpu.make_async_copy(own_q, full_ref.at[hops.me], own_sem.at[2])
     mine.start()
     items = [
-        (own_q, lambda dev: full_ref.at[dev], up, down, side),
-        (small_ref, lambda dev: smalls_ref.at[dev], up_s, down_s, side_s),
+        *in_halves(own_q, lambda dev: full_ref.at[dev], sems_q),
+        (small_ref, lambda dev: smalls_ref.at[dev], *sems_s),
     ]
     if split_out:
         rows = own_o.shape[0]
@@ -1184,7 +1199,7 @@
 
         mine_o = pltpu.make_async_copy(own_o, slot(hops.me), half_sem.at[3])
         mine_o.start()
-        items.append((own_o, slot, up_o, down_o, side_o))
+        items.append((own_o, slot, *sems_o))
     hops.turn(hops.gather(items, lambda d: None))
     for c in locals_:
         c.wait()
@@ -1213,6 +1228,7 @@
         scratch_shapes=[
             pltpu.VMEM((shard, wide), BF),
             pltpu.VMEM((half, D), BF),
+            *ring_sems(chips),
             *ring_sems(chips),
             *ring_sems(chips),
             *ring_sems(chips),

time: 782 us -> 776 us (level)
  transfers between devices with their start and end apart: 4 -> 4, of which waited for: 1 -> 1; matrix products, arithmetic and copies ran while one was open for 4% -> 4% of each run, Pallas kernels for 31% -> 32%
where the time goes in v7:
time: 776 us; the launch traced here: 768 us
  Pallas kernels  619 us (80%)
  waiting for transfers between devices  89.8 us (12%)
  other arithmetic  39.6 us (5%)
  local copies, waits for them, and re-layouts  13.3 us (2%)
    pallas_call x1, Pallas kernels, outputs(): pl.pallas_call(functools.partial(outputs_kernel, chips, cap), out_shape=(...  102 us
    pallas_call x1, Pallas kernels, dense_gradients(): pl.pallas_call(functools.partial(dense_gradients_kernel, chips, split_out...  101 us
    pallas_call x1, Pallas kernels, rows_back(): pl.pallas_call(functools.partial(rows_back_kernel, chips, cap), out_shape...  96.9 us
    pallas_call x1, Pallas kernels, start(): pl.pallas_call(functools.partial(start_kernel, chips, reps, heads, split_...  92.8 us
    pallas_call x1, Pallas kernels, expert_rows(): pl.pallas_call(functools.partial(experts_kernel, chips, cap), out_shape=(...  92.3 us
    ppermute x3, waiting for transfers between devices, from_rep(): return lax.ppermute(v, 'rep', [((s + k) % reps, s) for s in range(reps)])  89.8 us
    pallas_call x1, Pallas kernels, attention(): pl.pallas_call(functools.partial(attention_kernel, chips, reps, heads), o...  89.2 us
    pallas_call x1, Pallas kernels, attention_back(): pl.pallas_call(functools.partial(attention_back_kernel, heads), out_shape...  45.1 us
  transfers between devices with their start and end apart: 4, of which 1 were waited for; matrix products, arithmetic and copies ran while one was open for 4% of the time, Pallas kernels for 32%

profile of v7, /device:TPU:0, one launch (start us, length us, event | category | flops | bytes accessed | tf_op | source)
XLA Modules:
  0.0 768.2 jit_solution(2297047356819158042)
XLA Ops:
  0.6 0.7 pad_convert_fusion
  1.3 0.8 select_reduce_fusion
  2.2 0.7 maximum_maximum_fusion.small_ref
  2.9 92.8 %start.1 = (bf16[2,256,2048]{2,1,0:T(8,128)(2,1)}, f32[16,32,256]{2,1,0:T(8,128)}, bf16[16,128,3072]{2,1,0:T(8,128)(2,1)}, bf16[8,128,2048]{2,1,0:T(8,128)(2,1)}) custom-call(bf16[256,2048]{1,0:T(8,128)(2,1)} %bitcast.61, f32[32,256]{1,0:T(8,128)} %maximum_maximum_fusion.small_ref, bf16[128,6144]{1,0:T(8,128)(2,1)} %wq_ref.1, bf16[128,2048]{1,0:T(8,128)(2,1)} %wo_ref.1), custom_call_target="tpu_custom_call" | custom-call | bytes 209715200 | tf_op jit(solution)/shard_map/start/pallas_call | solution.py:1218
  95.7 0.9 slice.21
  96.6 0.1 reshape.91
  96.7 0.6 fusion.13
  97.3 0.6 slice_bitcast_fusion
  97.9 0.9 constant_dynamic-slice_fusion
  98.8 0.1 copy.42
  98.9 0.6 copy.52
  99.6 0.2 fusion.9
  99.8 0.7 copy.44.slot_ref
  100.5 0.7 convert_bitcast_fusion.slot_ref
  101.2 0.9 copy.41.dc_ref
  102.1 0.8 constant_dynamic-slice_fusion.1
  102.9 89.2 %attention.1 = (bf16[16,256,2048]{2,1,0:T(8,128)(2,1)}, bf16[512,2048]{1,0:T(8,128)(2,1)}, f32[512,3072]{1,0:T(8,128)}, bf16[512,1024]{1,0:T(8,128)(2,1)}, f32[2...) custom-call(bf16[256,2048]{1,0:T(8,128)(2,1)} %bitcast.68, bf16[512,2048]{1,0:T(8,128)(2,1)} %bitcast.69, f32[1,2048]{1,0:T(1,128)} %bitcast.77, ...), custom_call_target="tpu_custom_call" | custom-call | flops 6442450944 | bytes 104857600 | tf_op jit(solution)/shard_map/attention/pallas_call | solution.py:841
  192.2 92.3 %experts.1 = (bf16[8,288,2048]{2,1,0:T(8,128)(2,1)}, bf16[8,288,2048]{2,1,0:T(8,128)(2,1)}, bf16[8,288,1024]{2,1,0:T(8,128)(2,1)}, bf16[8,288,1024]{2,1,0:T(8,128)(2,1)}, bf16[8,288,1024]{2,1,0:T(8,128)(2,1)}) custom-call(bf16[256,2048]{1,0:T(8,128)(2,1)} %get-tuple-element.55.h2_ref, bf16[16,256,2048]{2,1,0:T(8,128)(2,1)} %get-tuple-element.56.dy_ref, ...), custom_call_target="tpu_custom_call" | custom-call | flops 28991029248 | bytes 209715200 | tf_op jit(solution)/shard_map/experts/pallas_call | solution.py:421
  284.5 101.8 %outputs.1 = (f32[256,2048]{1,0:T(8,128)}, bf16[1024,2048]{1,0:T(8,128)(2,1)}, bf16[1024,2048]{1,0:T(8,128)(2,1)}, bf16[2048,1024]{1,0:T(8,128)(2,1)}, bf16[2048,1024]{1,0:T(8,128)(2,1)}) custom-call(bf16[2304,1024]{1,0:T(8,128)(2,1)} %bitcast.99, bf16[2304,2048]{1,0:T(8,128)(2,1)} %bitcast.95, bf16[2304,2048]{1,0:T(8,128)(2,1)} %bitcast.96, ...), custom_call_target="tpu_custom_call" | custom-call | flops 38654705664 | bytes 209715200 | tf_op jit(solution)/shard_map/outputs/pallas_call | solution.py:597
  386.2 1.6 collective-permute-start.1
  387.8 0.5 collective-permute-start.3
  388.3 1.8 multiply_reduce_fusion.2
  390.2 96.9 %rows_back.1 = f32[256,2048]{1,0:T(8,128)} custom-call(bf16[8,288,1024]{2,1,0:T(8,128)(2,1)} %get-tuple-element.65.dg_ref, bf16[8,288,1024]{2,1,0:T(8,128)(2,1)} %get-tuple-element.66.du_ref, f32[256,16]{1,0:T(8,128)} %convert_bitcast_fusion.slot_ref, bf16[2048,1024]{1,0:T(8,128)(2,1)} %bitcast.92, bf16[2048,1024]{1,0:T(8,128)(2,1)} %bitcast.94), custom_call_target="tpu_custom_call" | custom-call | flops 28991029248 | bytes 209715200 | tf_op jit(solution)/shard_map/rows_back/pallas_call | solution.py:686
  487.1 2.3 multiply_reduce_fusion
  489.5 0.1 copy-done.8
  489.6 0.7 fusion.12
  490.3 1.3 collective-permute-start
  491.6 1.6 add.55
  493.2 0.3 fusion.7
  493.5 1.5 copy-done.6
  495.1 5.3 convert_add_fusion.1
  500.4 89.8 %collective-permute-done = bf16[256,2048]{1,0:T(8,128)(2,1)S(1)} collective-permute-done((bf16[256,2048]{1,0:T(8,128)(2,1)S(1)}, bf16[256,2048]{1,0:T(8,128)(2,1)S(1)}, u32[]{:S(2)}, u32[]{:S(2)}) %collective-permute-start) | collective-permute-done | bytes 1048608 | tf_op jit(solution)/shard_map/ppermute | solution.py:1262
  590.1 1.5 pad_maximum_fusion.mid_ref
  591.6 7.6 convert_add_fusion
  599.1 45.1 %attention_back.1 = (bf16[512,3072]{1,0:T(8,128)(2,1)}, f32[1,128]{1,0:T(1,128)}, f32[1,128]{1,0:T(1,128)}, f32[256,2048]{1,0:T(8,128)}, bf16[256,2048]{1,0:T(8,128)(2,1)}, /*index=5*/f32[1,2048]{1,0:T(1,128)}) custom-call(f32[512,3072]{1,0:T(8,128)} %get-tuple-element.75.proj_ref, bf16[512,2048]{1,0:T(8,128)(2,1)} %pad_maximum_fusion.mid_ref, ...), custom_call_target="tpu_custom_call" | custom-call | flops 5368709120 | bytes 20971520 | tf_op jit(solution)/shard_map/attention_back/pallas_call | solution.py:957
  644.2 0.7 pad_maximum_fusion.1
  645.0 0.1 reshape.99
  645.1 0.8 copy.50
  645.8 1.4 collective-permute-start.2
  647.2 101.1 %dense_gradients.1 = (f32[128,6144]{1,0:T(8,128)}, f32[128,2048]{1,0:T(8,128)}, f32[32,128]{1,0:T(8,128)}) custom-call(bf16[512,2048]{1,0:T(8,128)(2,1)} %get-tuple-element.79.h1_ref, bf16[512,3072]{1,0:T(8,128)(2,1)} %get-tuple-element.80.grad_ref, bf16[512,1024]{1,0:T(8,128)(2,1)} %get-tuple-element.81.ob_ref, bf16[512,2048]{1,0:T(8,128)(2,1)} %pad_maximum_fusion.mid_ref, ...), custom_call_target="tpu_custom_call" | custom-call | flops 6442450944 | bytes 209715200 | tf_op jit(solution)/shard_map/dense_gradients/pallas_call | solution.py:1114
  748.3 1.3 slice.33
  749.6 9.0 %add_bitcast_fusion = f32[1,2048,1024]{2,1,0:T(8,128)} fusion(bf16[2048,1024]{1,0:T(8,128)(2,1)} %collective-permute-done.3, bf16[2048,1024]{1,0:T(8,128)(2,1)} %get-tuple-element.89), kind=kLoop, calls=%fused_computation | loop fusion | flops 6291456 | bytes 16777216 | tf_op jit(solution)/shard_map/broadcast_in_dim | solution.py:1478
  758.6 2.0 fusion.2
  760.6 0.1 copy-done.9
  760.7 4.1 fusion.6
  764.8 1.7 copy.55
  766.5 0.3 copy-done.12
  766.8 1.0 copy.56
  (51 shorter events, 0.3 us)
Async XLA Ops:
  2.9 98.2 %copy-start.19 = (s32[1,512]{1,0:T(1,128)S(1)}, s32[1,512]{1,0:T(1,128)}, u32[]{:S(2)}) copy-start(s32[1,512]{1,0:T(1,128)} %param.20) | copy-start | bytes 6148
  2.9 99.2 %copy-start.14 = (f32[1024,128]{1,0:T(8,128)S(1)}, f32[1024,128]{1,0:T(8,128)}, u32[]{:S(2)}) copy-start(f32[1024,128]{1,0:T(8,128)} %constant.57) | copy-start | bytes 1572868
  2.9 99.2 %copy-start.15 = (f32[1024,128]{1,0:T(8,128)S(1)}, f32[1024,128]{1,0:T(8,128)}, u32[]{:S(2)}) copy-start(f32[1024,128]{1,0:T(8,128)} %constant.58) | copy-start | bytes 1572868
  98.9 93.2 %copy-start.13 = (f32[16,1,256]{0,2,1:T(8,128)}, f32[16,1,256]{0,2,1:T(8,128)S(1)}, u32[]{:S(2)}) copy-start(f32[16,1,256]{0,2,1:T(8,128)S(1)} %copy.42) | copy-start | bytes 49156
  101.2 1.7 copy-start.18
  386.2 205.3 %collective-permute-start.1 = (bf16[2048,1024]{1,0:T(8,128)(2,1)}, bf16[2048,1024]{1,0:T(8,128)(2,1)}, u32[]{:S(2)}, u32[]{:S(2)}) collective-permute-start(bf16[2048,1024]{1,0:T(8,128)(2,1)} %get-tuple-element.72), channel_id=1, source_target_pairs={{16,0},{0,16},{17,1},{1,17},{18,2},{2,18},{19,3},{3,19},{20,4},{4,... | collective-permute-start | bytes 12582920 | tf_op jit(solution)/shard_map/ppermute | solution.py:1262
  387.8 360.5 %collective-permute-start.3 = (bf16[2048,1024]{1,0:T(8,128)(2,1)}, bf16[2048,1024]{1,0:T(8,128)(2,1)}, u32[]{:S(2)}, u32[]{:S(2)}) collective-permute-start(bf16[2048,1024]{1,0:T(8,128)(2,1)} %get-tuple-element.89), channel_id=1, source_target_pairs={{16,0},{0,16},{17,1},{1,17},{18,2},{2,18},{19,3},{3,19},{20,4},{4,... | collective-permute-start | bytes 12582920 | tf_op jit(solution)/shard_map/ppermute | solution.py:1262
  390.2 96.9 %copy-start = (f32[256,2048]{1,0:T(8,128)S(1)}, f32[256,2048]{1,0:T(8,128)}, u32[]{:S(2)}) copy-start(f32[256,2048]{1,0:T(8,128)} %get-tuple-element.54) | copy-start | bytes 6291460
  390.2 96.9 %copy-start.16 = (f32[2048]{0:T(1024)S(1)}, f32[2048]{0:T(1024)}, u32[]{:S(2)}) copy-start(f32[2048]{0:T(1024)} %get-tuple-element.96) | copy-start | bytes 24580
  487.1 2.3 copy-start.1
  487.1 2.5 copy-start.8
  489.6 2.0 copy-start.11
  489.6 3.9 copy-start.7
  490.3 99.8 %collective-permute-start = (bf16[256,2048]{1,0:T(8,128)(2,1)S(1)}, bf16[256,2048]{1,0:T(8,128)(2,1)S(1)}, u32[]{:S(2)}, u32[]{:S(2)}) collective-permute-start(bf16[256,2048]{1,0:T(8,128)(2,1)S(1)} %fusion.12), channel_id=1, source_target_pairs={{16,0},{0,16},{17,1},{1,17},{18,2},{2,18},{19,3},{3,19},{20,4},{4,... | collective-permute-start | bytes 3145736 | tf_op jit(solution)/shard_map/ppermute | solution.py:1262
  491.6 1.7 copy-start.3
  491.6 3.5 copy-start.6
  500.4 91.2 %copy-start.5 = (bf16[2048,1024]{1,0:T(8,128)(2,1)S(1)}, bf16[2048,1024]{1,0:T(8,128)(2,1)}, u32[]{:S(2)}) copy-start(bf16[2048,1024]{1,0:T(8,128)(2,1)} %get-tuple-element.72) | copy-start | bytes 12582916
  645.8 112.7 %collective-permute-start.2 = (bf16[256,2048]{1,0:T(8,128)(2,1)}, bf16[256,2048]{1,0:T(8,128)(2,1)}, u32[]{:S(2)}, u32[]{:S(2)}) collective-permute-start(bf16[256,2048]{1,0:T(8,128)(2,1)} %get-tuple-element.78), channel_id=1, source_target_pairs={{0,16},{16,0},{1,17},{17,1},{2,18},{18,2},{3,19},{19,3},{4,20},{20... | collective-permute-start | bytes 3145736 | tf_op jit(solution)/shard_map/ppermute | solution.py:1265
  749.6 9.0 %copy-start.4 = (f32[256,2048]{1,0:T(8,128)S(1)}, f32[256,2048]{1,0:T(8,128)}, u32[]{:S(2)}) copy-start(f32[256,2048]{1,0:T(8,128)} %get-tuple-element.77) | copy-start | bytes 6291460
  749.6 9.0 %copy-start.17 = (f32[2048]{0:T(1024)S(1)}, f32[2048]{0:T(1024)}, u32[]{:S(2)}) copy-start(f32[2048]{0:T(1024)} %get-tuple-element.97) | copy-start | bytes 24580
  758.6 2.0 copy-start.2
  758.6 2.2 copy-start.9
  760.7 4.1 copy-start.10
  764.8 2.0 copy-start.12
